TPU v7x, 32 devices: a whole 2x2x4 slice. The times are simulated.
32 devices in a mesh: dp: 4 (over y, x), table: 8 (over z, core).
Axes of the slice: x: 2, y: 2, z: 4, core: 2. Of those that a mesh axis runs over, the one named last changes fastest.
Arguments:
- ids: int32 [16384], P('dp'), may hold values from 0 to 511
- lengths: int32 [32, 8], P(('dp', 'table')), may hold values from 1 to 64, 320 in all within a row
- table: bfloat16 [512, 512], P(None, 'table'), may hold values from -6 to 6
- w_uvqk: bfloat16 [512, 2048], replicated, may hold values from -0.25 to 0.25
- w_out: bfloat16 [512, 512], replicated, may hold values from -0.25 to 0.25
- cotangent: bfloat16 [16384, 512], P(('dp', 'table')), may hold values from -6 to 6
Outputs:
- output: bfloat16 [16384, 512], P(('dp', 'table'))
- grad_table: float32 [512, 512], P('dp', 'table')
- grad_uvqk: float32 [512, 2048], P(('dp', 'table'))
- grad_out_t: float32 [512, 512], P(('dp', 'table'))
Inputs may be any that keep to these rules, and one draw needn't show every extreme that they name: Each device's 8 histories have lengths summing to 320, the longest exactly 64.
All inputs are finite; a program needn't handle non-finite values.
Results may differ from a plain program's by a relative error of at most 0.017.
Values may be sent and summed in bfloat16 or wider, within the bound.
No kernel may reach another device: no remote copies, remote signals or barrier semaphores. Data moves between devices by JAX's collectives and lax.ppermute only.
A program may use at most 64 MiB of HBM per device.

v0:
```python
import jax
import jax.numpy as jnp
from jax import lax
from jax.sharding import PartitionSpec as P

H = 8
DH = 64
MAXLEN = 64


eps_norm = 1e-05


def layer_norm(values):
    centre_mean = jnp.mean(values, axis=-1, keepdims=True)
    centred = values - centre_mean
    spread = jnp.mean(centred * centred, axis=-1, keepdims=True)
    return centred * lax.rsqrt(spread + eps_norm)


def front(inputs):
    return layer_norm(inputs).astype(jnp.bfloat16)


def middle(project, hist_len):
    histories, history_len, total_width = project.shape
    inner_width = total_width // 4
    activated = jax.nn.silu(project).astype(jnp.bfloat16)
    gate_heads = activated[..., :inner_width]
    value_heads = activated[..., inner_width : 2 * inner_width].reshape(
        histories, history_len, H, DH
    )
    query_heads = activated[..., 2 * inner_width : 3 * inner_width].reshape(
        histories, history_len, H, DH
    )
    key_heads = activated[..., 3 * inner_width :].reshape(histories, history_len, H, DH)
    scores = jnp.einsum(
        "bihd,bjhd->bihj", query_heads, key_heads, preferred_element_type=jnp.float32
    ) * DH ** (-0.5)
    position = jnp.arange(history_len, dtype=jnp.int32)
    allowed = (position[None, :, None, None] >= position[None, None, None, :]) & (
        position[None, :, None, None] < hist_len[:, None, None, None]
    )
    weights = (jnp.where(allowed, jax.nn.silu(scores), jnp.zeros((), jnp.float32)) / MAXLEN).astype(
        jnp.bfloat16
    )
    attended = jnp.einsum(
        "bihj,bjhd->bihd", weights, value_heads, preferred_element_type=jnp.float32
    )
    attended = attended.reshape(histories, history_len, inner_width)
    return (layer_norm(attended) * gate_heads.astype(jnp.float32)).astype(jnp.bfloat16)


def layer_block(x_block, cot_block, hist_len, w_uvqk, w_out):
    histories, history_len, model_width = x_block.shape
    row_count = histories * history_len
    inputs = x_block.reshape(row_count, model_width).astype(jnp.float32)
    normed, front_back = jax.vjp(front, inputs)
    project = jnp.dot(normed, w_uvqk, preferred_element_type=jnp.float32)

    def middle_flat(flat_project):
        return middle(flat_project.reshape(histories, history_len, -1), hist_len).reshape(
            row_count, -1
        )

    gated_out, middle_back = jax.vjp(middle_flat, project)
    output = (inputs + jnp.dot(gated_out, w_out, preferred_element_type=jnp.float32)).astype(
        jnp.bfloat16
    )
    live_rows = (jnp.arange(history_len, dtype=jnp.int32)[None, :] < hist_len[:, None]).reshape(
        row_count, 1
    )
    out_grad = jnp.where(
        live_rows, cot_block.reshape(row_count, model_width), jnp.zeros((), jnp.bfloat16)
    )
    grad_out_t = lax.dot_general(
        out_grad, gated_out, (((0,), (0,)), ((), ())), preferred_element_type=jnp.float32
    )
    gated_grad = lax.dot_general(
        out_grad, w_out, (((1,), (1,)), ((), ())), preferred_element_type=jnp.float32
    ).astype(jnp.bfloat16)
    (project_grad,) = middle_back(gated_grad)
    project_grad_b = project_grad.astype(jnp.bfloat16)
    grad_uvqk = lax.dot_general(
        normed, project_grad_b, (((0,), (0,)), ((), ())), preferred_element_type=jnp.float32
    )
    normed_grad = lax.dot_general(
        project_grad_b, w_uvqk, (((1,), (1,)), ((), ())), preferred_element_type=jnp.float32
    ).astype(jnp.bfloat16)
    (front_grad,) = front_back(normed_grad)
    input_grad = (front_grad + out_grad.astype(jnp.float32)).astype(jnp.bfloat16)
    return (
        output.reshape(histories, history_len, model_width),
        input_grad.reshape(histories, history_len, model_width),
        grad_uvqk,
        grad_out_t,
    )


def lookup_rows(table_cols, ids_all):
    return jnp.take(table_cols, ids_all, axis=0)


def sum_rows(grad_rows, ids_all, item_count):
    return jax.ops.segment_sum(grad_rows.astype(jnp.float32), ids_all, num_segments=item_count)


def local(ids, lengths, table, w_uvqk, w_out, cotangent):
    groups = lax.axis_size("table")
    model_width = table.shape[1] * groups
    histories = lengths.shape[1]
    looked_up = lookup_rows(table, ids)
    embedded = lax.all_to_all(looked_up, "table", split_axis=0, concat_axis=1, tiled=True)
    own_hist = embedded.reshape(histories, MAXLEN, model_width)
    cot_hist = cotangent.reshape(histories, MAXLEN, model_width)
    out_home, grad_home, grad_u, grad_o = layer_block(own_hist, cot_hist, lengths[0], w_uvqk, w_out)
    output = out_home.reshape(histories * MAXLEN, model_width)
    home_grad = grad_home.reshape(histories * MAXLEN, model_width)
    column_grad = lax.all_to_all(home_grad, "table", split_axis=1, concat_axis=0, tiled=True)
    item_terms = sum_rows(column_grad, ids, table.shape[0])
    grad_table = lax.psum_scatter(
        item_terms.astype(jnp.bfloat16), "dp", scatter_dimension=0, tiled=True
    ).astype(jnp.float32)
    partial_u, partial_o = (
        lax.psum_scatter(grad_u, "dp", scatter_dimension=0, tiled=True),
        lax.psum_scatter(grad_o, "dp", scatter_dimension=0, tiled=True),
    )
    grad_uvqk, grad_out_t = (
        lax.psum_scatter(partial_u, "table", scatter_dimension=0, tiled=True),
        lax.psum_scatter(partial_o, "table", scatter_dimension=0, tiled=True),
    )
    return (output, grad_table, grad_uvqk, grad_out_t)


def solution(mesh):
    return jax.shard_map(
        local,
        mesh=mesh,
        in_specs=(
            P("dp"),
            P(("dp", "table"), None),
            P(None, "table"),
            P(),
            P(),
            P(("dp", "table"), None),
        ),
        out_specs=(
            P(("dp", "table"), None),
            P("dp", "table"),
            P(("dp", "table"), None),
            P(("dp", "table"), None),
        ),
        check_vma=False,
    )
```

profile of v0, /device:TPU:0, one launch (start us, length us, event | category | flops | bytes accessed | tf_op | source)
XLA Modules:
  0.0 278.9 jit_solution(867615328385242302)
XLA Ops:
  9.7 14.9 %gather_fusion = bf16[4096,64]{1,0:T(8,128)(2,1)} fusion(bf16[512,64]{1,0:T(8,128)(2,1)S(1)} %copy.48, s32[4096]{0:T(1024)S(1)} %fusion.39), kind=kCustom, calls=%fused_computation | custom fusion | bytes 1064960 | tf_op jit(solution)/shard_map/jit(_take)/gather | solution.py:101
  27.1 6.4 %all-to-all-start = ((bf16[8,512,64]{1,2,0:T(8,128)(2,1)}), bf16[8,512,64]{1,2,0:T(8,128)(2,1)S(1)}, u32[]{:S(2)}, u32[]{:S(2)}) async-start(bf16[8,512,64]{1,2,0:T(8,128)(2,1)} %broadcast_select_fusion.1), calls=%async_computation | async-start | bytes 1048576 | tf_op jit(solution)/shard_map/all_to_all | solution.py:113
  36.5 12.3 %all-to-all-done = bf16[8,512,64]{1,2,0:T(8,128)(2,1)S(1)} async-done(((bf16[8,512,64]{1,2,0:T(8,128)(2,1)}), bf16[8,512,64]{1,2,0:T(8,128)(2,1)S(1)}, u32[]{:S(2)}, u32[]{:S(2)}) %all-to-all-start) | async-done | bytes 524320 | tf_op jit(solution)/shard_map/all_to_all | solution.py:113
  50.9 2.7 reshape.244
  53.6 3.2 %copy.73 = f32[8,64,512]{2,1,0:T(8,128)} copy(f32[8,64,512]{1,0,2:T(8,128)} %reshape.244) | data formatting | bytes 2097152 | tf_op jit(solution)/shard_map/convert_element_type | solution.py:57
  56.8 4.8 %multiply_convert_fusion = (bf16[8,64,2048]{2,1,0:T(8,128)(2,1)S(1)}, f32[8,64,2048]{2,1,0:T(8,128)}) fusion(bf16[512,2048]{1,0:T(8,128)(2,1)S(1)} %copy-done, f32[8,64,512]{2,1,0:T(8,128)} %copy.73, f32[8,64]{1,0:T(8,128)S(1)} %rsqrt.25, f32[8,64]{1,0:T(8,128)S(1)} %div.56), kind=kOutput, calls=%fused_computation.8 | convolution fusion | flops 1079771136 | bytes 9441280 | tf_op jit(solution)/shard_map/dot_general | solution.py:59
  76.6 3.2 %copy.74 = f32[8,64,512]{2,1,0:T(8,128)} copy(f32[8,64,512]{1,2,0:T(8,128)} %bitcast.87) | data formatting | bytes 2097152 | tf_op jit(solution)/shard_map/jvp()/reshape | solution.py:50
  81.6 2.7 fusion.38
  88.9 3.6 %fusion.5 = bf16[8,8,64,64]{3,2,1,0:T(8,128)(2,1)S(1)} fusion(f32[8,8,64,64]{3,2,1,0:T(8,128)} %copy-done.11, bf16[8,8,64,64]{3,2,1,0:T(8,128)(2,1)} %bitcast.97, pred[8,64,64]{2,1,0:T(8,128)(4,1)S(1)} %broadcast_and_fusion, bf16[8,64,8,64]{3,2,1,0:T(8,128)(2,1)} %reshape.212), kind=kOutput, calls=%fused_computation.13 | convolution fusion | flops 37486592 | bytes 2654208 | tf_op jit(solution)/shard_map/transpose(jvp(bihj,bjhd->bihd))/dot_general | solution.py:47
  96.2 3.2 %fusion.17 = bf16[8,64,8,64]{3,1,2,0:T(8,128)(2,1)} fusion(bf16[8,8,64,64]{3,2,1,0:T(8,128)(2,1)} %copy-done.9, bf16[8,64,8,64]{3,2,1,0:T(8,128)(2,1)} %reshape.213), kind=kOutput, calls=%fused_computation.35 | convolution fusion | flops 33554432 | bytes 1572864 | tf_op jit(solution)/shard_map/transpose(jvp(bihd,bjhd->bihj))/dot_general | solution.py:37
  103.7 2.9 %copy.64 = bf16[8,64,8,64]{3,2,1,0:T(8,128)(2,1)} copy(bf16[8,64,8,64]{3,1,2,0:T(8,128)(2,1)} %fusion.17) | data formatting | bytes 1048576 | tf_op jit(solution)/shard_map/transpose(jvp(bihd,bjhd->bihj))/convert_element_type | solution.py:37
  109.2 4.0 %convolution_convert_fusion = bf16[8,8,64,64]{3,2,1,0:T(8,128)(2,1)} fusion(bf16[8,8,64,64]{3,2,1,0:T(8,128)(2,1)} %bitcast.98, f32[8,8,64,64]{3,2,1,0:T(8,128)} %copy-done.11, pred[8,64,64]{1,2,0:T(8,128)(4,1)S(1)} %broadcast_and_fusion.1), kind=kOutput, calls=%fused_computation.30 | convolution fusion | flops 35651584 | bytes 2129920 | tf_op jit(solution)/shard_map/transpose(jvp(bihj,bjhd->bihd))/dot_general | solution.py:47
  115.6 3.8 %fusion.1 = bf16[8,64,2048]{2,1,0:T(8,128)(2,1)S(1)} fusion(f32[8,64,2048]{2,1,0:T(8,128)} %get-tuple-element.23, bf16[8,64,512]{2,1,0:T(8,128)(2,1)} %get-tuple-element.17, bf16[8,64,512]{2,1,0:T(8,128)(2,1)} %copy.76, bf16[8,64,512]{2,1,0:T(8,128)(2,1)} %reshape.219, bf16[8,64,512]{2,1,0:T(8,128)(2,1)} %reshape.218), kind=kLoop, calls=%fused_computation.6 | loop fusion | flops 18874368 | bytes 8388608 | tf_op jit(solution)/shard_map/convert_element_type | solution.py:83
  120.8 3.2 %fusion.47 = f32[512,2048]{1,0:T(8,128)} fusion(bf16[512,512]{0,1:T(8,128)(2,1)S(1)} %bitcast.96, bf16[512,2048]{1,0:T(8,128)(2,1)S(1)} %bitcast.88), kind=kOutput, calls=%fused_computation.97 | convolution fusion | flops 1073741824 | bytes 6815744 | tf_op jit(solution)/shard_map/dot_general | solution.py:84
  124.0 2.9 %fusion.20 = (f32[512]{0:T(512)S(1)}, bf16[512,512]{0,1:T(8,128)(2,1)S(1)}) fusion(f32[512]{0:T(512)S(1)} %broadcast_multiply_fusion.1, bf16[8,512,64]{1,2,0:T(8,128)(2,1)S(1)} %all-to-all-done, bf16[512,2048]{1,0:T(8,128)(2,1)} %bitcast.89, bf16[512,2048]{1,0:T(8,128)(2,1)S(1)} %copy-done), kind=kOutput, calls=%fused_computation.46 | convolution fusion | flops 1075314176 | bytes 5246976 | tf_op jit(solution)/shard_map/dot_general | solution.py:87
  127.7 17.7 %all_to_all.23 = bf16[512,8,64]{0,2,1:T(8,128)(2,1)S(1)} all-to-all(bf16[512,8,64]{0,2,1:T(8,128)(2,1)S(1)} %bitcast.94), channel_id=1, replica_groups=mesh['dp'=4,'table'=8] {'table'}, dimensions={1} | all-to-all | bytes 1048576 | tf_op jit(solution)/shard_map/all_to_all | solution.py:119
  146.6 3.3 %copy.77 = f32[8,512,64]{2,1,0:T(8,128)} copy(f32[8,512,64]{1,2,0:T(8,128)} %convert_bitcast_fusion) | data formatting | bytes 2097152 | tf_op jit(solution)/shard_map/convert_element_type | solution.py:105
  149.9 22.7 %scatter_custom_fusion = f32[512,64]{1,0:T(8,128)S(1)} fusion(s32[4096]{0:T(1024)} %param.6, f32[4096,64]{1,0:T(8,128)} %bitcast.95, f32[]{:T(128)} %constant.43.clone.1), kind=kCustom, calls=%fused_computation.73 | custom fusion | flops 262144 | bytes 131584 | tf_op jit(solution)/shard_map/scatter-add | solution.py:105
  174.0 4.6 %reduce-scatter.8.cloned.1.call-done = f32[128,2048]{1,0:T(8,128)} async-done(((f32[512,2048]{1,0:T(8,128)}), f32[128,2048]{1,0:T(8,128)}) %reduce-scatter.8.cloned.1.call-update) | async-done | bytes 1048592 | tf_op jit(solution)/shard_map/reduce_scatter | solution.py:125
  178.6 2.6 copy.56
  181.2 2.6 fusion.18
  183.8 21.6 %reduce-scatter.6.cloned.1.call-done = bf16[128,64]{1,0:T(8,128)(2,1)} async-done(((bf16[512,64]{1,0:T(8,128)(2,1)}), bf16[128,64]{1,0:T(8,128)(2,1)}) %reduce-scatter.6.cloned.1.call-update) | async-done | bytes 16400 | tf_op jit(solution)/shard_map/reduce_scatter | solution.py:121
  206.9 32.0 %reduce-scatter.14.cloned.1.call-done = f32[16,512]{1,0:T(8,128)} async-done(((f32[128,512]{1,0:T(8,128)}), f32[16,512]{1,0:T(8,128)}) %reduce-scatter.14.cloned.1.call-update) | async-done | bytes 32784 | tf_op jit(solution)/shard_map/reduce_scatter | solution.py:130
  238.9 33.5 %reduce-scatter.10.cloned.1.call-done = f32[16,2048]{1,0:T(8,128)} async-done(((f32[128,2048]{1,0:T(8,128)}), f32[16,2048]{1,0:T(8,128)}) %reduce-scatter.10.cloned.1.call-update) | async-done | bytes 131088 | tf_op jit(solution)/shard_map/reduce_scatter | solution.py:129
  (89 shorter events, 50.6 us)
Async XLA Ops:
  7.2 49.6 %copy-start = (bf16[512,2048]{1,0:T(8,128)(2,1)S(1)}, bf16[512,2048]{1,0:T(8,128)(2,1)}, u32[]{:S(2)}) copy-start(bf16[512,2048]{1,0:T(8,128)(2,1)} %param.9) | copy-start | bytes 6291460
  24.6 8.9 %copy-start.14 = (s32[1,8]{1,0:T(1,128)S(1)}, s32[1,8]{1,0:T(1,128)}, u32[]{:S(2)}) copy-start(s32[1,8]{1,0:T(1,128)} %param.7) | copy-start | bytes 100
  24.6 9.1 %copy-start.13 = (bf16[512,512]{1,0:T(8,128)(2,1)S(1)}, bf16[512,512]{1,0:T(8,128)(2,1)}, u32[]{:S(2)}) copy-start(bf16[512,512]{1,0:T(8,128)(2,1)} %param.11) | copy-start | bytes 1572868
  27.1 21.7 %all-to-all-start = ((bf16[8,512,64]{1,2,0:T(8,128)(2,1)}), bf16[8,512,64]{1,2,0:T(8,128)(2,1)S(1)}, u32[]{:S(2)}, u32[]{:S(2)}) async-start(bf16[8,512,64]{1,2,0:T(8,128)(2,1)} %broadcast_select_fusion.1), calls=%async_computation | async-start | bytes 1048576 | tf_op jit(solution)/shard_map/all_to_all | solution.py:113
  33.5 139.9 %reduce-scatter.12.cloned.1.call-start = ((), (), s32[]{:S(2)}) async-start(), calls=%async_computation.10 | async-start | bytes 1310720 | tf_op jit(solution)/shard_map/reduce_scatter | solution.py:126
  61.6 1.3 copy-start.8
  71.3 2.3 copy-start.12
  73.6 1.3 copy-start.11
  75.0 1.4 copy-start.3
  79.8 1.8 copy-start.1
  88.9 3.6 %copy-start.2 = (bf16[8,64,8,64]{3,2,1,0:T(8,128)(2,1)S(1)}, bf16[8,64,8,64]{3,2,1,0:T(8,128)(2,1)}, u32[]{:S(2)}) copy-start(bf16[8,64,8,64]{3,2,1,0:T(8,128)(2,1)} %reshape.214) | copy-start | bytes 1572868
  92.5 1.5 copy-start.9
  92.5 1.5 copy-start.5
  92.5 1.9 copy-start.6
  95.9 82.6 %reduce-scatter.8.cloned.1.call-start = ((), (), s32[]{:S(2)}) async-start(), calls=%async_computation.8 | async-start | bytes 5242880 | tf_op jit(solution)/shard_map/reduce_scatter | solution.py:125
  96.2 3.2 %copy-start.10 = (bf16[8,64,8,64]{3,1,2,0:T(8,128)(2,1)S(1)}, bf16[8,64,8,64]{3,1,2,0:T(8,128)(2,1)}, u32[]{:S(2)}) copy-start(bf16[8,64,8,64]{3,1,2,0:T(8,128)(2,1)} %fusion.16) | copy-start | bytes 1572868
  119.4 1.3 copy-start.4
  124.0 81.5 %reduce-scatter.6.cloned.1.call-start = ((), (), s32[]{:S(2)}) async-start(), calls=%async_computation.7 | async-start | bytes 163840 | tf_op jit(solution)/shard_map/reduce_scatter | solution.py:121
  124.0 3.3 %copy-start.7 = (bf16[512,512]{0,1:T(8,128)(2,1)S(1)}, bf16[512,512]{0,1:T(8,128)(2,1)}, u32[]{:S(2)}) copy-start(bf16[512,512]{0,1:T(8,128)(2,1)} %copy.57) | copy-start | bytes 1572868
  173.4 65.6 %reduce-scatter.14.cloned.1.call-start = ((), (), s32[]{:S(2)}) async-start(), calls=%async_computation.11 | async-start | bytes 294912 | tf_op jit(solution)/shard_map/reduce_scatter | solution.py:130
  173.9 98.5 %reduce-scatter.10.cloned.1.call-start = ((), (), s32[]{:S(2)}) async-start(), calls=%async_computation.9 | async-start | bytes 1179648 | tf_op jit(solution)/shard_map/reduce_scatter | solution.py:129
Sparse Core Ops, SparseCore 0:
  96.0 26.8 reduce-scatter.11
  125.9 52.5 reduce-scatter.7
  181.3 24.1 reduce-scatter.5
  208.1 30.7 reduce-scatter.13
  241.6 30.7 reduce-scatter.9
where the time goes:
time: 280 us; the launch traced here: 279 us
  waiting for transfers between devices  105 us (38%)
  local copies, waits for them, and re-layouts  62.6 us (22%)
  other arithmetic  40.7 us (15%)
  matrix products  32.5 us (12%)
  blocking collectives  17.7 us (6%)
  between operations  14 us (5%)
  starting transfers between devices  6.77 us (2%)
    reduce_scatter x1, waiting for transfers between devices, local(): lax.psum_scatter(partial_u, 'table', scatter_dimension=0, tiled=True)  33.5 us
    reduce_scatter x1, waiting for transfers between devices, local(): lax.psum_scatter(partial_o, 'table', scatter_dimension=0, tiled=True)  32 us
    scatter-add x1, other arithmetic, sum_rows(): jax.ops.segment_sum(grad_rows.astype(jnp.float32), ids_all, num_segments=...  22.7 us
    reduce_scatter x1, waiting for transfers between devices, local(): lax.psum_scatter(item_terms.astype(jnp.bfloat16), 'dp', scatter_dimension...  21.6 us
    all_to_all x1, blocking collectives, local(): lax.all_to_all(home_grad, 'table', split_axis=1, concat_axis=0, tiled=True)  17.7 us
    gather x2, local copies, waits for them, and re-layouts, lookup_rows(): return jnp.take(table_cols, ids_all, axis=0)  16.5 us
    all_to_all x1, waiting for transfers between devices, local(): lax.all_to_all(looked_up, 'table', split_axis=0, concat_axis=1, tiled=True)  12.3 us
    dot_general x3, matrix products, middle(): jnp.einsum('bihj,bjhd->bihd', weights, value_heads, preferred_element_typ...  8.81 us
  transfers between devices with their start and end apart: 6, of which 5 were waited for; matrix products, arithmetic and copies ran while one was open for 24% of the time, Pallas kernels for 0%

commit v1 on v0

v1 whole, which is shorter than its diff:
```python
import functools
import jax
import jax.numpy as jnp
from jax import lax
from jax.experimental import pallas as pl
from jax.experimental.pallas import tpu as pltpu
from jax.sharding import PartitionSpec as P

H = 8
DH = 64
MAXLEN = 64
LANES = 128
EPS = 1e-05
BF = jnp.bfloat16
F32 = jnp.float32


def nt(a, b):
    return lax.dot_general(a, b, (((1,), (1,)), ((), ())), preferred_element_type=F32)


def nn(a, b):
    return jnp.dot(a, b, preferred_element_type=F32)


def tn(a, b):
    return lax.dot_general(a, b, (((0,), (0,)), ((), ())), preferred_element_type=F32)


def sigmoid(v):
    return 0.5 * jnp.tanh(0.5 * v) + 0.5


def origin_of(packed, len_ref, histories):
    shift = jnp.zeros_like(packed)
    end = jnp.int32(0)
    for b in range(histories):
        end = end + len_ref[0, b]
        shift = shift + jnp.where(packed >= end, MAXLEN - len_ref[0, b], 0)
    return packed + shift


def start_of(packed, len_ref, histories):
    start = jnp.zeros_like(packed)
    end = jnp.int32(0)
    for b in range(histories):
        end = end + len_ref[0, b]
        start = jnp.where(packed >= end, end, start)
    return start


def prep_kernel(len_ref, ids_ref, cot_ref, wout_ref, onehot_ref, outg_ref, gg_ref):
    histories = len_ref.shape[1]
    live, items = onehot_ref.shape
    rows = ids_ref.shape[1]
    own = lax.axis_index("table")
    ids = ids_ref[pl.ds(own, 1), :].astype(F32)
    packed = lax.broadcasted_iota(jnp.int32, (live, rows), 0)
    take = origin_of(packed, len_ref, histories) == lax.broadcasted_iota(jnp.int32, (live, rows), 1)
    own_id = jnp.sum(jnp.where(take, ids, 0.0), axis=1, keepdims=True).astype(jnp.int32)
    onehot_ref[...] = jnp.where(
        lax.broadcasted_iota(jnp.int32, (live, items), 1) == own_id, 1.0, 0.0
    ).astype(BF)
    out_grad = nn(jnp.where(take, 1.0, 0.0).astype(BF), cot_ref[...]).astype(BF)
    outg_ref[...] = out_grad
    gg_ref[...] = nt(out_grad, wout_ref[...]).astype(BF)


def out_kernel(len_ref, ids_ref, tab_ref, gated_ref, wout_ref, out_ref):
    histories = len_ref.shape[1]
    rows = ids_ref.shape[1]
    live = gated_ref.shape[0]
    items = tab_ref.shape[1]
    own = lax.axis_index("table")
    ids = ids_ref[pl.ds(own, 1), :].astype(F32)
    ids_col = jnp.transpose(jnp.broadcast_to(ids, (LANES, rows))).astype(jnp.int32)
    lane = lax.broadcasted_iota(jnp.int32, (rows, LANES), 1)
    onehot = jnp.concatenate(
        [jnp.where(ids_col == lane + k, 1.0, 0.0).astype(BF) for k in range(0, items, LANES)], axis=1
    )
    packed = lax.broadcasted_iota(jnp.int32, (rows, live), 1)
    put = origin_of(packed, len_ref, histories) == lax.broadcasted_iota(jnp.int32, (rows, live), 0)
    gated = nn(jnp.where(put, 1.0, 0.0).astype(BF), gated_ref[...]).astype(BF)
    out_ref[...] = (nt(onehot, tab_ref[...]) + nn(gated, wout_ref[...])).astype(BF)


def layer_kernel(
    order, shape, len_ref, tab_ref, onehot_ref, outg_ref, gg_ref, w_ref, gated_ref, *refs
):
    grads, scratch = refs[:-9], refs[-9:]
    layer_body(order, shape, len_ref, tab_ref, onehot_ref, outg_ref, gg_ref, w_ref, gated_ref, grads, *scratch)


def layer_body(
    order, shape, len_ref, tab_ref, onehot_ref, outg_ref, gg_ref, w_ref, gated_ref, grads,
    act_ref, dact_ref, fac_ref, att_ref, attended_ref, dkv_ref, pg_ref, tmp_ref, lhs_ref,
):
    histories = len_ref.shape[1]
    live, items = onehot_ref.shape
    width = tab_ref.shape[0]
    dps, tabs = shape
    devices = dps * tabs
    me_dp = lax.axis_index("dp")
    me_tab = lax.axis_index("table")
    me = me_dp * tabs + me_tab
    blk = width // devices
    half = width // 2

    x = nt(onehot_ref[...], tab_ref[...])
    centred = x - jnp.mean(x, axis=1, keepdims=True)
    rstd = lax.rsqrt(jnp.mean(centred * centred, axis=1, keepdims=True) + EPS)
    xhat = centred * rstd
    normed = xhat.astype(BF)
    for g in range(4):
        cols = slice(g * width, (g + 1) * width)
        p = nn(normed, w_ref[:, cols])
        s = sigmoid(p)
        a = p * s
        act_ref[:, cols] = a.astype(BF)
        dact_ref[:, cols] = s + a * (1.0 - s)

    tiles = live // MAXLEN
    pairs = width // LANES
    low = lax.broadcasted_iota(jnp.int32, (MAXLEN, LANES), 1) < DH
    zero = jnp.zeros((MAXLEN, LANES), BF)

    def stack(v):
        return jnp.concatenate([jnp.where(low, v, zero), jnp.where(low, zero, v)], axis=0)

    def merge(v):
        return jnp.where(low, v[:MAXLEN], v[MAXLEN:])

    for t in range(tiles):
        r0 = t * MAXLEN
        w0 = max(t - 1, 0) * MAXLEN
        row = r0 + lax.broadcasted_iota(jnp.int32, (MAXLEN, LANES), 0)
        col = w0 + lax.broadcasted_iota(jnp.int32, (MAXLEN, LANES), 1)
        seen = (col >= start_of(row, len_ref, histories)) & (col <= row)
        mask = jnp.where(seen, 1.0 / MAXLEN, 0.0)
        mask = jnp.concatenate([mask, mask], axis=0)
        for c in range(pairs):
            lo, hi = c * LANES, (c + 1) * LANES
            q = stack(act_ref[r0 : r0 + MAXLEN, 2 * width + lo : 2 * width + hi])
            k = act_ref[w0 : w0 + LANES, 3 * width + lo : 3 * width + hi]
            v = act_ref[w0 : w0 + LANES, width + lo : width + hi]
            sc = nt(q, k) * DH**-0.5
            sg = sigmoid(sc)
            si = sc * sg
            w = (si * mask).astype(BF)
            fac_ref[t * pairs + c] = (sg + si * (1.0 - sg)) * (mask * DH**-0.5)
            att_ref[t * pairs + c] = w
            attended_ref[r0 : r0 + MAXLEN, lo:hi] = merge(nn(w, v))

    attended = attended_ref[...]
    cen = attended - jnp.mean(attended, axis=1, keepdims=True)
    r = lax.rsqrt(jnp.mean(cen * cen, axis=1, keepdims=True) + EPS)
    yhat = cen * r
    u = act_ref[:, :width].astype(F32)
    gated = (yhat * u).astype(BF)
    gated_ref[...] = gated
    gg = gg_ref[...].astype(F32)
    pg_ref[:, :width] = ((gg * yhat).astype(BF).astype(F32) * dact_ref[:, :width]).astype(BF)
    dy = gg * u
    datt = r * (dy - jnp.mean(dy, axis=1, keepdims=True) - yhat * jnp.mean(dy * yhat, axis=1, keepdims=True))
    attended_ref[...] = datt

    dkv_ref[...] = jnp.zeros_like(dkv_ref)
    for t in range(tiles):
        r0 = t * MAXLEN
        w0 = max(t - 1, 0) * MAXLEN
        for c in range(pairs):
            lo, hi = c * LANES, (c + 1) * LANES
            q = stack(act_ref[r0 : r0 + MAXLEN, 2 * width + lo : 2 * width + hi])
            k = act_ref[w0 : w0 + LANES, 3 * width + lo : 3 * width + hi]
            v = act_ref[w0 : w0 + LANES, width + lo : width + hi]
            da = stack(attended_ref[r0 : r0 + MAXLEN, lo:hi].astype(BF))
            dw = nt(da, v).astype(BF).astype(F32)
            ds = (dw * fac_ref[t * pairs + c]).astype(BF)
            dq = merge(nn(ds, k)).astype(BF).astype(F32)
            qc = slice(2 * width + lo, 2 * width + hi)
            pg_ref[r0 : r0 + MAXLEN, qc] = (dq * dact_ref[r0 : r0 + MAXLEN, qc]).astype(BF)
            dkv_ref[w0 : w0 + LANES, lo:hi] += tn(att_ref[t * pairs + c], da)
            dkv_ref[w0 : w0 + LANES, width + lo : width + hi] += tn(ds, q)
    for g, c in ((1, 0), (3, 1)):
        cols = slice(g * width, (g + 1) * width)
        d = dkv_ref[:, c * width : (c + 1) * width].astype(BF).astype(F32)
        pg_ref[:, cols] = (d * dact_ref[:, cols]).astype(BF)

    dn = nt(pg_ref[...], w_ref[...]).astype(BF).astype(F32)
    dx = rstd * (dn - jnp.mean(dn, axis=1, keepdims=True) - xhat * jnp.mean(dn * xhat, axis=1, keepdims=True))
    in_grad = (dx + outg_ref[...].astype(F32)).astype(BF)

    def position(colour, rel):
        place = 0
        for bit in order[colour]:
            place = place * 2 + ((rel >> bit) & 1)
        return place

    def relative(colour, src):
        tmp_ref[...] = src
        for rel in range(devices):
            at = position(colour, rel) * blk
            src_at = pl.multiple_of((me ^ rel) * blk, blk)
            lhs_ref[at : at + blk, :] = tmp_ref[pl.ds(src_at, blk), :]
        return lhs_ref[...]

    normed_t = jnp.transpose(normed)
    outg_t = jnp.transpose(outg_ref[...])
    if order is None:
        grad_o_ref, grad_u_ref, grad_t_ref = grads
        grad_o_ref[...] = nn(outg_t, gated)
        grad_u_ref[...] = nn(normed_t, pg_ref[...])
        grad_t_ref[...] = nn(jnp.transpose(in_grad), onehot_ref[...]).astype(BF)
        return
    keep1_ref, send1_ref, keep2_ref, send2_ref = grads
    lhs = relative(0, outg_t)
    res = nn(lhs, gated).astype(BF)
    keep1_ref[:, :width] = res[:half]
    send1_ref[:, :width] = res[half:]
    lhs = relative(0, normed_t)
    res = nn(lhs, pg_ref[:, : 2 * width]).astype(BF)
    keep1_ref[:, width:] = res[:half]
    send1_ref[:, width:] = res[half:]
    lhs = relative(1, normed_t)
    res = nn(lhs, pg_ref[:, 2 * width :]).astype(BF)
    keep2_ref[:, : 2 * width] = res[:half]
    send2_ref[:, : 2 * width] = res[half:]
    tmp_ref[...] = jnp.transpose(in_grad)
    feats = width // tabs
    span = items // dps
    for rt in range(tabs):
        at = pl.multiple_of((me_tab ^ rt) * feats, feats)
        lhs_ref[rt * feats : (rt + 1) * feats, :] = tmp_ref[pl.ds(at, feats), :]
    for rd in range(dps):
        at = pl.multiple_of((me_dp ^ rd) * span, span)
        res = nn(lhs_ref[...], onehot_ref[:, pl.ds(at, span)]).astype(BF)
        for rt in range(tabs):
            place = position(1, rd * tabs + rt) * blk
            dst = keep2_ref if place < half else send2_ref
            place = place % half
            for j in range(feats // blk):
                dst[place : place + blk, 2 * width + j * span : 2 * width + (j + 1) * span] = res[
                    rt * feats + j * blk : rt * feats + (j + 1) * blk, :
                ]


VMEM_SPEC = pl.BlockSpec(memory_space=pltpu.VMEM)
SMEM_SPEC = pl.BlockSpec(memory_space=pltpu.SMEM)


def swap(v, bit, tab_bits, dps, tabs):
    if bit < tab_bits:
        return lax.ppermute(v, "table", [(i, i ^ (1 << bit)) for i in range(tabs)])
    b = bit - tab_bits
    return lax.ppermute(v, "dp", [(i, i ^ (1 << b)) for i in range(dps)])


def local(ids, lengths, table, w_uvqk, w_out, cotangent):
    tabs = lax.axis_size("table")
    dps = lax.axis_size("dp")
    devices = tabs * dps
    tab_bits = tabs.bit_length() - 1
    bits = devices.bit_length() - 1
    histories = lengths.shape[1]
    rows = histories * MAXLEN
    live = rows * 5 // 8
    items = table.shape[0]
    feats = table.shape[1]
    width = feats * tabs
    ids2 = ids.reshape(tabs, rows)

    onehot, outg, gg = pl.pallas_call(
        prep_kernel,
        out_shape=(
            jax.ShapeDtypeStruct((live, items), BF),
            jax.ShapeDtypeStruct((live, width), BF),
            jax.ShapeDtypeStruct((live, width), BF),
        ),
        in_specs=[SMEM_SPEC, VMEM_SPEC, VMEM_SPEC, VMEM_SPEC],
        out_specs=(VMEM_SPEC,) * 3,
        name="prep",
    )(lengths, ids2, cotangent, w_out)

    tab_t = lax.all_gather(table.T, "table", axis=0, tiled=True)

    dp_order = list(range(tab_bits, bits))
    z_order = list(range(1, tab_bits))
    order = ([0] + dp_order + z_order, [0] + dp_order[::-1] + z_order)
    w1 = 3 * width
    sds = jax.ShapeDtypeStruct
    blk = width // devices
    span = items // dps
    halving = blk % 16 == 0 and feats % blk == 0 and span == LANES and width % (feats // blk * span) == 0
    if halving:
        grad_shapes = (sds((width // 2, w1), BF),) * 4
    else:
        order = None
        grad_shapes = (sds((width, width), F32), sds((width, 4 * width), F32), sds((width, items), BF))
    tiles = live // MAXLEN * (width // LANES)
    gated, *grads = pl.pallas_call(
        functools.partial(layer_kernel, order, (dps, tabs)),
        out_shape=(sds((live, width), BF),) + grad_shapes,
        in_specs=[SMEM_SPEC] + [VMEM_SPEC] * 5,
        out_specs=(VMEM_SPEC,) * (1 + len(grad_shapes)),
        scratch_shapes=[
            pltpu.VMEM((live, 4 * width), BF),
            pltpu.VMEM((live, 4 * width), F32),
            pltpu.VMEM((tiles, LANES, LANES), F32),
            pltpu.VMEM((tiles, LANES, LANES), BF),
            pltpu.VMEM((live, width), F32),
            pltpu.VMEM((live, 2 * width), F32),
            pltpu.VMEM((live, 4 * width), BF),
            pltpu.VMEM((width, live), BF),
            pltpu.VMEM((width, live), BF),
        ],
        name="layer",
    )(lengths, tab_t, onehot, outg, gg, w_uvqk)

    output = pl.pallas_call(
        out_kernel,
        out_shape=sds((rows, width), BF),
        in_specs=[SMEM_SPEC] + [VMEM_SPEC] * 4,
        out_specs=VMEM_SPEC,
        name="out",
    )(lengths, ids2, tab_t, gated, w_out)

    if not halving:
        grad_o, grad_u, grad_t = grads
        grad_t = grad_t.reshape(tabs, feats, dps, span).transpose(2, 0, 1, 3).reshape(devices, feats * span)

        def share(v):
            v = lax.psum_scatter(v, "dp", scatter_dimension=0, tiled=True)
            return lax.psum_scatter(v, "table", scatter_dimension=0, tiled=True)

        return (output, share(grad_t).astype(F32).reshape(feats, span).T, share(grad_u), share(grad_o))

    keep1, send1, keep2, send2 = grads
    parts = []
    for keep, send, bit_order in ((keep1, send1, order[0]), (keep2, send2, order[1])):
        for n, bit in enumerate(bit_order):
            got = swap(send, bit, tab_bits, dps, tabs)
            total = keep.astype(F32) + got.astype(F32)
            if n + 1 < len(bit_order):
                total = total.astype(BF)
                h = total.shape[0] // 2
                keep, send = total[:h], total[h:]
        parts.append(total)
    one, two = parts
    grad_out_t = one[:, :width]
    grad_uvqk = jnp.concatenate([one[:, width:], two[:, : 2 * width]], axis=1)
    gt = jnp.concatenate([two[:, 2 * width + j * span : 2 * width + (j + 1) * span] for j in range(feats // blk)], axis=0)
    return (output, gt.T, grad_uvqk, grad_out_t)


def solution(mesh):
    return jax.shard_map(
        local,
        mesh=mesh,
        in_specs=(
            P("dp"),
            P(("dp", "table"), None),
            P(None, "table"),
            P(),
            P(),
            P(("dp", "table"), None),
        ),
        out_specs=(
            P(("dp", "table"), None),
            P("dp", "table"),
            P(("dp", "table"), None),
            P(("dp", "table"), None),
        ),
        check_vma=False,
    )
```

time: 280 us -> 73.5 us (0.26)
  waiting for transfers between devices: 105 us -> 16.3 us
  local copies, waits for them, and re-layouts: 62.6 us -> 2.08 us
  other arithmetic: 40.7 us -> 2.02 us
  matrix products: 32.5 us -> 0 us
  Pallas kernels: 0 us -> 20.4 us
  between operations: 14 us -> 0.77 us
  starting transfers between devices: 6.77 us -> 13.9 us
    reduce_scatter x5 -> x0, waiting for transfers between devices: 91.7 us -> none  [the longest x1 33.5 us: local(): lax.psum_scatter(partial_u, 'table', scatter_dimension=0, tiled=True)]
    dot_general x12 -> x0, matrix products: 32.5 us -> none  [the longest x3 8.81 us: middle(): jnp.einsum('bihj,bjhd->bihd', weights, value_heads, preferred_element_typ...]
    scatter-add x1 -> x0, other arithmetic: 22.7 us -> none  [sum_rows(): jax.ops.segment_sum(grad_rows.astype(jnp.float32), ids_all, num_segments=...]
    pallas_call x0 -> x3, Pallas kernels: none -> 20.4 us  [the longest x1 14.6 us: local(): pl.pallas_call(functools.partial(layer_kernel, order, (dps, tabs)), out_s...]
    reshape x8 -> x1, local copies, waits for them, and re-layouts: 20.2 us -> 1.33 us  [local(): ids2 = ids.reshape(tabs, rows)]
    all_to_all x1 -> x0, blocking collectives: 17.7 us -> none  [local(): lax.all_to_all(home_grad, 'table', split_axis=1, concat_axis=0, tiled=True)]
    all_gather x0 -> x1, blocking collectives: none -> 17.7 us  [local(): tab_t = lax.all_gather(table.T, 'table', axis=0, tiled=True)]
    gather x2 -> x0, local copies, waits for them, and re-layouts: 16.5 us -> none  [lookup_rows(): return jnp.take(table_cols, ids_all, axis=0)]
  transfers between devices with their start and end apart: 6 -> 10, of which waited for: 5 -> 5; matrix products, arithmetic and copies ran while one was open for 24% -> 1% of each run, Pallas kernels for 0% -> 4%
where the time goes in v1:
time: 73.5 us; the launch traced here: 73.2 us
  Pallas kernels  20.4 us (28%)
  blocking collectives  17.7 us (24%)
  waiting for transfers between devices  16.3 us (22%)
  starting transfers between devices  13.9 us (19%)
  local copies, waits for them, and re-layouts  2.08 us (3%)
  other arithmetic  2.02 us (3%)
  between operations  0.77 us (1%)
    all_gather x1, blocking collectives, local(): tab_t = lax.all_gather(table.T, 'table', axis=0, tiled=True)  17.7 us
    pallas_call x1, Pallas kernels, local(): pl.pallas_call(functools.partial(layer_kernel, order, (dps, tabs)), out_s...  14.6 us
    ppermute x4, waiting for transfers between devices, swap(): return lax.ppermute(v, 'dp', [(i, i ^ 1 << b) for i in range(dps)])  11.2 us
    ppermute x6, starting transfers between devices, swap(): return lax.ppermute(v, 'table', [(i, i ^ 1 << bit) for i in range(tabs)])  7.62 us
    ppermute x4, starting transfers between devices, swap(): return lax.ppermute(v, 'dp', [(i, i ^ 1 << b) for i in range(dps)])  6.29 us
    ppermute x6, waiting for transfers between devices, swap(): return lax.ppermute(v, 'table', [(i, i ^ 1 << bit) for i in range(tabs)])  5.18 us
    pallas_call x1, Pallas kernels, local(): pl.pallas_call(out_kernel, out_shape=sds((rows, width), BF), in_specs=[SM...  3.11 us
    pallas_call x1, Pallas kernels, local(): pl.pallas_call(prep_kernel, out_shape=(jax.ShapeDtypeStruct((live, items)...  2.69 us
  transfers between devices with their start and end apart: 10, of which 5 were waited for; matrix products, arithmetic and copies ran while one was open for 1% of the time, Pallas kernels for 4%

profile of v1, /device:TPU:0, one launch (start us, length us, event | category | flops | bytes accessed | tf_op | source)
XLA Modules:
  0.0 73.2 jit_solution(15808364144524857028)
XLA Ops:
  0.6 1.3 %reshape.11.ids_ref = s32[8,512]{1,0:T(8,128)} reshape(s32[4096]{0:T(1024)} %param.6) | data formatting | bytes 32768 | tf_op jit(solution)/shard_map/reshape | solution.py:270
  2.0 17.7 %all_gather.3.tab_ref = bf16[512,512]{1,0:T(8,128)(2,1)} all-gather(bf16[64,512]{1,0:T(8,128)(2,1)} %bitcast.3), channel_id=1, replica_groups=mesh['dp'=4,'table'=8] {'table'}, dimensions={0}, use_global_device_ids=true | all-gather | bytes 589824 | tf_op jit(solution)/shard_map/all_gather | solution.py:284
  19.7 2.7 %prep.1 = (bf16[320,512]{1,0:T(8,128)(2,1)}, bf16[320,512]{1,0:T(8,128)(2,1)}, bf16[320,512]{1,0:T(8,128)(2,1)}) custom-call(s32[1,8]{1,0:T(1,128)} %len_ref.5, s32[8,512]{1,0:T(8,128)} %reshape.11.ids_ref, bf16[512,512]{1,0:T(8,128)(2,1)} %cot_ref.1, bf16[512,512]{1,0:T(8,128)(2,1)} %wout_ref.3), custom_call_target="tpu_custom_call" | custom-call | tf_op jit(solution)/shard_map/prep/pallas_call | solution.py:272
  22.4 14.6 %layer.1 = (bf16[320,512]{1,0:T(8,128)(2,1)}, bf16[256,1536]{1,0:T(8,128)(2,1)}, bf16[256,1536]{1,0:T(8,128)(2,1)}, bf16[256,1536]{1,0:T(8,128)(2,1)}, bf16[256,1536]{1,0:T(8,128)(2,1)}) custom-call(s32[1,8]{1,0:T(1,128)} %len_ref.5, bf16[512,512]{1,0:T(8,128)(2,1)} %all_gather.3.tab_ref, bf16[320,512]{1,0:T(8,128)(2,1)} %get-tuple-element.12.onehot_ref, ...), custom_call_target="tpu_custom_call" | custom-call | tf_op jit(solution)/shard_map/layer/pallas_call | solution.py:300
  36.9 0.4 collective-permute-start
  37.5 3.1 %out.1 = bf16[512,512]{1,0:T(8,128)(2,1)} custom-call(s32[1,8]{1,0:T(1,128)} %len_ref.5, s32[8,512]{1,0:T(8,128)} %reshape.11.ids_ref, bf16[512,512]{1,0:T(8,128)(2,1)} %all_gather.3.tab_ref, bf16[320,512]{1,0:T(8,128)(2,1)} %get-tuple-element.15.gated_ref, bf16[512,512]{1,0:T(8,128)(2,1)} %wout_ref.3), custom_call_target="tpu_custom_call" | custom-call | tf_op jit(solution)/shard_map/out/pallas_call | solution.py:319
  40.6 0.2 add_convert_fusion.1
  40.8 1.6 %collective-permute-start.1 = (bf16[128,1536]{1,0:T(8,128)(2,1)S(1)}, bf16[128,1536]{1,0:T(8,128)(2,1)S(1)}, u32[]{:S(2)}, u32[]{:S(2)}) collective-permute-start(bf16[128,1536]{1,0:T(8,128)(2,1)S(1)} %slice.93), channel_id=1, source_target_pairs={{0,16},{8,24},{16,0},{24,8},{1,17},{9,25},{17,1},{25,9},{2,18},{10... | collective-permute-start | bytes 1179656 | tf_op jit(solution)/shard_map/ppermute | solution.py:255
  42.4 0.2 add_convert_fusion
  42.6 1.6 %collective-permute-start.6 = (bf16[128,1536]{1,0:T(8,128)(2,1)S(1)}, bf16[128,1536]{1,0:T(8,128)(2,1)S(1)}, u32[]{:S(2)}, u32[]{:S(2)}) collective-permute-start(bf16[128,1536]{1,0:T(8,128)(2,1)S(1)} %slice.105), channel_id=1, source_target_pairs={{0,8},{8,0},{16,24},{24,16},{1,9},{9,1},{17,25},{25,17},{2,10},{10... | collective-permute-start | bytes 1179656 | tf_op jit(solution)/shard_map/ppermute | solution.py:255
  44.2 8.1 %collective-permute-done.1 = bf16[128,1536]{1,0:T(8,128)(2,1)S(1)} collective-permute-done((bf16[128,1536]{1,0:T(8,128)(2,1)S(1)}, bf16[128,1536]{1,0:T(8,128)(2,1)S(1)}, u32[]{:S(2)}, u32[]{:S(2)}) %collective-permute-start.1) | collective-permute-done | bytes 393248 | tf_op jit(solution)/shard_map/ppermute | solution.py:255
  52.4 1.5 %collective-permute-start.2 = (bf16[64,1536]{1,0:T(8,128)(2,1)S(1)}, bf16[64,1536]{1,0:T(8,128)(2,1)S(1)}, u32[]{:S(2)}, u32[]{:S(2)}) collective-permute-start(bf16[64,1536]{1,0:T(8,128)(2,1)S(1)} %slice.95), channel_id=1, source_target_pairs={{0,8},{8,0},{16,24},{24,16},{1,9},{9,1},{17,25},{25,17},{2,10},{10... | collective-permute-start | bytes 589832 | tf_op jit(solution)/shard_map/ppermute | solution.py:255
  54.0 1.6 %collective-permute-start.7 = (bf16[64,1536]{1,0:T(8,128)(2,1)S(1)}, bf16[64,1536]{1,0:T(8,128)(2,1)S(1)}, u32[]{:S(2)}, u32[]{:S(2)}) collective-permute-start(bf16[64,1536]{1,0:T(8,128)(2,1)S(1)} %slice.107), channel_id=1, source_target_pairs={{0,16},{8,24},{16,0},{24,8},{1,17},{9,25},{17,1},{25,9},{2,18},{10... | collective-permute-start | bytes 589832 | tf_op jit(solution)/shard_map/ppermute | solution.py:255
  55.6 3.1 %collective-permute-done.2 = bf16[64,1536]{1,0:T(8,128)(2,1)S(1)} collective-permute-done((bf16[64,1536]{1,0:T(8,128)(2,1)S(1)}, bf16[64,1536]{1,0:T(8,128)(2,1)S(1)}, u32[]{:S(2)}, u32[]{:S(2)}) %collective-permute-start.2) | collective-permute-done | bytes 196640 | tf_op jit(solution)/shard_map/ppermute | solution.py:255
  58.8 1.7 %collective-permute-start.3 = (bf16[32,1536]{1,0:T(8,128)(2,1)S(1)}, bf16[32,1536]{1,0:T(8,128)(2,1)S(1)}, u32[]{:S(2)}, u32[]{:S(2)}) collective-permute-start(bf16[32,1536]{1,0:T(8,128)(2,1)S(1)} %slice.97), channel_id=1, source_target_pairs={{0,2},{1,3},{2,0},{3,1},{4,6},{5,7},{6,4},{7,5},{8,10},{9,11},{10,... | collective-permute-start | bytes 294920 | tf_op jit(solution)/shard_map/ppermute | solution.py:253
  60.5 1.3 %collective-permute-start.8 = (bf16[32,1536]{1,0:T(8,128)(2,1)S(1)}, bf16[32,1536]{1,0:T(8,128)(2,1)S(1)}, u32[]{:S(2)}, u32[]{:S(2)}) collective-permute-start(bf16[32,1536]{1,0:T(8,128)(2,1)S(1)} %slice.109), channel_id=1, source_target_pairs={{0,2},{1,3},{2,0},{3,1},{4,6},{5,7},{6,4},{7,5},{8,10},{9,11},{10,... | collective-permute-start | bytes 294920 | tf_op jit(solution)/shard_map/ppermute | solution.py:253
  61.9 1.8 %collective-permute-done.3 = bf16[32,1536]{1,0:T(8,128)(2,1)S(1)} collective-permute-done((bf16[32,1536]{1,0:T(8,128)(2,1)S(1)}, bf16[32,1536]{1,0:T(8,128)(2,1)S(1)}, u32[]{:S(2)}, u32[]{:S(2)}) %collective-permute-start.3) | collective-permute-done | bytes 98336 | tf_op jit(solution)/shard_map/ppermute | solution.py:253
  63.7 2.5 %collective-permute-start.4 = (bf16[16,1536]{1,0:T(8,128)(2,1)S(1)}, bf16[16,1536]{1,0:T(8,128)(2,1)S(1)}, u32[]{:S(2)}, u32[]{:S(2)}) collective-permute-start(bf16[16,1536]{1,0:T(8,128)(2,1)S(1)} %slice.99), channel_id=1, source_target_pairs={{0,4},{1,5},{2,6},{3,7},{4,0},{5,1},{6,2},{7,3},{8,12},{9,13},{10,... | collective-permute-start | bytes 147464 | tf_op jit(solution)/shard_map/ppermute | solution.py:253
  66.2 1.6 %collective-permute-start.9 = (bf16[16,1536]{1,0:T(8,128)(2,1)S(1)}, bf16[16,1536]{1,0:T(8,128)(2,1)S(1)}, u32[]{:S(2)}, u32[]{:S(2)}) collective-permute-start(bf16[16,1536]{1,0:T(8,128)(2,1)S(1)} %slice.111), channel_id=1, source_target_pairs={{0,4},{1,5},{2,6},{3,7},{4,0},{5,1},{6,2},{7,3},{8,12},{9,13},{10,... | collective-permute-start | bytes 147464 | tf_op jit(solution)/shard_map/ppermute | solution.py:253
  67.9 1.1 %collective-permute-done.4 = bf16[16,1536]{1,0:T(8,128)(2,1)S(1)} collective-permute-done((bf16[16,1536]{1,0:T(8,128)(2,1)S(1)}, bf16[16,1536]{1,0:T(8,128)(2,1)S(1)}, u32[]{:S(2)}, u32[]{:S(2)}) %collective-permute-start.4) | collective-permute-done | bytes 49184 | tf_op jit(solution)/shard_map/ppermute | solution.py:253
  69.0 2.3 %collective-permute-done.9 = bf16[16,1536]{1,0:T(8,128)(2,1)S(1)} collective-permute-done((bf16[16,1536]{1,0:T(8,128)(2,1)S(1)}, bf16[16,1536]{1,0:T(8,128)(2,1)S(1)}, u32[]{:S(2)}, u32[]{:S(2)}) %collective-permute-start.9) | collective-permute-done | bytes 49184 | tf_op jit(solution)/shard_map/ppermute | solution.py:253
  71.3 0.6 slice.114
  71.9 0.7 pad_maximum_fusion
  72.6 0.6 maximum_bitcast_fusion
  (29 shorter events, 0.7 us)
Async XLA Ops:
  36.9 3.6 %copy-start.1 = (bf16[256,1536]{1,0:T(8,128)(2,1)S(1)}, bf16[256,1536]{1,0:T(8,128)(2,1)}, u32[]{:S(2)}) copy-start(bf16[256,1536]{1,0:T(8,128)(2,1)} %get-tuple-element.16) | copy-start | bytes 2359300
  36.9 3.6 %collective-permute-start = (bf16[256,1536]{1,0:T(8,128)(2,1)}, bf16[256,1536]{1,0:T(8,128)(2,1)S(1)}, u32[]{:S(2)}, u32[]{:S(2)}) collective-permute-start(bf16[256,1536]{1,0:T(8,128)(2,1)} %get-tuple-element.17), channel_id=1, source_target_pairs={{0,1},{1,0},{2,3},{3,2},{4,5},{5,4},{6,7},{7,6},{8,9},{9,8},{10,11... | collective-permute-start | bytes 2359304 | tf_op jit(solution)/shard_map/ppermute | solution.py:253
  37.3 5.1 %collective-permute-start.5 = (bf16[256,1536]{1,0:T(8,128)(2,1)}, bf16[256,1536]{1,0:T(8,128)(2,1)S(1)}, u32[]{:S(2)}, u32[]{:S(2)}) collective-permute-start(bf16[256,1536]{1,0:T(8,128)(2,1)} %get-tuple-element.19), channel_id=1, source_target_pairs={{0,1},{1,0},{2,3},{3,2},{4,5},{5,4},{6,7},{7,6},{8,9},{9,8},{10,11... | collective-permute-start | bytes 2359304 | tf_op jit(solution)/shard_map/ppermute | solution.py:253
  40.6 1.8 %copy-start = (bf16[256,1536]{1,0:T(8,128)(2,1)S(1)}, bf16[256,1536]{1,0:T(8,128)(2,1)}, u32[]{:S(2)}) copy-start(bf16[256,1536]{1,0:T(8,128)(2,1)} %get-tuple-element.18) | copy-start | bytes 2359300
  40.8 11.4 %collective-permute-start.1 = (bf16[128,1536]{1,0:T(8,128)(2,1)S(1)}, bf16[128,1536]{1,0:T(8,128)(2,1)S(1)}, u32[]{:S(2)}, u32[]{:S(2)}) collective-permute-start(bf16[128,1536]{1,0:T(8,128)(2,1)S(1)} %slice.93), channel_id=1, source_target_pairs={{0,16},{8,24},{16,0},{24,8},{1,17},{9,25},{17,1},{25,9},{2,18},{10... | collective-permute-start | bytes 1179656 | tf_op jit(solution)/shard_map/ppermute | solution.py:255
  42.6 11.3 %collective-permute-start.6 = (bf16[128,1536]{1,0:T(8,128)(2,1)S(1)}, bf16[128,1536]{1,0:T(8,128)(2,1)S(1)}, u32[]{:S(2)}, u32[]{:S(2)}) collective-permute-start(bf16[128,1536]{1,0:T(8,128)(2,1)S(1)} %slice.105), channel_id=1, source_target_pairs={{0,8},{8,0},{16,24},{24,16},{1,9},{9,1},{17,25},{25,17},{2,10},{10... | collective-permute-start | bytes 1179656 | tf_op jit(solution)/shard_map/ppermute | solution.py:255
  52.4 6.4 %collective-permute-start.2 = (bf16[64,1536]{1,0:T(8,128)(2,1)S(1)}, bf16[64,1536]{1,0:T(8,128)(2,1)S(1)}, u32[]{:S(2)}, u32[]{:S(2)}) collective-permute-start(bf16[64,1536]{1,0:T(8,128)(2,1)S(1)} %slice.95), channel_id=1, source_target_pairs={{0,8},{8,0},{16,24},{24,16},{1,9},{9,1},{17,25},{25,17},{2,10},{10... | collective-permute-start | bytes 589832 | tf_op jit(solution)/shard_map/ppermute | solution.py:255
  54.0 6.4 %collective-permute-start.7 = (bf16[64,1536]{1,0:T(8,128)(2,1)S(1)}, bf16[64,1536]{1,0:T(8,128)(2,1)S(1)}, u32[]{:S(2)}, u32[]{:S(2)}) collective-permute-start(bf16[64,1536]{1,0:T(8,128)(2,1)S(1)} %slice.107), channel_id=1, source_target_pairs={{0,16},{8,24},{16,0},{24,8},{1,17},{9,25},{17,1},{25,9},{2,18},{10... | collective-permute-start | bytes 589832 | tf_op jit(solution)/shard_map/ppermute | solution.py:255
  58.8 4.9 %collective-permute-start.3 = (bf16[32,1536]{1,0:T(8,128)(2,1)S(1)}, bf16[32,1536]{1,0:T(8,128)(2,1)S(1)}, u32[]{:S(2)}, u32[]{:S(2)}) collective-permute-start(bf16[32,1536]{1,0:T(8,128)(2,1)S(1)} %slice.97), channel_id=1, source_target_pairs={{0,2},{1,3},{2,0},{3,1},{4,6},{5,7},{6,4},{7,5},{8,10},{9,11},{10,... | collective-permute-start | bytes 294920 | tf_op jit(solution)/shard_map/ppermute | solution.py:253
  60.5 5.6 %collective-permute-start.8 = (bf16[32,1536]{1,0:T(8,128)(2,1)S(1)}, bf16[32,1536]{1,0:T(8,128)(2,1)S(1)}, u32[]{:S(2)}, u32[]{:S(2)}) collective-permute-start(bf16[32,1536]{1,0:T(8,128)(2,1)S(1)} %slice.109), channel_id=1, source_target_pairs={{0,2},{1,3},{2,0},{3,1},{4,6},{5,7},{6,4},{7,5},{8,10},{9,11},{10,... | collective-permute-start | bytes 294920 | tf_op jit(solution)/shard_map/ppermute | solution.py:253
  63.7 5.2 %collective-permute-start.4 = (bf16[16,1536]{1,0:T(8,128)(2,1)S(1)}, bf16[16,1536]{1,0:T(8,128)(2,1)S(1)}, u32[]{:S(2)}, u32[]{:S(2)}) collective-permute-start(bf16[16,1536]{1,0:T(8,128)(2,1)S(1)} %slice.99), channel_id=1, source_target_pairs={{0,4},{1,5},{2,6},{3,7},{4,0},{5,1},{6,2},{7,3},{8,12},{9,13},{10,... | collective-permute-start | bytes 147464 | tf_op jit(solution)/shard_map/ppermute | solution.py:253
  66.2 5.1 %collective-permute-start.9 = (bf16[16,1536]{1,0:T(8,128)(2,1)S(1)}, bf16[16,1536]{1,0:T(8,128)(2,1)S(1)}, u32[]{:S(2)}, u32[]{:S(2)}) collective-permute-start(bf16[16,1536]{1,0:T(8,128)(2,1)S(1)} %slice.111), channel_id=1, source_target_pairs={{0,4},{1,5},{2,6},{3,7},{4,0},{5,1},{6,2},{7,3},{8,12},{9,13},{10,... | collective-permute-start | bytes 147464 | tf_op jit(solution)/shard_map/ppermute | solution.py:253

commit v2 on v1

--- a/solution.py
+++ b/solution.py
@@ -84,10 +84,16 @@
     out_ref[...] = (nt(onehot, tab_ref[...]) + nn(gated, wout_ref[...])).astype(BF)
 
 
-def layer_kernel(
-    order, shape, len_ref, tab_ref, onehot_ref, outg_ref, gg_ref, w_ref, gated_ref, *refs
-):
-    grads, scratch = refs[:-9], refs[-9:]
+def layer_kernel(order, shape, len_ref, onehot_ref, outg_ref, gg_ref, w_ref, *refs):
+    dps, tabs = shape
+    pieces, refs = refs[:tabs], refs[tabs:]
+    gated_ref, tab_ref = refs[:2]
+    grads, scratch = refs[2:-9], refs[-9:]
+    me_tab = lax.axis_index("table")
+    for rel in range(tabs):
+        feats = pieces[rel].shape[0]
+        at = pl.multiple_of((me_tab ^ rel) * feats, feats)
+        tab_ref[pl.ds(at, feats), :] = pieces[rel][...]
     layer_body(order, shape, len_ref, tab_ref, onehot_ref, outg_ref, gg_ref, w_ref, gated_ref, grads, *scratch)
 
 
@@ -244,6 +250,16 @@
                 ]
 
 
+def finish_kernel(keep_ref, got_ref, grad_u_ref, grad_o_ref, grad_t_ref):
+    blk, width = grad_o_ref.shape
+    feats, span = grad_t_ref.shape
+    total = keep_ref[...].astype(F32) + got_ref[...].astype(F32)
+    grad_o_ref[...] = total[:, :width]
+    grad_u_ref[...] = total[:, width : 5 * width]
+    for j in range(feats // blk):
+        grad_t_ref[j * blk : (j + 1) * blk, :] = total[:, 5 * width + j * span : 5 * width + (j + 1) * span]
+
+
 VMEM_SPEC = pl.BlockSpec(memory_space=pltpu.VMEM)
 SMEM_SPEC = pl.BlockSpec(memory_space=pltpu.SMEM)
 
@@ -278,10 +294,18 @@
         ),
         in_specs=[SMEM_SPEC, VMEM_SPEC, VMEM_SPEC, VMEM_SPEC],
         out_specs=(VMEM_SPEC,) * 3,
+        compiler_params=pltpu.CompilerParams(vmem_limit_bytes=16 << 20),
         name="prep",
     )(lengths, ids2, cotangent, w_out)
 
-    tab_t = lax.all_gather(table.T, "table", axis=0, tiled=True)
+    def other(v, rel):
+        return lax.ppermute(v, "table", [(i, i ^ rel) for i in range(tabs)])
+
+    mine = table.T
+    pieces = []
+    for rel in range(0, tabs, 2):
+        piece = other(mine, rel) if rel else mine
+        pieces += [piece, other(piece, 1)]
 
     dp_order = list(range(tab_bits, bits))
     z_order = list(range(1, tab_bits))
@@ -297,11 +321,11 @@
         order = None
         grad_shapes = (sds((width, width), F32), sds((width, 4 * width), F32), sds((width, items), BF))
     tiles = live // MAXLEN * (width // LANES)
-    gated, *grads = pl.pallas_call(
+    gated, tab_t, *grads = pl.pallas_call(
         functools.partial(layer_kernel, order, (dps, tabs)),
-        out_shape=(sds((live, width), BF),) + grad_shapes,
-        in_specs=[SMEM_SPEC] + [VMEM_SPEC] * 5,
-        out_specs=(VMEM_SPEC,) * (1 + len(grad_shapes)),
+        out_shape=(sds((live, width), BF), sds((width, items), BF)) + grad_shapes,
+        in_specs=[SMEM_SPEC] + [VMEM_SPEC] * (4 + tabs),
+        out_specs=(VMEM_SPEC,) * (2 + len(grad_shapes)),
         scratch_shapes=[
             pltpu.VMEM((live, 4 * width), BF),
             pltpu.VMEM((live, 4 * width), F32),
@@ -313,16 +337,19 @@
             pltpu.VMEM((width, live), BF),
             pltpu.VMEM((width, live), BF),
         ],
+        compiler_params=pltpu.CompilerParams(vmem_limit_bytes=32 << 20),
         name="layer",
-    )(lengths, tab_t, onehot, outg, gg, w_uvqk)
-
-    output = pl.pallas_call(
-        out_kernel,
-        out_shape=sds((rows, width), BF),
-        in_specs=[SMEM_SPEC] + [VMEM_SPEC] * 4,
-        out_specs=VMEM_SPEC,
+    )(lengths, onehot, outg, gg, w_uvqk, *pieces)
+
+    def finish_output(gated):
+        return pl.pallas_call(
+            out_kernel,
+            out_shape=sds((rows, width), BF),
+            in_specs=[SMEM_SPEC] + [VMEM_SPEC] * 4,
+            out_specs=VMEM_SPEC,
+            compiler_params=pltpu.CompilerParams(vmem_limit_bytes=16 << 20),
         name="out",
-    )(lengths, ids2, tab_t, gated, w_out)
+        )(lengths, ids2, tab_t, gated, w_out)
 
     if not halving:
         grad_o, grad_u, grad_t = grads
@@ -332,24 +359,40 @@
             v = lax.psum_scatter(v, "dp", scatter_dimension=0, tiled=True)
             return lax.psum_scatter(v, "table", scatter_dimension=0, tiled=True)
 
-        return (output, share(grad_t).astype(F32).reshape(feats, span).T, share(grad_u), share(grad_o))
+        return (finish_output(gated), share(grad_t).astype(F32).reshape(feats, span).T, share(grad_u), share(grad_o))
+
+    def add(keep, got):
+        return (keep.astype(F32) + got.astype(F32)).astype(BF)
+
+    def halves(v):
+        h = v.shape[0] // 2
+        return v[:h], v[h:]
 
     keep1, send1, keep2, send2 = grads
-    parts = []
-    for keep, send, bit_order in ((keep1, send1, order[0]), (keep2, send2, order[1])):
-        for n, bit in enumerate(bit_order):
-            got = swap(send, bit, tab_bits, dps, tabs)
-            total = keep.astype(F32) + got.astype(F32)
-            if n + 1 < len(bit_order):
-                total = total.astype(BF)
-                h = total.shape[0] // 2
-                keep, send = total[:h], total[h:]
-        parts.append(total)
-    one, two = parts
-    grad_out_t = one[:, :width]
-    grad_uvqk = jnp.concatenate([one[:, width:], two[:, : 2 * width]], axis=1)
-    gt = jnp.concatenate([two[:, 2 * width + j * span : 2 * width + (j + 1) * span] for j in range(feats // blk)], axis=0)
-    return (output, gt.T, grad_uvqk, grad_out_t)
+    totals = [add(keep, other(send, 1)) for keep, send in ((keep1, send1), (keep2, send2))]
+    gated, *totals = lax.optimization_barrier((gated, *totals))
+    output = finish_output(gated)
+    for n in range(len(dp_order)):
+        for c in range(2):
+            keep, send = halves(totals[c])
+            totals[c] = add(keep, swap(send, order[c][1 + n], tab_bits, dps, tabs))
+        if n == 0:
+            output, *totals = lax.optimization_barrier((output, *totals))
+    total = jnp.concatenate(totals, axis=1)
+    for bit in z_order[:-1]:
+        keep, send = halves(total)
+        total = add(keep, swap(send, bit, tab_bits, dps, tabs))
+    keep, send = halves(total)
+    got = swap(send, z_order[-1], tab_bits, dps, tabs)
+    grad_uvqk, grad_out_t, grad_t = pl.pallas_call(
+        finish_kernel,
+        out_shape=(sds((blk, 4 * width), F32), sds((blk, width), F32), sds((feats, span), F32)),
+        in_specs=[VMEM_SPEC] * 2,
+        out_specs=(VMEM_SPEC,) * 3,
+        compiler_params=pltpu.CompilerParams(vmem_limit_bytes=8 << 20),
+        name="finish",
+    )(keep, got)
+    return (output, grad_t.T, grad_uvqk, grad_out_t)
 
 
 def solution(mesh):

time: 73.5 us -> 69.1 us (0.940)
  blocking collectives: 17.7 us -> 0 us
  waiting for transfers between devices: 16.3 us -> 29.7 us
  local copies, waits for them, and re-layouts: 2.08 us -> 6.64 us
  Pallas kernels: 20.4 us -> 16.1 us
  other arithmetic: 2.02 us -> 0.73 us
  starting transfers between devices: 13.9 us -> 14.8 us
    all_gather x1 -> x0, blocking collectives: 17.7 us -> none  [local(): tab_t = lax.all_gather(table.T, 'table', axis=0, tiled=True)]
    ppermute x0 -> x9, waiting for transfers between devices: none -> 7.88 us  [other(): return lax.ppermute(v, 'table', [(i, i ^ rel) for i in range(tabs)])]
    ppermute x0 -> x9, starting transfers between devices: none -> 6.87 us  [other(): return lax.ppermute(v, 'table', [(i, i ^ rel) for i in range(tabs)])]
    unnamed x4 -> x14, local copies, waits for them, and re-layouts: 0.01 us -> 5.82 us
    ppermute x6 -> x2, starting transfers between devices: 7.62 us -> 2.64 us  [swap(): return lax.ppermute(v, 'table', [(i, i ^ 1 << bit) for i in range(tabs)])]
    ppermute x6 -> x2, waiting for transfers between devices: 5.18 us -> 9.73 us  [swap(): return lax.ppermute(v, 'table', [(i, i ^ 1 << bit) for i in range(tabs)])]
    pallas_call x1, Pallas kernels: 14.6 us -> 12 us  [local(): pl.pallas_call(functools.partial(layer_kernel, order, (dps, tabs)), out_s...]
    pallas_call x1, Pallas kernels: 2.69 us -> 1.18 us  [local(): pl.pallas_call(prep_kernel, out_shape=(jax.ShapeDtypeStruct((live, items)...]
  transfers between devices with their start and end apart: 10 -> 15, of which waited for: 5 -> 10; matrix products, arithmetic and copies ran while one was open for 1% -> 2% of each run, Pallas kernels for 4% -> 5%
where the time goes in v2:
time: 69.1 us; the launch traced here: 68.7 us
  waiting for transfers between devices  29.7 us (43%)
  Pallas kernels  16.1 us (23%)
  starting transfers between devices  14.8 us (21%)
  local copies, waits for them, and re-layouts  6.64 us (10%)
  between operations  0.78 us (1%)
  other arithmetic  0.73 us (1%)
    ppermute x4, waiting for transfers between devices, swap(): return lax.ppermute(v, 'dp', [(i, i ^ 1 << b) for i in range(dps)])  12.1 us
    pallas_call x1, Pallas kernels, local(): pl.pallas_call(functools.partial(layer_kernel, order, (dps, tabs)), out_s...  12 us
    ppermute x2, waiting for transfers between devices, swap(): return lax.ppermute(v, 'table', [(i, i ^ 1 << bit) for i in range(tabs)])  9.73 us
    ppermute x9, waiting for transfers between devices, other(): return lax.ppermute(v, 'table', [(i, i ^ rel) for i in range(tabs)])  7.88 us
    ppermute x9, starting transfers between devices, other(): return lax.ppermute(v, 'table', [(i, i ^ rel) for i in range(tabs)])  6.87 us
    unnamed x14, local copies, waits for them, and re-layouts  5.82 us
    ppermute x4, starting transfers between devices, swap(): return lax.ppermute(v, 'dp', [(i, i ^ 1 << b) for i in range(dps)])  5.28 us
    ppermute x2, starting transfers between devices, swap(): return lax.ppermute(v, 'table', [(i, i ^ 1 << bit) for i in range(tabs)])  2.64 us
  transfers between devices with their start and end apart: 15, of which 10 were waited for; matrix products, arithmetic and copies ran while one was open for 2% of the time, Pallas kernels for 5%

profile of v2, /device:TPU:0, one launch (start us, length us, event | category | flops | bytes accessed | tf_op | source)
XLA Modules:
  0.0 68.7 jit_solution(16471917154764868597)
XLA Ops:
  0.6 5.1 %collective-permute-start.5 = (bf16[64,512]{1,0:T(8,128)(2,1)}, bf16[64,512]{1,0:T(8,128)(2,1)S(1)}, u32[]{:S(2)}, u32[]{:S(2)}) collective-permute-start(bf16[64,512]{1,0:T(8,128)(2,1)} %bitcast.2), channel_id=1, source_target_pairs={{0,6},{1,7},{2,4},{3,5},{4,2},{5,3},{6,0},{7,1},{8,14},{9,15},{10,... | collective-permute-start | bytes 196616 | tf_op jit(solution)/shard_map/ppermute | solution.py:302
  6.4 2.2 %collective-permute-done.5.refs_6_ = bf16[64,512]{1,0:T(8,128)(2,1)S(1)} collective-permute-done((bf16[64,512]{1,0:T(8,128)(2,1)}, bf16[64,512]{1,0:T(8,128)(2,1)S(1)}, u32[]{:S(2)}, u32[]{:S(2)}) %collective-permute-start.5) | collective-permute-done | bytes 65568 | tf_op jit(solution)/shard_map/ppermute | solution.py:302
  8.6 3.0 %collective-permute-done.3.refs_4_ = bf16[64,512]{1,0:T(8,128)(2,1)S(1)} collective-permute-done((bf16[64,512]{1,0:T(8,128)(2,1)}, bf16[64,512]{1,0:T(8,128)(2,1)S(1)}, u32[]{:S(2)}, u32[]{:S(2)}) %collective-permute-start.3) | collective-permute-done | bytes 65568 | tf_op jit(solution)/shard_map/ppermute | solution.py:302
  12.1 0.7 %reshape.11.ids_ref = s32[8,512]{1,0:T(8,128)S(1)} reshape(s32[4096]{0:T(1024)} %param.6) | data formatting | bytes 32768 | tf_op jit(solution)/shard_map/reshape | solution.py:286
  12.8 1.0 %copy-done.1 = bf16[512,512]{1,0:T(8,128)(2,1)S(1)} copy-done((bf16[512,512]{1,0:T(8,128)(2,1)S(1)}, bf16[512,512]{1,0:T(8,128)(2,1)}, u32[]{:S(2)}) %copy-start.1) | copy-done | bytes 524312
  13.9 1.0 %copy-done.3 = bf16[512,512]{1,0:T(8,128)(2,1)S(1)} copy-done((bf16[512,512]{1,0:T(8,128)(2,1)S(1)}, bf16[512,512]{1,0:T(8,128)(2,1)}, u32[]{:S(2)}) %copy-start.3) | copy-done | bytes 524312
  15.6 1.2 %prep.1 = (bf16[320,512]{1,0:T(8,128)(2,1)S(1)}, bf16[320,512]{1,0:T(8,128)(2,1)S(1)}, bf16[320,512]{1,0:T(8,128)(2,1)S(1)}) custom-call(s32[1,8]{1,0:T(1,128)S(1)} %copy-done.5, s32[8,512]{1,0:T(8,128)S(1)} %reshape.11.ids_ref, bf16[512,512]{1,0:T(8,128)(2,1)S(1)} %copy-done.3, bf16[512,512]{1,0:T(8,128)(2,1)S(1)} %copy-done.1), custom_call_target="tpu_custom_call" | custom-call | tf_op jit(solution)/shard_map/prep/pallas_call | solution.py:288
  16.8 1.6 %copy-done = bf16[512,2048]{1,0:T(8,128)(2,1)S(1)} copy-done((bf16[512,2048]{1,0:T(8,128)(2,1)S(1)}, bf16[512,2048]{1,0:T(8,128)(2,1)}, u32[]{:S(2)}) %copy-start) | copy-done | bytes 2097176
  18.4 0.8 %copy-done.4 = bf16[512,64]{0,1:T(8,128)(2,1)S(1)} copy-done((bf16[512,64]{0,1:T(8,128)(2,1)S(1)}, bf16[512,64]{0,1:T(8,128)(2,1)}, u32[]{:S(2)}) %copy-start.4) | copy-done | bytes 65560
  19.9 12.0 %layer.1 = (bf16[320,512]{1,0:T(8,128)(2,1)S(1)}, bf16[512,512]{1,0:T(8,128)(2,1)S(1)}, bf16[256,1536]{1,0:T(8,128)(2,1)S(1)}, bf16[256,1536]{1,0:T(8,128)(2,1)S...) custom-call(s32[1,8]{1,0:T(1,128)S(1)} %copy-done.6, ...), custom_call_target="tpu_custom_call" | custom-call | tf_op jit(solution)/shard_map/layer/pallas_call | solution.py:324
  32.4 1.8 %collective-permute-done.7 = bf16[256,1536]{1,0:T(8,128)(2,1)S(1)} collective-permute-done((bf16[256,1536]{1,0:T(8,128)(2,1)S(1)}, bf16[256,1536]{1,0:T(8,128)(2,1)S(1)}, u32[]{:S(2)}, u32[]{:S(2)}) %collective-permute-start.7) | collective-permute-done | bytes 786464 | tf_op jit(solution)/shard_map/ppermute | solution.py:302
  34.4 0.9 %collective-permute-done.8 = bf16[256,1536]{1,0:T(8,128)(2,1)S(1)} collective-permute-done((bf16[256,1536]{1,0:T(8,128)(2,1)S(1)}, bf16[256,1536]{1,0:T(8,128)(2,1)S(1)}, u32[]{:S(2)}, u32[]{:S(2)}) %collective-permute-start.8) | collective-permute-done | bytes 786464 | tf_op jit(solution)/shard_map/ppermute | solution.py:302
  35.5 1.6 %collective-permute-start.10 = (bf16[128,1536]{1,0:T(8,128)(2,1)S(1)}, bf16[128,1536]{1,0:T(8,128)(2,1)S(1)}, u32[]{:S(2)}, u32[]{:S(2)}) collective-permute-start(bf16[128,1536]{1,0:T(8,128)(2,1)S(1)} %slice.39), channel_id=1, source_target_pairs={{0,16},{8,24},{16,0},{24,8},{1,17},{9,25},{17,1},{25,9},{2,18},{10... | collective-permute-start | bytes 1179656 | tf_op jit(solution)/shard_map/ppermute | solution.py:271
  37.2 1.6 %collective-permute-start.9 = (bf16[128,1536]{1,0:T(8,128)(2,1)S(1)}, bf16[128,1536]{1,0:T(8,128)(2,1)S(1)}, u32[]{:S(2)}, u32[]{:S(2)}) collective-permute-start(bf16[128,1536]{1,0:T(8,128)(2,1)S(1)} %slice.37), channel_id=1, source_target_pairs={{0,8},{8,0},{16,24},{24,16},{1,9},{9,1},{17,25},{25,17},{2,10},{10... | collective-permute-start | bytes 1179656 | tf_op jit(solution)/shard_map/ppermute | solution.py:271
  38.7 2.3 %out.1 = bf16[512,512]{1,0:T(8,128)(2,1)} custom-call(s32[1,8]{1,0:T(1,128)S(1)} %copy-done.6, s32[8,512]{1,0:T(8,128)S(1)} %reshape.11.ids_ref, bf16[512,512]{1,0:T(8,128)(2,1)S(1)} %get-tuple-element.25.tab_ref, bf16[320,512]{1,0:T(8,128)(2,1)S(1)} %get-tuple-element.31.gated_ref, bf16[512,512]{1,0:T(8,128)(2,1)S(1)} %copy-done.2), custom_call_target="tpu_custom_call" | custom-call | tf_op jit(solution)/shard_map/out/pallas_call | solution.py:345
  41.0 5.7 %collective-permute-done.10 = bf16[128,1536]{1,0:T(8,128)(2,1)S(1)} collective-permute-done((bf16[128,1536]{1,0:T(8,128)(2,1)S(1)}, bf16[128,1536]{1,0:T(8,128)(2,1)S(1)}, u32[]{:S(2)}, u32[]{:S(2)}) %collective-permute-start.10) | collective-permute-done | bytes 393248 | tf_op jit(solution)/shard_map/ppermute | solution.py:271
  46.9 1.2 %collective-permute-done.9 = bf16[128,1536]{1,0:T(8,128)(2,1)S(1)} collective-permute-done((bf16[128,1536]{1,0:T(8,128)(2,1)S(1)}, bf16[128,1536]{1,0:T(8,128)(2,1)S(1)}, u32[]{:S(2)}, u32[]{:S(2)}) %collective-permute-start.9) | collective-permute-done | bytes 393248 | tf_op jit(solution)/shard_map/ppermute | solution.py:271
  48.2 1.6 %collective-permute-start.12 = (bf16[64,1536]{1,0:T(8,128)(2,1)S(1)}, bf16[64,1536]{1,0:T(8,128)(2,1)S(1)}, u32[]{:S(2)}, u32[]{:S(2)}) collective-permute-start(bf16[64,1536]{1,0:T(8,128)(2,1)S(1)} %slice.43), channel_id=1, source_target_pairs={{0,8},{8,0},{16,24},{24,16},{1,9},{9,1},{17,25},{25,17},{2,10},{10... | collective-permute-start | bytes 589832 | tf_op jit(solution)/shard_map/ppermute | solution.py:271
  50.4 3.7 %collective-permute-done.12 = bf16[64,1536]{1,0:T(8,128)(2,1)S(1)} collective-permute-done((bf16[64,1536]{1,0:T(8,128)(2,1)S(1)}, bf16[64,1536]{1,0:T(8,128)(2,1)S(1)}, u32[]{:S(2)}, u32[]{:S(2)}) %collective-permute-start.12) | collective-permute-done | bytes 196640 | tf_op jit(solution)/shard_map/ppermute | solution.py:271
  54.1 1.4 %collective-permute-done.11 = bf16[64,1536]{1,0:T(8,128)(2,1)S(1)} collective-permute-done((bf16[64,1536]{1,0:T(8,128)(2,1)S(1)}, bf16[64,1536]{1,0:T(8,128)(2,1)S(1)}, u32[]{:S(2)}, u32[]{:S(2)}) %collective-permute-start.11) | collective-permute-done | bytes 196640 | tf_op jit(solution)/shard_map/ppermute | solution.py:271
  55.6 1.1 %collective-permute-start.13 = (bf16[32,3072]{1,0:T(8,128)(2,1)S(1)}, bf16[32,3072]{1,0:T(8,128)(2,1)S(1)}, u32[]{:S(2)}, u32[]{:S(2)}) collective-permute-start(bf16[32,3072]{1,0:T(8,128)(2,1)S(1)} %pad_maximum_fusion), channel_id=1, source_target_pairs={{0,2},{1,3},{2,0},{3,1},{4,6},{5,7},{6,4},{7,5},{8,10},{9,11},{10,... | collective-permute-start | bytes 589832 | tf_op jit(solution)/shard_map/ppermute | solution.py:269
  56.7 4.6 %collective-permute-done.13 = bf16[32,3072]{1,0:T(8,128)(2,1)S(1)} collective-permute-done((bf16[32,3072]{1,0:T(8,128)(2,1)S(1)}, bf16[32,3072]{1,0:T(8,128)(2,1)S(1)}, u32[]{:S(2)}, u32[]{:S(2)}) %collective-permute-start.13) | collective-permute-done | bytes 196640 | tf_op jit(solution)/shard_map/ppermute | solution.py:269
  61.4 1.5 %collective-permute-start.14 = (bf16[16,3072]{1,0:T(8,128)(2,1)S(1)}, bf16[16,3072]{1,0:T(8,128)(2,1)S(1)}, u32[]{:S(2)}, u32[]{:S(2)}) collective-permute-start(bf16[16,3072]{1,0:T(8,128)(2,1)S(1)} %get-tuple-element.40), channel_id=1, source_target_pairs={{0,4},{1,5},{2,6},{3,7},{4,0},{5,1},{6,2},{7,3},{8,12},{9,13},{10,... | collective-permute-start | bytes 294920 | tf_op jit(solution)/shard_map/ppermute | solution.py:269
  62.9 5.1 %collective-permute-done.14.got_ref = bf16[16,3072]{1,0:T(8,128)(2,1)S(1)} collective-permute-done((bf16[16,3072]{1,0:T(8,128)(2,1)S(1)}, bf16[16,3072]{1,0:T(8,128)(2,1)S(1)}, u32[]{:S(2)}, u32[]{:S(2)}) %collective-permute-start.14) | collective-permute-done | bytes 98336 | tf_op jit(solution)/shard_map/ppermute | solution.py:269
  (38 shorter events, 5.1 us)
Async XLA Ops:
  0.6 7.9 %collective-permute-start.5 = (bf16[64,512]{1,0:T(8,128)(2,1)}, bf16[64,512]{1,0:T(8,128)(2,1)S(1)}, u32[]{:S(2)}, u32[]{:S(2)}) collective-permute-start(bf16[64,512]{1,0:T(8,128)(2,1)} %bitcast.2), channel_id=1, source_target_pairs={{0,6},{1,7},{2,4},{3,5},{4,2},{5,3},{6,0},{7,1},{8,14},{9,15},{10,... | collective-permute-start | bytes 196616 | tf_op jit(solution)/shard_map/ppermute | solution.py:302
  5.8 5.8 %collective-permute-start.3 = (bf16[64,512]{1,0:T(8,128)(2,1)}, bf16[64,512]{1,0:T(8,128)(2,1)S(1)}, u32[]{:S(2)}, u32[]{:S(2)}) collective-permute-start(bf16[64,512]{1,0:T(8,128)(2,1)} %bitcast.3), channel_id=1, source_target_pairs={{0,4},{1,5},{2,6},{3,7},{4,0},{5,1},{6,2},{7,3},{8,12},{9,13},{10,... | collective-permute-start | bytes 196616 | tf_op jit(solution)/shard_map/ppermute | solution.py:302
  5.8 5.8 %collective-permute-start.1 = (bf16[64,512]{1,0:T(8,128)(2,1)}, bf16[64,512]{1,0:T(8,128)(2,1)S(1)}, u32[]{:S(2)}, u32[]{:S(2)}) collective-permute-start(bf16[64,512]{1,0:T(8,128)(2,1)} %bitcast.4), channel_id=1, source_target_pairs={{0,2},{1,3},{2,0},{3,1},{4,6},{5,7},{6,4},{7,5},{8,10},{9,11},{10,... | collective-permute-start | bytes 196616 | tf_op jit(solution)/shard_map/ppermute | solution.py:302
  6.4 10.3 %collective-permute-start = (bf16[64,512]{1,0:T(8,128)(2,1)}, bf16[64,512]{1,0:T(8,128)(2,1)S(1)}, u32[]{:S(2)}, u32[]{:S(2)}) collective-permute-start(bf16[64,512]{1,0:T(8,128)(2,1)} %bitcast.5), channel_id=1, source_target_pairs={{0,1},{1,0},{2,3},{3,2},{4,5},{5,4},{6,7},{7,6},{8,9},{9,8},{10,11... | collective-permute-start | bytes 196616 | tf_op jit(solution)/shard_map/ppermute | solution.py:302
  8.6 8.2 %collective-permute-start.6 = (bf16[64,512]{1,0:T(8,128)(2,1)S(1)}, bf16[64,512]{1,0:T(8,128)(2,1)S(1)}, u32[]{:S(2)}, u32[]{:S(2)}) collective-permute-start(bf16[64,512]{1,0:T(8,128)(2,1)S(1)} %collective-permute-done.5.refs_6_), channel_id=1, source_target_pairs={{0,1},{1,0},{2,3},{3,2},{4,5},{5,4},{6,7},{7,6},{8,9},{9,8},{10,11... | collective-permute-start | bytes 196616 | tf_op jit(solution)/shard_map/ppermute | solution.py:302
  11.6 5.2 %collective-permute-start.4 = (bf16[64,512]{1,0:T(8,128)(2,1)S(1)}, bf16[64,512]{1,0:T(8,128)(2,1)S(1)}, u32[]{:S(2)}, u32[]{:S(2)}) collective-permute-start(bf16[64,512]{1,0:T(8,128)(2,1)S(1)} %collective-permute-done.3.refs_4_), channel_id=1, source_target_pairs={{0,1},{1,0},{2,3},{3,2},{4,5},{5,4},{6,7},{7,6},{8,9},{9,8},{10,11... | collective-permute-start | bytes 196616 | tf_op jit(solution)/shard_map/ppermute | solution.py:302
  11.6 5.2 %collective-permute-start.2 = (bf16[64,512]{1,0:T(8,128)(2,1)S(1)}, bf16[64,512]{1,0:T(8,128)(2,1)S(1)}, u32[]{:S(2)}, u32[]{:S(2)}) collective-permute-start(bf16[64,512]{1,0:T(8,128)(2,1)S(1)} %collective-permute-done.1.refs_2_), channel_id=1, source_target_pairs={{0,1},{1,0},{2,3},{3,2},{4,5},{5,4},{6,7},{7,6},{8,9},{9,8},{10,11... | collective-permute-start | bytes 196616 | tf_op jit(solution)/shard_map/ppermute | solution.py:302
  12.8 1.0 %copy-start.1 = (bf16[512,512]{1,0:T(8,128)(2,1)S(1)}, bf16[512,512]{1,0:T(8,128)(2,1)}, u32[]{:S(2)}) copy-start(bf16[512,512]{1,0:T(8,128)(2,1)} %wout_ref.3) | copy-start | bytes 1572868
  13.9 1.0 %copy-start.3 = (bf16[512,512]{1,0:T(8,128)(2,1)S(1)}, bf16[512,512]{1,0:T(8,128)(2,1)}, u32[]{:S(2)}) copy-start(bf16[512,512]{1,0:T(8,128)(2,1)} %cot_ref.1) | copy-start | bytes 1572868
  14.9 0.7 copy-start.5
  16.8 1.6 %copy-start = (bf16[512,2048]{1,0:T(8,128)(2,1)S(1)}, bf16[512,2048]{1,0:T(8,128)(2,1)}, u32[]{:S(2)}) copy-start(bf16[512,2048]{1,0:T(8,128)(2,1)} %w_ref.1) | copy-start | bytes 6291460
  18.4 0.8 %copy-start.4 = (bf16[512,64]{0,1:T(8,128)(2,1)S(1)}, bf16[512,64]{0,1:T(8,128)(2,1)}, u32[]{:S(2)}) copy-start(bf16[512,64]{0,1:T(8,128)(2,1)} %param.8) | copy-start | bytes 196612
  19.2 0.7 copy-start.6
  31.8 2.4 %collective-permute-start.7 = (bf16[256,1536]{1,0:T(8,128)(2,1)S(1)}, bf16[256,1536]{1,0:T(8,128)(2,1)S(1)}, u32[]{:S(2)}, u32[]{:S(2)}) collective-permute-start(bf16[256,1536]{1,0:T(8,128)(2,1)S(1)} %get-tuple-element.28), channel_id=1, source_target_pairs={{0,1},{1,0},{2,3},{3,2},{4,5},{5,4},{6,7},{7,6},{8,9},{9,8},{10,11... | collective-permute-start | bytes 2359304 | tf_op jit(solution)/shard_map/ppermute | solution.py:302
  31.9 3.4 %collective-permute-start.8 = (bf16[256,1536]{1,0:T(8,128)(2,1)S(1)}, bf16[256,1536]{1,0:T(8,128)(2,1)S(1)}, u32[]{:S(2)}, u32[]{:S(2)}) collective-permute-start(bf16[256,1536]{1,0:T(8,128)(2,1)S(1)} %get-tuple-element.30), channel_id=1, source_target_pairs={{0,1},{1,0},{2,3},{3,2},{4,5},{5,4},{6,7},{7,6},{8,9},{9,8},{10,11... | collective-permute-start | bytes 2359304 | tf_op jit(solution)/shard_map/ppermute | solution.py:302
  35.3 3.4 %copy-start.2 = (bf16[512,512]{1,0:T(8,128)(2,1)S(1)}, bf16[512,512]{1,0:T(8,128)(2,1)}, u32[]{:S(2)}) copy-start(bf16[512,512]{1,0:T(8,128)(2,1)} %wout_ref.3) | copy-start | bytes 1572868
  35.5 11.2 %collective-permute-start.10 = (bf16[128,1536]{1,0:T(8,128)(2,1)S(1)}, bf16[128,1536]{1,0:T(8,128)(2,1)S(1)}, u32[]{:S(2)}, u32[]{:S(2)}) collective-permute-start(bf16[128,1536]{1,0:T(8,128)(2,1)S(1)} %slice.39), channel_id=1, source_target_pairs={{0,16},{8,24},{16,0},{24,8},{1,17},{9,25},{17,1},{25,9},{2,18},{10... | collective-permute-start | bytes 1179656 | tf_op jit(solution)/shard_map/ppermute | solution.py:271
  37.2 10.9 %collective-permute-start.9 = (bf16[128,1536]{1,0:T(8,128)(2,1)S(1)}, bf16[128,1536]{1,0:T(8,128)(2,1)S(1)}, u32[]{:S(2)}, u32[]{:S(2)}) collective-permute-start(bf16[128,1536]{1,0:T(8,128)(2,1)S(1)} %slice.37), channel_id=1, source_target_pairs={{0,8},{8,0},{16,24},{24,16},{1,9},{9,1},{17,25},{25,17},{2,10},{10... | collective-permute-start | bytes 1179656 | tf_op jit(solution)/shard_map/ppermute | solution.py:271
  48.2 5.9 %collective-permute-start.12 = (bf16[64,1536]{1,0:T(8,128)(2,1)S(1)}, bf16[64,1536]{1,0:T(8,128)(2,1)S(1)}, u32[]{:S(2)}, u32[]{:S(2)}) collective-permute-start(bf16[64,1536]{1,0:T(8,128)(2,1)S(1)} %slice.43), channel_id=1, source_target_pairs={{0,8},{8,0},{16,24},{24,16},{1,9},{9,1},{17,25},{25,17},{2,10},{10... | collective-permute-start | bytes 589832 | tf_op jit(solution)/shard_map/ppermute | solution.py:271
  49.8 5.7 %collective-permute-start.11 = (bf16[64,1536]{1,0:T(8,128)(2,1)S(1)}, bf16[64,1536]{1,0:T(8,128)(2,1)S(1)}, u32[]{:S(2)}, u32[]{:S(2)}) collective-permute-start(bf16[64,1536]{1,0:T(8,128)(2,1)S(1)} %slice.41), channel_id=1, source_target_pairs={{0,16},{8,24},{16,0},{24,8},{1,17},{9,25},{17,1},{25,9},{2,18},{10... | collective-permute-start | bytes 589832 | tf_op jit(solution)/shard_map/ppermute | solution.py:271
  55.6 5.7 %collective-permute-start.13 = (bf16[32,3072]{1,0:T(8,128)(2,1)S(1)}, bf16[32,3072]{1,0:T(8,128)(2,1)S(1)}, u32[]{:S(2)}, u32[]{:S(2)}) collective-permute-start(bf16[32,3072]{1,0:T(8,128)(2,1)S(1)} %pad_maximum_fusion), channel_id=1, source_target_pairs={{0,2},{1,3},{2,0},{3,1},{4,6},{5,7},{6,4},{7,5},{8,10},{9,11},{10,... | collective-permute-start | bytes 589832 | tf_op jit(solution)/shard_map/ppermute | solution.py:269
  61.4 6.6 %collective-permute-start.14 = (bf16[16,3072]{1,0:T(8,128)(2,1)S(1)}, bf16[16,3072]{1,0:T(8,128)(2,1)S(1)}, u32[]{:S(2)}, u32[]{:S(2)}) collective-permute-start(bf16[16,3072]{1,0:T(8,128)(2,1)S(1)} %get-tuple-element.40), channel_id=1, source_target_pairs={{0,4},{1,5},{2,6},{3,7},{4,0},{5,1},{6,2},{7,3},{8,12},{9,13},{10,... | collective-permute-start | bytes 294920 | tf_op jit(solution)/shard_map/ppermute | solution.py:269

commit v3 on v2

--- a/solution.py
+++ b/solution.py
@@ -6,7 +6,7 @@
 from jax.experimental.pallas import tpu as pltpu
 from jax.sharding import PartitionSpec as P
 
-H = 8
+
 DH = 64
 MAXLEN = 64
 LANES = 128
@@ -49,25 +49,43 @@
     return start
 
 
-def prep_kernel(len_ref, ids_ref, cot_ref, wout_ref, onehot_ref, outg_ref, gg_ref):
+def prep_kernel(
+    len_hbm, ids_ref, cot_hbm, wout_hbm, w_hbm, mine_hbm,
+    onehot_ref, outg_ref, gg_ref, start_ref, origin_ref, w_ref, mine_ref,
+    len_ref, cot_ref, wout_ref, sems,
+):
+    moves = [
+        pltpu.make_async_copy(src, dst, sems.at[n])
+        for n, (src, dst) in enumerate(
+            ((len_hbm, len_ref), (cot_hbm, cot_ref), (wout_hbm, wout_ref), (w_hbm, w_ref), (mine_hbm, mine_ref))
+        )
+    ]
+    for move in moves:
+        move.start()
     histories = len_ref.shape[1]
     live, items = onehot_ref.shape
     rows = ids_ref.shape[1]
     own = lax.axis_index("table")
     ids = ids_ref[pl.ds(own, 1), :].astype(F32)
+    moves[0].wait()
+    start_ref[...] = start_of(lax.broadcasted_iota(jnp.int32, start_ref.shape, 0), len_ref, histories)
+    origin_ref[...] = origin_of(lax.broadcasted_iota(jnp.int32, origin_ref.shape, 1), len_ref, histories)
     packed = lax.broadcasted_iota(jnp.int32, (live, rows), 0)
     take = origin_of(packed, len_ref, histories) == lax.broadcasted_iota(jnp.int32, (live, rows), 1)
     own_id = jnp.sum(jnp.where(take, ids, 0.0), axis=1, keepdims=True).astype(jnp.int32)
     onehot_ref[...] = jnp.where(
         lax.broadcasted_iota(jnp.int32, (live, items), 1) == own_id, 1.0, 0.0
     ).astype(BF)
+    moves[1].wait()
     out_grad = nn(jnp.where(take, 1.0, 0.0).astype(BF), cot_ref[...]).astype(BF)
     outg_ref[...] = out_grad
+    moves[2].wait()
     gg_ref[...] = nt(out_grad, wout_ref[...]).astype(BF)
-
-
-def out_kernel(len_ref, ids_ref, tab_ref, gated_ref, wout_ref, out_ref):
-    histories = len_ref.shape[1]
+    moves[3].wait()
+    moves[4].wait()
+
+
+def out_kernel(origin_ref, ids_ref, tab_ref, gated_ref, wout_ref, out_ref):
     rows = ids_ref.shape[1]
     live = gated_ref.shape[0]
     items = tab_ref.shape[1]
@@ -78,14 +96,13 @@
     onehot = jnp.concatenate(
         [jnp.where(ids_col == lane + k, 1.0, 0.0).astype(BF) for k in range(0, items, LANES)], axis=1
     )
-    packed = lax.broadcasted_iota(jnp.int32, (rows, live), 1)
-    put = origin_of(packed, len_ref, histories) == lax.broadcasted_iota(jnp.int32, (rows, live), 0)
+    put = origin_ref[0:1, :] == lax.broadcasted_iota(jnp.int32, (rows, live), 0)
     gated = nn(jnp.where(put, 1.0, 0.0).astype(BF), gated_ref[...]).astype(BF)
     out_ref[...] = (nt(onehot, tab_ref[...]) + nn(gated, wout_ref[...])).astype(BF)
 
 
-def layer_kernel(order, shape, len_ref, onehot_ref, outg_ref, gg_ref, w_ref, *refs):
-    dps, tabs = shape
+def layer_kernel(order, shape, start_ref, onehot_ref, outg_ref, gg_ref, w_ref, *refs):
+    _, tabs = shape
     pieces, refs = refs[:tabs], refs[tabs:]
     gated_ref, tab_ref = refs[:2]
     grads, scratch = refs[2:-9], refs[-9:]
@@ -94,14 +111,13 @@
         feats = pieces[rel].shape[0]
         at = pl.multiple_of((me_tab ^ rel) * feats, feats)
         tab_ref[pl.ds(at, feats), :] = pieces[rel][...]
-    layer_body(order, shape, len_ref, tab_ref, onehot_ref, outg_ref, gg_ref, w_ref, gated_ref, grads, *scratch)
+    layer_body(order, shape, start_ref, tab_ref, onehot_ref, outg_ref, gg_ref, w_ref, gated_ref, grads, *scratch)
 
 
 def layer_body(
-    order, shape, len_ref, tab_ref, onehot_ref, outg_ref, gg_ref, w_ref, gated_ref, grads,
+    order, shape, start_ref, tab_ref, onehot_ref, outg_ref, gg_ref, w_ref, gated_ref, grads,
     act_ref, dact_ref, fac_ref, att_ref, attended_ref, dkv_ref, pg_ref, tmp_ref, lhs_ref,
 ):
-    histories = len_ref.shape[1]
     live, items = onehot_ref.shape
     width = tab_ref.shape[0]
     dps, tabs = shape
@@ -141,7 +157,7 @@
         w0 = max(t - 1, 0) * MAXLEN
         row = r0 + lax.broadcasted_iota(jnp.int32, (MAXLEN, LANES), 0)
         col = w0 + lax.broadcasted_iota(jnp.int32, (MAXLEN, LANES), 1)
-        seen = (col >= start_of(row, len_ref, histories)) & (col <= row)
+        seen = (col >= start_ref[r0 : r0 + MAXLEN, :]) & (col <= row)
         mask = jnp.where(seen, 1.0 / MAXLEN, 0.0)
         mask = jnp.concatenate([mask, mask], axis=0)
         for c in range(pairs):
@@ -261,7 +277,11 @@
 
 
 VMEM_SPEC = pl.BlockSpec(memory_space=pltpu.VMEM)
-SMEM_SPEC = pl.BlockSpec(memory_space=pltpu.SMEM)
+HBM_SPEC = pl.BlockSpec(memory_space=pltpu.HBM)
+
+
+def in_hbm(v):
+    return pltpu.with_memory_space_constraint(v, pltpu.HBM)
 
 
 def swap(v, bit, tab_bits, dps, tabs):
@@ -271,7 +291,7 @@
     return lax.ppermute(v, "dp", [(i, i ^ (1 << b)) for i in range(dps)])
 
 
-def local(ids, lengths, table, w_uvqk, w_out, cotangent):
+def layer(ids, lengths, table, w_uvqk, w_out, cotangent):
     tabs = lax.axis_size("table")
     dps = lax.axis_size("dp")
     devices = tabs * dps
@@ -285,33 +305,45 @@
     width = feats * tabs
     ids2 = ids.reshape(tabs, rows)
 
-    onehot, outg, gg = pl.pallas_call(
+    sds = jax.ShapeDtypeStruct
+
+    def other(v, rel):
+        return lax.ppermute(v, "table", [(i, i ^ rel) for i in range(tabs)])
+
+    mine = table.T
+    far = {}
+    for rel in range(2, tabs, 2):
+        far[rel] = other(mine, rel)
+    onehot, outg, gg, start, origin, w_near, mine_near = pl.pallas_call(
         prep_kernel,
         out_shape=(
-            jax.ShapeDtypeStruct((live, items), BF),
-            jax.ShapeDtypeStruct((live, width), BF),
-            jax.ShapeDtypeStruct((live, width), BF),
+            sds((live, items), BF),
+            sds((live, width), BF),
+            sds((live, width), BF),
+            sds((live, LANES), jnp.int32),
+            sds((8, live), jnp.int32),
+            sds(w_uvqk.shape, BF),
+            sds(mine.shape, BF),
         ),
-        in_specs=[SMEM_SPEC, VMEM_SPEC, VMEM_SPEC, VMEM_SPEC],
-        out_specs=(VMEM_SPEC,) * 3,
+        in_specs=[HBM_SPEC, VMEM_SPEC] + [HBM_SPEC] * 4,
+        out_specs=(VMEM_SPEC,) * 7,
+        scratch_shapes=[
+            pltpu.SMEM(lengths.shape, jnp.int32),
+            pltpu.VMEM(cotangent.shape, BF),
+            pltpu.VMEM(w_out.shape, BF),
+            pltpu.SemaphoreType.DMA((5,)),
+        ],
         compiler_params=pltpu.CompilerParams(vmem_limit_bytes=16 << 20),
         name="prep",
-    )(lengths, ids2, cotangent, w_out)
-
-    def other(v, rel):
-        return lax.ppermute(v, "table", [(i, i ^ rel) for i in range(tabs)])
-
-    mine = table.T
-    pieces = []
-    for rel in range(0, tabs, 2):
-        piece = other(mine, rel) if rel else mine
-        pieces += [piece, other(piece, 1)]
+    )(in_hbm(lengths), ids2, *map(in_hbm, (cotangent, w_out, w_uvqk, mine)))
+    pieces = [mine_near, other(mine, 1)]
+    for rel in range(2, tabs, 2):
+        pieces += [far[rel], other(far[rel], 1)]
 
     dp_order = list(range(tab_bits, bits))
     z_order = list(range(1, tab_bits))
     order = ([0] + dp_order + z_order, [0] + dp_order[::-1] + z_order)
     w1 = 3 * width
-    sds = jax.ShapeDtypeStruct
     blk = width // devices
     span = items // dps
     halving = blk % 16 == 0 and feats % blk == 0 and span == LANES and width % (feats // blk * span) == 0
@@ -324,7 +356,7 @@
     gated, tab_t, *grads = pl.pallas_call(
         functools.partial(layer_kernel, order, (dps, tabs)),
         out_shape=(sds((live, width), BF), sds((width, items), BF)) + grad_shapes,
-        in_specs=[SMEM_SPEC] + [VMEM_SPEC] * (4 + tabs),
+        in_specs=[VMEM_SPEC] * (5 + tabs),
         out_specs=(VMEM_SPEC,) * (2 + len(grad_shapes)),
         scratch_shapes=[
             pltpu.VMEM((live, 4 * width), BF),
@@ -339,17 +371,17 @@
         ],
         compiler_params=pltpu.CompilerParams(vmem_limit_bytes=32 << 20),
         name="layer",
-    )(lengths, onehot, outg, gg, w_uvqk, *pieces)
+    )(start, onehot, outg, gg, w_near, *pieces)
 
     def finish_output(gated):
         return pl.pallas_call(
             out_kernel,
             out_shape=sds((rows, width), BF),
-            in_specs=[SMEM_SPEC] + [VMEM_SPEC] * 4,
+            in_specs=[VMEM_SPEC] * 5,
             out_specs=VMEM_SPEC,
             compiler_params=pltpu.CompilerParams(vmem_limit_bytes=16 << 20),
         name="out",
-        )(lengths, ids2, tab_t, gated, w_out)
+        )(origin, ids2, tab_t, gated, w_out)
 
     if not halving:
         grad_o, grad_u, grad_t = grads
@@ -397,7 +429,7 @@
 
 def solution(mesh):
     return jax.shard_map(
-        local,
+        layer,
         mesh=mesh,
         in_specs=(
             P("dp"),

time: 69.1 us -> 63.4 us (0.918)
  local copies, waits for them, and re-layouts: 6.64 us -> 0.82 us
    unnamed x14 -> x2, local copies, waits for them, and re-layouts: 5.82 us -> 0.01 us
  transfers between devices with their start and end apart: 15 -> 15, of which waited for: 10 -> 10; matrix products, arithmetic and copies ran while one was open for 2% -> 2% of each run, Pallas kernels for 5% -> 6%
where the time goes in v3:
time: 63.4 us; the launch traced here: 63.1 us
  waiting for transfers between devices  30.2 us (48%)
  Pallas kernels  15.8 us (25%)
  starting transfers between devices  14.8 us (23%)
  local copies, waits for them, and re-layouts  0.82 us (1%)
  between operations  0.76 us (1%)
  other arithmetic  0.72 us (1%)
    ppermute x4, waiting for transfers between devices, swap(): return lax.ppermute(v, 'dp', [(i, i ^ 1 << b) for i in range(dps)])  12.6 us
    pallas_call x1, Pallas kernels, layer(): pl.pallas_call(functools.partial(layer_kernel, order, (dps, tabs)), out_s...  11.4 us
    ppermute x2, waiting for transfers between devices, swap(): return lax.ppermute(v, 'table', [(i, i ^ 1 << bit) for i in range(tabs)])  9.73 us
    ppermute x9, waiting for transfers between devices, other(): return lax.ppermute(v, 'table', [(i, i ^ rel) for i in range(tabs)])  7.88 us
    ppermute x9, starting transfers between devices, other(): return lax.ppermute(v, 'table', [(i, i ^ rel) for i in range(tabs)])  6.87 us
    ppermute x4, starting transfers between devices, swap(): return lax.ppermute(v, 'dp', [(i, i ^ 1 << b) for i in range(dps)])  5.26 us
    ppermute x2, starting transfers between devices, swap(): return lax.ppermute(v, 'table', [(i, i ^ 1 << bit) for i in range(tabs)])  2.64 us
    pallas_call x1, Pallas kernels, layer(): pl.pallas_call(prep_kernel, out_shape=(sds((live, items), BF), sds((live,...  1.97 us
  transfers between devices with their start and end apart: 15, of which 10 were waited for; matrix products, arithmetic and copies ran while one was open for 2% of the time, Pallas kernels for 6%

profile of v3, /device:TPU:0, one launch (start us, length us, event | category | flops | bytes accessed | tf_op | source)
XLA Modules:
  0.0 63.1 jit_solution(2441487838203240124)
XLA Ops:
  0.6 5.1 %collective-permute-start.5 = (bf16[64,512]{1,0:T(8,128)(2,1)}, bf16[64,512]{1,0:T(8,128)(2,1)S(1)}, u32[]{:S(2)}, u32[]{:S(2)}) collective-permute-start(bf16[64,512]{1,0:T(8,128)(2,1)} %bitcast.2), channel_id=1, source_target_pairs={{0,6},{1,7},{2,4},{3,5},{4,2},{5,3},{6,0},{7,1},{8,14},{9,15},{10,... | collective-permute-start | bytes 196616 | tf_op jit(solution)/shard_map/ppermute | solution.py:311
  5.8 0.6 %collective-permute-start.1 = (bf16[64,512]{1,0:T(8,128)(2,1)}, bf16[64,512]{1,0:T(8,128)(2,1)S(1)}, u32[]{:S(2)}, u32[]{:S(2)}) collective-permute-start(bf16[64,512]{1,0:T(8,128)(2,1)} %bitcast.4), channel_id=1, source_target_pairs={{0,2},{1,3},{2,0},{3,1},{4,6},{5,7},{6,4},{7,5},{8,10},{9,11},{10,... | collective-permute-start | bytes 196616 | tf_op jit(solution)/shard_map/ppermute | solution.py:311
  6.4 2.2 %collective-permute-done.5.refs_6_ = bf16[64,512]{1,0:T(8,128)(2,1)S(1)} collective-permute-done((bf16[64,512]{1,0:T(8,128)(2,1)}, bf16[64,512]{1,0:T(8,128)(2,1)S(1)}, u32[]{:S(2)}, u32[]{:S(2)}) %collective-permute-start.5) | collective-permute-done | bytes 65568 | tf_op jit(solution)/shard_map/ppermute | solution.py:311
  8.6 3.0 %collective-permute-done.3.refs_4_ = bf16[64,512]{1,0:T(8,128)(2,1)S(1)} collective-permute-done((bf16[64,512]{1,0:T(8,128)(2,1)}, bf16[64,512]{1,0:T(8,128)(2,1)S(1)}, u32[]{:S(2)}, u32[]{:S(2)}) %collective-permute-start.3) | collective-permute-done | bytes 65568 | tf_op jit(solution)/shard_map/ppermute | solution.py:311
  11.6 0.5 collective-permute-start.2
  12.1 0.7 %reshape.11.ids_ref = s32[8,512]{1,0:T(8,128)S(1)} reshape(s32[4096]{0:T(1024)} %param.6) | data formatting | bytes 32768 | tf_op jit(solution)/shard_map/reshape | solution.py:306
  12.8 2.0 %prep.1 = (bf16[320,512]{1,0:T(8,128)(2,1)S(1)}, bf16[320,512]{1,0:T(8,128)(2,1)S(1)}, bf16[320,512]{1,0:T(8,128)(2,1)S(1)}, s32[320,128]{1,0:T(8,128)S(1)}, s32...) custom-call(s32[1,8]{1,0:T(1,128)} %len_hbm.1, s32[8,512]{1,0:T(8,128)S(1)} %reshape.11.ids_ref, ...), custom_call_target="tpu_custom_call" | custom-call | tf_op jit(solution)/shard_map/prep/pallas_call | solution.py:317
  14.8 11.4 %layer.1 = (bf16[320,512]{1,0:T(8,128)(2,1)S(1)}, bf16[512,512]{1,0:T(8,128)(2,1)S(1)}, bf16[256,1536]{1,0:T(8,128)(2,1)S(1)}, bf16[256,1536]{1,0:T(8,128)(2,1)S...) custom-call(s32[320,128]{1,0:T(8,128)S(1)} %get-tuple-element.27.start_ref, ...), custom_call_target="tpu_custom_call" | custom-call | tf_op jit(solution)/shard_map/layer/pallas_call | solution.py:356
  26.8 1.8 %collective-permute-done.7 = bf16[256,1536]{1,0:T(8,128)(2,1)S(1)} collective-permute-done((bf16[256,1536]{1,0:T(8,128)(2,1)S(1)}, bf16[256,1536]{1,0:T(8,128)(2,1)S(1)}, u32[]{:S(2)}, u32[]{:S(2)}) %collective-permute-start.7) | collective-permute-done | bytes 786464 | tf_op jit(solution)/shard_map/ppermute | solution.py:311
  28.8 0.9 %collective-permute-done.8 = bf16[256,1536]{1,0:T(8,128)(2,1)S(1)} collective-permute-done((bf16[256,1536]{1,0:T(8,128)(2,1)S(1)}, bf16[256,1536]{1,0:T(8,128)(2,1)S(1)}, u32[]{:S(2)}, u32[]{:S(2)}) %collective-permute-start.8) | collective-permute-done | bytes 786464 | tf_op jit(solution)/shard_map/ppermute | solution.py:311
  29.9 1.6 %collective-permute-start.10 = (bf16[128,1536]{1,0:T(8,128)(2,1)S(1)}, bf16[128,1536]{1,0:T(8,128)(2,1)S(1)}, u32[]{:S(2)}, u32[]{:S(2)}) collective-permute-start(bf16[128,1536]{1,0:T(8,128)(2,1)S(1)} %slice.39), channel_id=1, source_target_pairs={{0,16},{8,24},{16,0},{24,8},{1,17},{9,25},{17,1},{25,9},{2,18},{10... | collective-permute-start | bytes 1179656 | tf_op jit(solution)/shard_map/ppermute | solution.py:291
  31.5 1.6 %collective-permute-start.9 = (bf16[128,1536]{1,0:T(8,128)(2,1)S(1)}, bf16[128,1536]{1,0:T(8,128)(2,1)S(1)}, u32[]{:S(2)}, u32[]{:S(2)}) collective-permute-start(bf16[128,1536]{1,0:T(8,128)(2,1)S(1)} %slice.37), channel_id=1, source_target_pairs={{0,8},{8,0},{16,24},{24,16},{1,9},{9,1},{17,25},{25,17},{2,10},{10... | collective-permute-start | bytes 1179656 | tf_op jit(solution)/shard_map/ppermute | solution.py:291
  33.1 1.8 %out.1 = bf16[512,512]{1,0:T(8,128)(2,1)} custom-call(s32[8,320]{1,0:T(8,128)S(1)} %get-tuple-element.26.origin_ref, s32[8,512]{1,0:T(8,128)S(1)} %reshape.11.ids_ref, bf16[512,512]{1,0:T(8,128)(2,1)S(1)} %get-tuple-element.33.tab_ref, bf16[320,512]{1,0:T(8,128)(2,1)S(1)} %get-tuple-element.39.gated_ref, bf16[512,512]{1,0:T(8,128)(2,1)S(1)} %copy-done), custom_call_target="tpu_custom_call" | custom-call | tf_op jit(solution)/shard_map/out/pallas_call | solution.py:377
  34.9 6.3 %collective-permute-done.10 = bf16[128,1536]{1,0:T(8,128)(2,1)S(1)} collective-permute-done((bf16[128,1536]{1,0:T(8,128)(2,1)S(1)}, bf16[128,1536]{1,0:T(8,128)(2,1)S(1)}, u32[]{:S(2)}, u32[]{:S(2)}) %collective-permute-start.10) | collective-permute-done | bytes 393248 | tf_op jit(solution)/shard_map/ppermute | solution.py:291
  41.2 1.2 %collective-permute-done.9 = bf16[128,1536]{1,0:T(8,128)(2,1)S(1)} collective-permute-done((bf16[128,1536]{1,0:T(8,128)(2,1)S(1)}, bf16[128,1536]{1,0:T(8,128)(2,1)S(1)}, u32[]{:S(2)}, u32[]{:S(2)}) %collective-permute-start.9) | collective-permute-done | bytes 393248 | tf_op jit(solution)/shard_map/ppermute | solution.py:291
  42.6 1.6 %collective-permute-start.12 = (bf16[64,1536]{1,0:T(8,128)(2,1)S(1)}, bf16[64,1536]{1,0:T(8,128)(2,1)S(1)}, u32[]{:S(2)}, u32[]{:S(2)}) collective-permute-start(bf16[64,1536]{1,0:T(8,128)(2,1)S(1)} %slice.43), channel_id=1, source_target_pairs={{0,8},{8,0},{16,24},{24,16},{1,9},{9,1},{17,25},{25,17},{2,10},{10... | collective-permute-start | bytes 589832 | tf_op jit(solution)/shard_map/ppermute | solution.py:291
  44.2 0.6 collective-permute-start.11
  44.7 3.7 %collective-permute-done.12 = bf16[64,1536]{1,0:T(8,128)(2,1)S(1)} collective-permute-done((bf16[64,1536]{1,0:T(8,128)(2,1)S(1)}, bf16[64,1536]{1,0:T(8,128)(2,1)S(1)}, u32[]{:S(2)}, u32[]{:S(2)}) %collective-permute-start.12) | collective-permute-done | bytes 196640 | tf_op jit(solution)/shard_map/ppermute | solution.py:291
  48.5 1.4 %collective-permute-done.11 = bf16[64,1536]{1,0:T(8,128)(2,1)S(1)} collective-permute-done((bf16[64,1536]{1,0:T(8,128)(2,1)S(1)}, bf16[64,1536]{1,0:T(8,128)(2,1)S(1)}, u32[]{:S(2)}, u32[]{:S(2)}) %collective-permute-start.11) | collective-permute-done | bytes 196640 | tf_op jit(solution)/shard_map/ppermute | solution.py:291
  50.0 1.1 %collective-permute-start.13 = (bf16[32,3072]{1,0:T(8,128)(2,1)S(1)}, bf16[32,3072]{1,0:T(8,128)(2,1)S(1)}, u32[]{:S(2)}, u32[]{:S(2)}) collective-permute-start(bf16[32,3072]{1,0:T(8,128)(2,1)S(1)} %pad_maximum_fusion), channel_id=1, source_target_pairs={{0,2},{1,3},{2,0},{3,1},{4,6},{5,7},{6,4},{7,5},{8,10},{9,11},{10,... | collective-permute-start | bytes 589832 | tf_op jit(solution)/shard_map/ppermute | solution.py:289
  51.1 4.6 %collective-permute-done.13 = bf16[32,3072]{1,0:T(8,128)(2,1)S(1)} collective-permute-done((bf16[32,3072]{1,0:T(8,128)(2,1)S(1)}, bf16[32,3072]{1,0:T(8,128)(2,1)S(1)}, u32[]{:S(2)}, u32[]{:S(2)}) %collective-permute-start.13) | collective-permute-done | bytes 196640 | tf_op jit(solution)/shard_map/ppermute | solution.py:289
  55.8 1.5 %collective-permute-start.14 = (bf16[16,3072]{1,0:T(8,128)(2,1)S(1)}, bf16[16,3072]{1,0:T(8,128)(2,1)S(1)}, u32[]{:S(2)}, u32[]{:S(2)}) collective-permute-start(bf16[16,3072]{1,0:T(8,128)(2,1)S(1)} %get-tuple-element.48), channel_id=1, source_target_pairs={{0,4},{1,5},{2,6},{3,7},{4,0},{5,1},{6,2},{7,3},{8,12},{9,13},{10,... | collective-permute-start | bytes 294920 | tf_op jit(solution)/shard_map/ppermute | solution.py:289
  57.3 5.1 %collective-permute-done.14.got_ref = bf16[16,3072]{1,0:T(8,128)(2,1)S(1)} collective-permute-done((bf16[16,3072]{1,0:T(8,128)(2,1)S(1)}, bf16[16,3072]{1,0:T(8,128)(2,1)S(1)}, u32[]{:S(2)}, u32[]{:S(2)}) %collective-permute-start.14) | collective-permute-done | bytes 98336 | tf_op jit(solution)/shard_map/ppermute | solution.py:289
  62.4 0.7 %finish.1 = (f32[16,2048]{1,0:T(8,128)}, f32[16,512]{1,0:T(8,128)}, f32[64,128]{1,0:T(8,128)}) custom-call(bf16[16,3072]{1,0:T(8,128)(2,1)S(1)} %get-tuple-element.49.keep_ref, bf16[16,3072]{1,0:T(8,128)(2,1)S(1)} %collective-permute-done.14.got_ref), custom_call_target="tpu_custom_call" | custom-call | tf_op jit(solution)/shard_map/finish/pallas_call | solution.py:419
  (26 shorter events, 1.4 us)
Async XLA Ops:
  0.6 7.9 %collective-permute-start.5 = (bf16[64,512]{1,0:T(8,128)(2,1)}, bf16[64,512]{1,0:T(8,128)(2,1)S(1)}, u32[]{:S(2)}, u32[]{:S(2)}) collective-permute-start(bf16[64,512]{1,0:T(8,128)(2,1)} %bitcast.2), channel_id=1, source_target_pairs={{0,6},{1,7},{2,4},{3,5},{4,2},{5,3},{6,0},{7,1},{8,14},{9,15},{10,... | collective-permute-start | bytes 196616 | tf_op jit(solution)/shard_map/ppermute | solution.py:311
  5.8 5.8 %collective-permute-start.3 = (bf16[64,512]{1,0:T(8,128)(2,1)}, bf16[64,512]{1,0:T(8,128)(2,1)S(1)}, u32[]{:S(2)}, u32[]{:S(2)}) collective-permute-start(bf16[64,512]{1,0:T(8,128)(2,1)} %bitcast.3), channel_id=1, source_target_pairs={{0,4},{1,5},{2,6},{3,7},{4,0},{5,1},{6,2},{7,3},{8,12},{9,13},{10,... | collective-permute-start | bytes 196616 | tf_op jit(solution)/shard_map/ppermute | solution.py:311
  5.8 5.8 %collective-permute-start.1 = (bf16[64,512]{1,0:T(8,128)(2,1)}, bf16[64,512]{1,0:T(8,128)(2,1)S(1)}, u32[]{:S(2)}, u32[]{:S(2)}) collective-permute-start(bf16[64,512]{1,0:T(8,128)(2,1)} %bitcast.4), channel_id=1, source_target_pairs={{0,2},{1,3},{2,0},{3,1},{4,6},{5,7},{6,4},{7,5},{8,10},{9,11},{10,... | collective-permute-start | bytes 196616 | tf_op jit(solution)/shard_map/ppermute | solution.py:311
  6.4 8.4 %collective-permute-start = (bf16[64,512]{1,0:T(8,128)(2,1)}, bf16[64,512]{1,0:T(8,128)(2,1)S(1)}, u32[]{:S(2)}, u32[]{:S(2)}) collective-permute-start(bf16[64,512]{1,0:T(8,128)(2,1)} %bitcast.5), channel_id=1, source_target_pairs={{0,1},{1,0},{2,3},{3,2},{4,5},{5,4},{6,7},{7,6},{8,9},{9,8},{10,11... | collective-permute-start | bytes 196616 | tf_op jit(solution)/shard_map/ppermute | solution.py:311
  8.6 6.2 %collective-permute-start.6 = (bf16[64,512]{1,0:T(8,128)(2,1)S(1)}, bf16[64,512]{1,0:T(8,128)(2,1)S(1)}, u32[]{:S(2)}, u32[]{:S(2)}) collective-permute-start(bf16[64,512]{1,0:T(8,128)(2,1)S(1)} %collective-permute-done.5.refs_6_), channel_id=1, source_target_pairs={{0,1},{1,0},{2,3},{3,2},{4,5},{5,4},{6,7},{7,6},{8,9},{9,8},{10,11... | collective-permute-start | bytes 196616 | tf_op jit(solution)/shard_map/ppermute | solution.py:311
  11.6 3.2 %collective-permute-start.4 = (bf16[64,512]{1,0:T(8,128)(2,1)S(1)}, bf16[64,512]{1,0:T(8,128)(2,1)S(1)}, u32[]{:S(2)}, u32[]{:S(2)}) collective-permute-start(bf16[64,512]{1,0:T(8,128)(2,1)S(1)} %collective-permute-done.3.refs_4_), channel_id=1, source_target_pairs={{0,1},{1,0},{2,3},{3,2},{4,5},{5,4},{6,7},{7,6},{8,9},{9,8},{10,11... | collective-permute-start | bytes 196616 | tf_op jit(solution)/shard_map/ppermute | solution.py:311
  11.6 3.2 %collective-permute-start.2 = (bf16[64,512]{1,0:T(8,128)(2,1)S(1)}, bf16[64,512]{1,0:T(8,128)(2,1)S(1)}, u32[]{:S(2)}, u32[]{:S(2)}) collective-permute-start(bf16[64,512]{1,0:T(8,128)(2,1)S(1)} %collective-permute-done.1.refs_2_), channel_id=1, source_target_pairs={{0,1},{1,0},{2,3},{3,2},{4,5},{5,4},{6,7},{7,6},{8,9},{9,8},{10,11... | collective-permute-start | bytes 196616 | tf_op jit(solution)/shard_map/ppermute | solution.py:311
  26.2 2.4 %collective-permute-start.7 = (bf16[256,1536]{1,0:T(8,128)(2,1)S(1)}, bf16[256,1536]{1,0:T(8,128)(2,1)S(1)}, u32[]{:S(2)}, u32[]{:S(2)}) collective-permute-start(bf16[256,1536]{1,0:T(8,128)(2,1)S(1)} %get-tuple-element.36), channel_id=1, source_target_pairs={{0,1},{1,0},{2,3},{3,2},{4,5},{5,4},{6,7},{7,6},{8,9},{9,8},{10,11... | collective-permute-start | bytes 2359304 | tf_op jit(solution)/shard_map/ppermute | solution.py:311
  26.3 3.4 %collective-permute-start.8 = (bf16[256,1536]{1,0:T(8,128)(2,1)S(1)}, bf16[256,1536]{1,0:T(8,128)(2,1)S(1)}, u32[]{:S(2)}, u32[]{:S(2)}) collective-permute-start(bf16[256,1536]{1,0:T(8,128)(2,1)S(1)} %get-tuple-element.38), channel_id=1, source_target_pairs={{0,1},{1,0},{2,3},{3,2},{4,5},{5,4},{6,7},{7,6},{8,9},{9,8},{10,11... | collective-permute-start | bytes 2359304 | tf_op jit(solution)/shard_map/ppermute | solution.py:311
  29.7 3.4 %copy-start = (bf16[512,512]{1,0:T(8,128)(2,1)S(1)}, bf16[512,512]{1,0:T(8,128)(2,1)}, u32[]{:S(2)}) copy-start(bf16[512,512]{1,0:T(8,128)(2,1)} %wout_ref.1) | copy-start | bytes 1572868
  29.9 11.2 %collective-permute-start.10 = (bf16[128,1536]{1,0:T(8,128)(2,1)S(1)}, bf16[128,1536]{1,0:T(8,128)(2,1)S(1)}, u32[]{:S(2)}, u32[]{:S(2)}) collective-permute-start(bf16[128,1536]{1,0:T(8,128)(2,1)S(1)} %slice.39), channel_id=1, source_target_pairs={{0,16},{8,24},{16,0},{24,8},{1,17},{9,25},{17,1},{25,9},{2,18},{10... | collective-permute-start | bytes 1179656 | tf_op jit(solution)/shard_map/ppermute | solution.py:291
  31.5 10.9 %collective-permute-start.9 = (bf16[128,1536]{1,0:T(8,128)(2,1)S(1)}, bf16[128,1536]{1,0:T(8,128)(2,1)S(1)}, u32[]{:S(2)}, u32[]{:S(2)}) collective-permute-start(bf16[128,1536]{1,0:T(8,128)(2,1)S(1)} %slice.37), channel_id=1, source_target_pairs={{0,8},{8,0},{16,24},{24,16},{1,9},{9,1},{17,25},{25,17},{2,10},{10... | collective-permute-start | bytes 1179656 | tf_op jit(solution)/shard_map/ppermute | solution.py:291
  42.6 5.9 %collective-permute-start.12 = (bf16[64,1536]{1,0:T(8,128)(2,1)S(1)}, bf16[64,1536]{1,0:T(8,128)(2,1)S(1)}, u32[]{:S(2)}, u32[]{:S(2)}) collective-permute-start(bf16[64,1536]{1,0:T(8,128)(2,1)S(1)} %slice.43), channel_id=1, source_target_pairs={{0,8},{8,0},{16,24},{24,16},{1,9},{9,1},{17,25},{25,17},{2,10},{10... | collective-permute-start | bytes 589832 | tf_op jit(solution)/shard_map/ppermute | solution.py:291
  44.2 5.7 %collective-permute-start.11 = (bf16[64,1536]{1,0:T(8,128)(2,1)S(1)}, bf16[64,1536]{1,0:T(8,128)(2,1)S(1)}, u32[]{:S(2)}, u32[]{:S(2)}) collective-permute-start(bf16[64,1536]{1,0:T(8,128)(2,1)S(1)} %slice.41), channel_id=1, source_target_pairs={{0,16},{8,24},{16,0},{24,8},{1,17},{9,25},{17,1},{25,9},{2,18},{10... | collective-permute-start | bytes 589832 | tf_op jit(solution)/shard_map/ppermute | solution.py:291
  50.0 5.7 %collective-permute-start.13 = (bf16[32,3072]{1,0:T(8,128)(2,1)S(1)}, bf16[32,3072]{1,0:T(8,128)(2,1)S(1)}, u32[]{:S(2)}, u32[]{:S(2)}) collective-permute-start(bf16[32,3072]{1,0:T(8,128)(2,1)S(1)} %pad_maximum_fusion), channel_id=1, source_target_pairs={{0,2},{1,3},{2,0},{3,1},{4,6},{5,7},{6,4},{7,5},{8,10},{9,11},{10,... | collective-permute-start | bytes 589832 | tf_op jit(solution)/shard_map/ppermute | solution.py:289
  55.8 6.6 %collective-permute-start.14 = (bf16[16,3072]{1,0:T(8,128)(2,1)S(1)}, bf16[16,3072]{1,0:T(8,128)(2,1)S(1)}, u32[]{:S(2)}, u32[]{:S(2)}) collective-permute-start(bf16[16,3072]{1,0:T(8,128)(2,1)S(1)} %get-tuple-element.48), channel_id=1, source_target_pairs={{0,4},{1,5},{2,6},{3,7},{4,0},{5,1},{6,2},{7,3},{8,12},{9,13},{10,... | collective-permute-start | bytes 294920 | tf_op jit(solution)/shard_map/ppermute | solution.py:289

commit v4 on v3

--- a/solution.py
+++ b/solution.py
@@ -11,6 +11,7 @@
 MAXLEN = 64
 LANES = 128
 EPS = 1e-05
+SCRATCH = 13
 BF = jnp.bfloat16
 F32 = jnp.float32
 
@@ -21,10 +22,6 @@
 
 def nn(a, b):
     return jnp.dot(a, b, preferred_element_type=F32)
-
-
-def tn(a, b):
-    return lax.dot_general(a, b, (((0,), (0,)), ((), ())), preferred_element_type=F32)
 
 
 def sigmoid(v):
@@ -105,7 +102,7 @@
     _, tabs = shape
     pieces, refs = refs[:tabs], refs[tabs:]
     gated_ref, tab_ref = refs[:2]
-    grads, scratch = refs[2:-9], refs[-9:]
+    grads, scratch = refs[2:-SCRATCH], refs[-SCRATCH:]
     me_tab = lax.axis_index("table")
     for rel in range(tabs):
         feats = pieces[rel].shape[0]
@@ -116,7 +113,8 @@
 
 def layer_body(
     order, shape, start_ref, tab_ref, onehot_ref, outg_ref, gg_ref, w_ref, gated_ref, grads,
-    act_ref, dact_ref, fac_ref, att_ref, attended_ref, dkv_ref, pg_ref, tmp_ref, lhs_ref,
+    act_ref, dact_ref, sc_ref, fac_ref, qs_ref, das_ref, att_ref, ds_ref, turned_ref,
+    attended_ref, pg_ref, tmp_ref, lhs_ref,
 ):
     live, items = onehot_ref.shape
     width = tab_ref.shape[0]
@@ -152,26 +150,31 @@
     def merge(v):
         return jnp.where(low, v[:MAXLEN], v[MAXLEN:])
 
+    spots = [
+        (t * pairs + c, t * MAXLEN, max(t - 1, 0) * MAXLEN, c * LANES) for t in range(tiles) for c in range(pairs)
+    ]
+    for n, r0, w0, lo in spots:
+        q = stack(act_ref[r0 : r0 + MAXLEN, 2 * width + lo : 2 * width + lo + LANES])
+        qs_ref[n] = q
+        sc_ref[n] = nt(q, act_ref[w0 : w0 + LANES, 3 * width + lo : 3 * width + lo + LANES])
     for t in range(tiles):
         r0 = t * MAXLEN
-        w0 = max(t - 1, 0) * MAXLEN
         row = r0 + lax.broadcasted_iota(jnp.int32, (MAXLEN, LANES), 0)
-        col = w0 + lax.broadcasted_iota(jnp.int32, (MAXLEN, LANES), 1)
+        col = max(t - 1, 0) * MAXLEN + lax.broadcasted_iota(jnp.int32, (MAXLEN, LANES), 1)
         seen = (col >= start_ref[r0 : r0 + MAXLEN, :]) & (col <= row)
         mask = jnp.where(seen, 1.0 / MAXLEN, 0.0)
         mask = jnp.concatenate([mask, mask], axis=0)
+        slope = mask * DH**-0.5
         for c in range(pairs):
-            lo, hi = c * LANES, (c + 1) * LANES
-            q = stack(act_ref[r0 : r0 + MAXLEN, 2 * width + lo : 2 * width + hi])
-            k = act_ref[w0 : w0 + LANES, 3 * width + lo : 3 * width + hi]
-            v = act_ref[w0 : w0 + LANES, width + lo : width + hi]
-            sc = nt(q, k) * DH**-0.5
+            n = t * pairs + c
+            sc = sc_ref[n] * DH**-0.5
             sg = sigmoid(sc)
             si = sc * sg
-            w = (si * mask).astype(BF)
-            fac_ref[t * pairs + c] = (sg + si * (1.0 - sg)) * (mask * DH**-0.5)
-            att_ref[t * pairs + c] = w
-            attended_ref[r0 : r0 + MAXLEN, lo:hi] = merge(nn(w, v))
+            att_ref[n * LANES : (n + 1) * LANES, :] = (si * mask).astype(BF)
+            fac_ref[n] = (sg + si * (1.0 - sg)) * slope
+    for n, r0, w0, lo in spots:
+        v = act_ref[w0 : w0 + LANES, width + lo : width + lo + LANES]
+        attended_ref[r0 : r0 + MAXLEN, lo : lo + LANES] = merge(nn(att_ref[n * LANES : (n + 1) * LANES, :], v))
 
     attended = attended_ref[...]
     cen = attended - jnp.mean(attended, axis=1, keepdims=True)
@@ -186,27 +189,34 @@
     datt = r * (dy - jnp.mean(dy, axis=1, keepdims=True) - yhat * jnp.mean(dy * yhat, axis=1, keepdims=True))
     attended_ref[...] = datt
 
-    dkv_ref[...] = jnp.zeros_like(dkv_ref)
-    for t in range(tiles):
-        r0 = t * MAXLEN
-        w0 = max(t - 1, 0) * MAXLEN
-        for c in range(pairs):
-            lo, hi = c * LANES, (c + 1) * LANES
-            q = stack(act_ref[r0 : r0 + MAXLEN, 2 * width + lo : 2 * width + hi])
-            k = act_ref[w0 : w0 + LANES, 3 * width + lo : 3 * width + hi]
-            v = act_ref[w0 : w0 + LANES, width + lo : width + hi]
-            da = stack(attended_ref[r0 : r0 + MAXLEN, lo:hi].astype(BF))
-            dw = nt(da, v).astype(BF).astype(F32)
-            ds = (dw * fac_ref[t * pairs + c]).astype(BF)
-            dq = merge(nn(ds, k)).astype(BF).astype(F32)
-            qc = slice(2 * width + lo, 2 * width + hi)
-            pg_ref[r0 : r0 + MAXLEN, qc] = (dq * dact_ref[r0 : r0 + MAXLEN, qc]).astype(BF)
-            dkv_ref[w0 : w0 + LANES, lo:hi] += tn(att_ref[t * pairs + c], da)
-            dkv_ref[w0 : w0 + LANES, width + lo : width + hi] += tn(ds, q)
-    for g, c in ((1, 0), (3, 1)):
-        cols = slice(g * width, (g + 1) * width)
-        d = dkv_ref[:, c * width : (c + 1) * width].astype(BF).astype(F32)
-        pg_ref[:, cols] = (d * dact_ref[:, cols]).astype(BF)
+    for n, r0, w0, lo in spots:
+        da = stack(attended_ref[r0 : r0 + MAXLEN, lo : lo + LANES].astype(BF))
+        das_ref[n] = da
+        sc_ref[n] = nt(da, act_ref[w0 : w0 + LANES, width + lo : width + lo + LANES])
+    for n in range(tiles * pairs):
+        dw = sc_ref[n].astype(BF).astype(F32)
+        ds_ref[n * LANES : (n + 1) * LANES, :] = (dw * fac_ref[n]).astype(BF)
+    for n, r0, w0, lo in spots:
+        k = act_ref[w0 : w0 + LANES, 3 * width + lo : 3 * width + lo + LANES]
+        dq = merge(nn(ds_ref[n * LANES : (n + 1) * LANES, :], k)).astype(BF).astype(F32)
+        qc = slice(2 * width + lo, 2 * width + lo + LANES)
+        pg_ref[r0 : r0 + MAXLEN, qc] = (dq * dact_ref[r0 : r0 + MAXLEN, qc]).astype(BF)
+    for src_ref, rhs_ref, g in ((att_ref, das_ref, 1), (ds_ref, qs_ref, 3)):
+        turned_ref[...] = jnp.transpose(src_ref[...])
+        for t in range(tiles):
+            off = MAXLEN if t else 0
+            for c in range(pairs):
+                n = t * pairs + c
+                lhs = turned_ref[off : off + MAXLEN, n * LANES : (n + 1) * LANES]
+                rhs = rhs_ref[n]
+                if t + 1 < tiles:
+                    m = n + pairs
+                    lhs = jnp.concatenate([lhs, turned_ref[:MAXLEN, m * LANES : (m + 1) * LANES]], axis=1)
+                    rhs = jnp.concatenate([rhs, rhs_ref[m]], axis=0)
+                cols = slice(g * width + c * LANES, g * width + (c + 1) * LANES)
+                rows = slice(t * MAXLEN, (t + 1) * MAXLEN)
+                d = nn(lhs, rhs).astype(BF).astype(F32)
+                pg_ref[rows, cols] = (d * dact_ref[rows, cols]).astype(BF)
 
     dn = nt(pg_ref[...], w_ref[...]).astype(BF).astype(F32)
     dx = rstd * (dn - jnp.mean(dn, axis=1, keepdims=True) - xhat * jnp.mean(dn * xhat, axis=1, keepdims=True))
@@ -234,19 +244,17 @@
         grad_u_ref[...] = nn(normed_t, pg_ref[...])
         grad_t_ref[...] = nn(jnp.transpose(in_grad), onehot_ref[...]).astype(BF)
         return
-    keep1_ref, send1_ref, keep2_ref, send2_ref = grads
-    lhs = relative(0, outg_t)
-    res = nn(lhs, gated).astype(BF)
-    keep1_ref[:, :width] = res[:half]
-    send1_ref[:, :width] = res[half:]
-    lhs = relative(0, normed_t)
-    res = nn(lhs, pg_ref[:, : 2 * width]).astype(BF)
-    keep1_ref[:, width:] = res[:half]
-    send1_ref[:, width:] = res[half:]
-    lhs = relative(1, normed_t)
-    res = nn(lhs, pg_ref[:, 2 * width :]).astype(BF)
-    keep2_ref[:, : 2 * width] = res[:half]
-    send2_ref[:, : 2 * width] = res[half:]
+
+    def emit(colour, at, lhs, rhs):
+        res = nn(lhs, rhs).astype(BF)
+        cols = slice(at, at + rhs.shape[1])
+        grads[2 * colour][:, cols] = res[:half]
+        grads[2 * colour + 1][:, cols] = res[half:]
+
+    emit(0, 0, relative(0, outg_t), gated)
+    emit(0, width, relative(0, normed_t), pg_ref[:, :width])
+    emit(1, 0, relative(1, normed_t), pg_ref[:, width : 3 * width])
+    emit(2, 0, relative(2, normed_t), pg_ref[:, 3 * width :])
     tmp_ref[...] = jnp.transpose(in_grad)
     feats = width // tabs
     span = items // dps
@@ -257,11 +265,11 @@
         at = pl.multiple_of((me_dp ^ rd) * span, span)
         res = nn(lhs_ref[...], onehot_ref[:, pl.ds(at, span)]).astype(BF)
         for rt in range(tabs):
-            place = position(1, rd * tabs + rt) * blk
-            dst = keep2_ref if place < half else send2_ref
+            place = position(2, rd * tabs + rt) * blk
+            dst = grads[4] if place < half else grads[5]
             place = place % half
             for j in range(feats // blk):
-                dst[place : place + blk, 2 * width + j * span : 2 * width + (j + 1) * span] = res[
+                dst[place : place + blk, width + j * span : width + (j + 1) * span] = res[
                     rt * feats + j * blk : rt * feats + (j + 1) * blk, :
                 ]
 
@@ -340,15 +348,15 @@
     for rel in range(2, tabs, 2):
         pieces += [far[rel], other(far[rel], 1)]
 
-    dp_order = list(range(tab_bits, bits))
-    z_order = list(range(1, tab_bits))
-    order = ([0] + dp_order + z_order, [0] + dp_order[::-1] + z_order)
-    w1 = 3 * width
+    ring = list(range(tab_bits, bits)) + list(range(1, tab_bits - 1))
+    colours = 3
+    order = [[0] + ring[c:] + ring[:c] + [tab_bits - 1] for c in range(colours)]
+    w1 = 2 * width
     blk = width // devices
     span = items // dps
     halving = blk % 16 == 0 and feats % blk == 0 and span == LANES and width % (feats // blk * span) == 0
     if halving:
-        grad_shapes = (sds((width // 2, w1), BF),) * 4
+        grad_shapes = (sds((width // 2, w1), BF),) * (2 * colours)
     else:
         order = None
         grad_shapes = (sds((width, width), F32), sds((width, 4 * width), F32), sds((width, items), BF))
@@ -362,9 +370,13 @@
             pltpu.VMEM((live, 4 * width), BF),
             pltpu.VMEM((live, 4 * width), F32),
             pltpu.VMEM((tiles, LANES, LANES), F32),
+            pltpu.VMEM((tiles, LANES, LANES), F32),
             pltpu.VMEM((tiles, LANES, LANES), BF),
+            pltpu.VMEM((tiles, LANES, LANES), BF),
+            pltpu.VMEM((tiles * LANES, LANES), BF),
+            pltpu.VMEM((tiles * LANES, LANES), BF),
+            pltpu.VMEM((LANES, tiles * LANES), BF),
             pltpu.VMEM((live, width), F32),
-            pltpu.VMEM((live, 2 * width), F32),
             pltpu.VMEM((live, 4 * width), BF),
             pltpu.VMEM((width, live), BF),
             pltpu.VMEM((width, live), BF),
@@ -400,22 +412,17 @@
         h = v.shape[0] // 2
         return v[:h], v[h:]
 
-    keep1, send1, keep2, send2 = grads
-    totals = [add(keep, other(send, 1)) for keep, send in ((keep1, send1), (keep2, send2))]
+    totals = [add(keep, other(send, 1)) for keep, send in zip(grads[::2], grads[1::2])]
     gated, *totals = lax.optimization_barrier((gated, *totals))
     output = finish_output(gated)
-    for n in range(len(dp_order)):
-        for c in range(2):
+    for n in range(len(ring)):
+        for c in range(colours):
             keep, send = halves(totals[c])
             totals[c] = add(keep, swap(send, order[c][1 + n], tab_bits, dps, tabs))
         if n == 0:
             output, *totals = lax.optimization_barrier((output, *totals))
-    total = jnp.concatenate(totals, axis=1)
-    for bit in z_order[:-1]:
-        keep, send = halves(total)
-        total = add(keep, swap(send, bit, tab_bits, dps, tabs))
-    keep, send = halves(total)
-    got = swap(send, z_order[-1], tab_bits, dps, tabs)
+    keep, send = halves(jnp.concatenate(totals, axis=1))
+    got = swap(send, tab_bits - 1, tab_bits, dps, tabs)
     grad_uvqk, grad_out_t, grad_t = pl.pallas_call(
         finish_kernel,
         out_shape=(sds((blk, 4 * width), F32), sds((blk, width), F32), sds((feats, span), F32)),

time: 63.4 us -> 56.6 us (0.89)
  waiting for transfers between devices: 30.2 us -> 23.8 us
  Pallas kernels: 15.8 us -> 11.6 us
  starting transfers between devices: 14.8 us -> 18.3 us
    ppermute x4 -> x6, waiting for transfers between devices: 12.6 us -> 6.36 us  [swap(): return lax.ppermute(v, 'dp', [(i, i ^ 1 << b) for i in range(dps)])]
    pallas_call x1, Pallas kernels: 11.4 us -> 7.17 us  [layer(): pl.pallas_call(functools.partial(layer_kernel, order, (dps, tabs)), out_s...]
    ppermute x2 -> x4, starting transfers between devices: 2.64 us -> 4.99 us  [swap(): return lax.ppermute(v, 'table', [(i, i ^ 1 << bit) for i in range(tabs)])]
    ppermute x4 -> x6, starting transfers between devices: 5.26 us -> 6.39 us  [swap(): return lax.ppermute(v, 'dp', [(i, i ^ 1 << b) for i in range(dps)])]
    ppermute x9 -> x10, waiting for transfers between devices: 7.88 us -> 7.6 us  [other(): return lax.ppermute(v, 'table', [(i, i ^ rel) for i in range(tabs)])]
    ppermute x2 -> x4, waiting for transfers between devices: 9.73 us -> 9.88 us  [swap(): return lax.ppermute(v, 'table', [(i, i ^ 1 << bit) for i in range(tabs)])]
    ppermute x9 -> x10, starting transfers between devices: 6.87 us -> 6.96 us  [other(): return lax.ppermute(v, 'table', [(i, i ^ rel) for i in range(tabs)])]
  transfers between devices with their start and end apart: 15 -> 20, of which waited for: 10 -> 15; matrix products, arithmetic and copies ran while one was open for 2% -> 3% of each run, Pallas kernels for 6% -> 7%
where the time goes in v4:
time: 56.6 us; the launch traced here: 56.4 us
  waiting for transfers between devices  23.8 us (42%)
  starting transfers between devices  18.3 us (32%)
  Pallas kernels  11.6 us (20%)
  other arithmetic  0.94 us (2%)
  local copies, waits for them, and re-layouts  0.84 us (1%)
  between operations  0.84 us (1%)
    ppermute x4, waiting for transfers between devices, swap(): return lax.ppermute(v, 'table', [(i, i ^ 1 << bit) for i in range(tabs)])  9.88 us
    ppermute x10, waiting for transfers between devices, other(): return lax.ppermute(v, 'table', [(i, i ^ rel) for i in range(tabs)])  7.6 us
    pallas_call x1, Pallas kernels, layer(): pl.pallas_call(functools.partial(layer_kernel, order, (dps, tabs)), out_s...  7.17 us
    ppermute x10, starting transfers between devices, other(): return lax.ppermute(v, 'table', [(i, i ^ rel) for i in range(tabs)])  6.96 us
    ppermute x6, starting transfers between devices, swap(): return lax.ppermute(v, 'dp', [(i, i ^ 1 << b) for i in range(dps)])  6.39 us
    ppermute x6, waiting for transfers between devices, swap(): return lax.ppermute(v, 'dp', [(i, i ^ 1 << b) for i in range(dps)])  6.36 us
    ppermute x4, starting transfers between devices, swap(): return lax.ppermute(v, 'table', [(i, i ^ 1 << bit) for i in range(tabs)])  4.99 us
    pallas_call x1, Pallas kernels, layer(): pl.pallas_call(prep_kernel, out_shape=(sds((live, items), BF), sds((live,...  1.97 us
  transfers between devices with their start and end apart: 20, of which 15 were waited for; matrix products, arithmetic and copies ran while one was open for 3% of the time, Pallas kernels for 7%

profile of v4, /device:TPU:0, one launch (start us, length us, event | category | flops | bytes accessed | tf_op | source)
XLA Modules:
  0.0 56.4 jit_solution(1810383656289314742)
XLA Ops:
  0.6 5.1 %collective-permute-start.5 = (bf16[64,512]{1,0:T(8,128)(2,1)}, bf16[64,512]{1,0:T(8,128)(2,1)S(1)}, u32[]{:S(2)}, u32[]{:S(2)}) collective-permute-start(bf16[64,512]{1,0:T(8,128)(2,1)} %bitcast.2), channel_id=1, source_target_pairs={{0,6},{1,7},{2,4},{3,5},{4,2},{5,3},{6,0},{7,1},{8,14},{9,15},{10,... | collective-permute-start | bytes 196616 | tf_op jit(solution)/shard_map/ppermute | solution.py:319
  6.4 2.2 %collective-permute-done.5.refs_6_ = bf16[64,512]{1,0:T(8,128)(2,1)S(1)} collective-permute-done((bf16[64,512]{1,0:T(8,128)(2,1)}, bf16[64,512]{1,0:T(8,128)(2,1)S(1)}, u32[]{:S(2)}, u32[]{:S(2)}) %collective-permute-start.5) | collective-permute-done | bytes 65568 | tf_op jit(solution)/shard_map/ppermute | solution.py:319
  8.6 3.0 %collective-permute-done.3.refs_4_ = bf16[64,512]{1,0:T(8,128)(2,1)S(1)} collective-permute-done((bf16[64,512]{1,0:T(8,128)(2,1)}, bf16[64,512]{1,0:T(8,128)(2,1)S(1)}, u32[]{:S(2)}, u32[]{:S(2)}) %collective-permute-start.3) | collective-permute-done | bytes 65568 | tf_op jit(solution)/shard_map/ppermute | solution.py:319
  12.1 0.7 %reshape.11.ids_ref = s32[8,512]{1,0:T(8,128)S(1)} reshape(s32[4096]{0:T(1024)} %param.6) | data formatting | bytes 32768 | tf_op jit(solution)/shard_map/reshape | solution.py:314
  12.8 2.0 %prep.1 = (bf16[320,512]{1,0:T(8,128)(2,1)S(1)}, bf16[320,512]{1,0:T(8,128)(2,1)S(1)}, bf16[320,512]{1,0:T(8,128)(2,1)S(1)}, s32[320,128]{1,0:T(8,128)S(1)}, s32...) custom-call(s32[1,8]{1,0:T(1,128)} %len_hbm.1, s32[8,512]{1,0:T(8,128)S(1)} %reshape.11.ids_ref, ...), custom_call_target="tpu_custom_call" | custom-call | tf_op jit(solution)/shard_map/prep/pallas_call | solution.py:325
  14.8 7.2 %layer.1 = (bf16[320,512]{1,0:T(8,128)(2,1)S(1)}, bf16[512,512]{1,0:T(8,128)(2,1)S(1)}, bf16[256,1024]{1,0:T(8,128)(2,1)S(1)}, bf16[256,1024]{1,0:T(8,128)(2,1)S...) custom-call(s32[320,128]{1,0:T(8,128)S(1)} %get-tuple-element.31.sta, ...), custom_call_target="tpu_custom_call" | custom-call | tf_op jit(solution)/shard_map/layer/pallas_call | solution.py:364
  22.7 1.3 %collective-permute-done.7 = bf16[256,1024]{1,0:T(8,128)(2,1)S(1)} collective-permute-done((bf16[256,1024]{1,0:T(8,128)(2,1)S(1)}, bf16[256,1024]{1,0:T(8,128)(2,1)S(1)}, u32[]{:S(2)}, u32[]{:S(2)}) %collective-permute-start.7) | collective-permute-done | bytes 524320 | tf_op jit(solution)/shard_map/ppermute | solution.py:319
  25.7 0.8 %collective-permute-start.12 = (bf16[128,1024]{1,0:T(8,128)(2,1)S(1)}, bf16[128,1024]{1,0:T(8,128)(2,1)S(1)}, u32[]{:S(2)}, u32[]{:S(2)}) collective-permute-start(bf16[128,1024]{1,0:T(8,128)(2,1)S(1)} %slice.65), channel_id=1, source_target_pairs={{0,2},{1,3},{2,0},{3,1},{4,6},{5,7},{6,4},{7,5},{8,10},{9,11},{10,... | collective-permute-start | bytes 786440 | tf_op jit(solution)/shard_map/ppermute | solution.py:297
  26.5 1.6 %collective-permute-start.11 = (bf16[128,1024]{1,0:T(8,128)(2,1)S(1)}, bf16[128,1024]{1,0:T(8,128)(2,1)S(1)}, u32[]{:S(2)}, u32[]{:S(2)}) collective-permute-start(bf16[128,1024]{1,0:T(8,128)(2,1)S(1)} %slice.63), channel_id=1, source_target_pairs={{0,16},{8,24},{16,0},{24,8},{1,17},{9,25},{17,1},{25,9},{2,18},{10... | collective-permute-start | bytes 786440 | tf_op jit(solution)/shard_map/ppermute | solution.py:299
  28.1 1.6 %collective-permute-start.10 = (bf16[128,1024]{1,0:T(8,128)(2,1)S(1)}, bf16[128,1024]{1,0:T(8,128)(2,1)S(1)}, u32[]{:S(2)}, u32[]{:S(2)}) collective-permute-start(bf16[128,1024]{1,0:T(8,128)(2,1)S(1)} %slice.61), channel_id=1, source_target_pairs={{0,8},{8,0},{16,24},{24,16},{1,9},{9,1},{17,25},{25,17},{2,10},{10... | collective-permute-start | bytes 786440 | tf_op jit(solution)/shard_map/ppermute | solution.py:299
  29.7 1.8 %out.1 = bf16[512,512]{1,0:T(8,128)(2,1)} custom-call(s32[8,320]{1,0:T(8,128)S(1)} %get-tuple-element.30.origin_ref, s32[8,512]{1,0:T(8,128)S(1)} %reshape.11.ids_ref, bf16[512,512]{1,0:T(8,128)(2,1)S(1)} %get-tuple-element.37.tab_ref, bf16[320,512]{1,0:T(8,128)(2,1)S(1)} %get-tuple-element.45.gated_ref, bf16[512,512]{1,0:T(8,128)(2,1)S(1)} %copy-done), custom_call_target="tpu_custom_call" | custom-call | tf_op jit(solution)/shard_map/out/pallas_call | solution.py:389
  31.5 2.7 %collective-permute-done.12 = bf16[128,1024]{1,0:T(8,128)(2,1)S(1)} collective-permute-done((bf16[128,1024]{1,0:T(8,128)(2,1)S(1)}, bf16[128,1024]{1,0:T(8,128)(2,1)S(1)}, u32[]{:S(2)}, u32[]{:S(2)}) %collective-permute-start.12) | collective-permute-done | bytes 262176 | tf_op jit(solution)/shard_map/ppermute | solution.py:297
  34.2 0.7 %collective-permute-done.11 = bf16[128,1024]{1,0:T(8,128)(2,1)S(1)} collective-permute-done((bf16[128,1024]{1,0:T(8,128)(2,1)S(1)}, bf16[128,1024]{1,0:T(8,128)(2,1)S(1)}, u32[]{:S(2)}, u32[]{:S(2)}) %collective-permute-start.11) | collective-permute-done | bytes 262176 | tf_op jit(solution)/shard_map/ppermute | solution.py:299
  35.0 1.3 %collective-permute-done.10 = bf16[128,1024]{1,0:T(8,128)(2,1)S(1)} collective-permute-done((bf16[128,1024]{1,0:T(8,128)(2,1)S(1)}, bf16[128,1024]{1,0:T(8,128)(2,1)S(1)}, u32[]{:S(2)}, u32[]{:S(2)}) %collective-permute-start.10) | collective-permute-done | bytes 262176 | tf_op jit(solution)/shard_map/ppermute | solution.py:299
  36.3 1.6 %collective-permute-start.17 = (bf16[64,1024]{1,0:T(8,128)(2,1)S(1)}, bf16[64,1024]{1,0:T(8,128)(2,1)S(1)}, u32[]{:S(2)}, u32[]{:S(2)}) collective-permute-start(bf16[64,1024]{1,0:T(8,128)(2,1)S(1)} %slice.75), channel_id=1, source_target_pairs={{0,8},{8,0},{16,24},{24,16},{1,9},{9,1},{17,25},{25,17},{2,10},{10... | collective-permute-start | bytes 393224 | tf_op jit(solution)/shard_map/ppermute | solution.py:299
  37.9 1.1 %collective-permute-start.15 = (bf16[64,1024]{1,0:T(8,128)(2,1)S(1)}, bf16[64,1024]{1,0:T(8,128)(2,1)S(1)}, u32[]{:S(2)}, u32[]{:S(2)}) collective-permute-start(bf16[64,1024]{1,0:T(8,128)(2,1)S(1)} %slice.71), channel_id=1, source_target_pairs={{0,2},{1,3},{2,0},{3,1},{4,6},{5,7},{6,4},{7,5},{8,10},{9,11},{10,... | collective-permute-start | bytes 393224 | tf_op jit(solution)/shard_map/ppermute | solution.py:297
  39.5 1.8 %collective-permute-done.17 = bf16[64,1024]{1,0:T(8,128)(2,1)S(1)} collective-permute-done((bf16[64,1024]{1,0:T(8,128)(2,1)S(1)}, bf16[64,1024]{1,0:T(8,128)(2,1)S(1)}, u32[]{:S(2)}, u32[]{:S(2)}) %collective-permute-start.17) | collective-permute-done | bytes 131104 | tf_op jit(solution)/shard_map/ppermute | solution.py:299
  42.0 1.0 %collective-permute-done.15 = bf16[64,1024]{1,0:T(8,128)(2,1)S(1)} collective-permute-done((bf16[64,1024]{1,0:T(8,128)(2,1)S(1)}, bf16[64,1024]{1,0:T(8,128)(2,1)S(1)}, u32[]{:S(2)}, u32[]{:S(2)}) %collective-permute-start.15) | collective-permute-done | bytes 131104 | tf_op jit(solution)/shard_map/ppermute | solution.py:297
  44.1 1.0 %collective-permute-start.14 = (bf16[32,1024]{1,0:T(8,128)(2,1)S(1)}, bf16[32,1024]{1,0:T(8,128)(2,1)S(1)}, u32[]{:S(2)}, u32[]{:S(2)}) collective-permute-start(bf16[32,1024]{1,0:T(8,128)(2,1)S(1)} %slice.81), channel_id=1, source_target_pairs={{0,2},{1,3},{2,0},{3,1},{4,6},{5,7},{6,4},{7,5},{8,10},{9,11},{10,... | collective-permute-start | bytes 196616 | tf_op jit(solution)/shard_map/ppermute | solution.py:297
  45.7 1.6 %collective-permute-done.16 = bf16[32,1024]{1,0:T(8,128)(2,1)S(1)} collective-permute-done((bf16[32,1024]{1,0:T(8,128)(2,1)S(1)}, bf16[32,1024]{1,0:T(8,128)(2,1)S(1)}, u32[]{:S(2)}, u32[]{:S(2)}) %collective-permute-start.16) | collective-permute-done | bytes 65568 | tf_op jit(solution)/shard_map/ppermute | solution.py:299
  47.3 1.8 %collective-permute-done.14 = bf16[32,1024]{1,0:T(8,128)(2,1)S(1)} collective-permute-done((bf16[32,1024]{1,0:T(8,128)(2,1)S(1)}, bf16[32,1024]{1,0:T(8,128)(2,1)S(1)}, u32[]{:S(2)}, u32[]{:S(2)}) %collective-permute-start.14) | collective-permute-done | bytes 65568 | tf_op jit(solution)/shard_map/ppermute | solution.py:297
  49.2 2.1 %collective-permute-start.19 = (bf16[16,3072]{1,0:T(8,128)(2,1)S(1)}, bf16[16,3072]{1,0:T(8,128)(2,1)S(1)}, u32[]{:S(2)}, u32[]{:S(2)}) collective-permute-start(bf16[16,3072]{1,0:T(8,128)(2,1)S(1)} %get-tuple-element.56), channel_id=1, source_target_pairs={{0,4},{1,5},{2,6},{3,7},{4,0},{5,1},{6,2},{7,3},{8,12},{9,13},{10,... | collective-permute-start | bytes 294920 | tf_op jit(solution)/shard_map/ppermute | solution.py:297
  51.2 4.5 %collective-permute-done.19.got_ref = bf16[16,3072]{1,0:T(8,128)(2,1)S(1)} collective-permute-done((bf16[16,3072]{1,0:T(8,128)(2,1)S(1)}, bf16[16,3072]{1,0:T(8,128)(2,1)S(1)}, u32[]{:S(2)}, u32[]{:S(2)}) %collective-permute-start.19) | collective-permute-done | bytes 98336 | tf_op jit(solution)/shard_map/ppermute | solution.py:297
  55.7 0.7 %finish.1 = (f32[16,2048]{1,0:T(8,128)}, f32[16,512]{1,0:T(8,128)}, f32[64,128]{1,0:T(8,128)}) custom-call(bf16[16,3072]{1,0:T(8,128)(2,1)S(1)} %get-tuple-element.57.keep_ref, bf16[16,3072]{1,0:T(8,128)(2,1)S(1)} %collective-permute-done.19.got_ref), custom_call_target="tpu_custom_call" | custom-call | tf_op jit(solution)/shard_map/finish/pallas_call | solution.py:426
  (46 shorter events, 6.7 us)
Async XLA Ops:
  0.6 7.9 %collective-permute-start.5 = (bf16[64,512]{1,0:T(8,128)(2,1)}, bf16[64,512]{1,0:T(8,128)(2,1)S(1)}, u32[]{:S(2)}, u32[]{:S(2)}) collective-permute-start(bf16[64,512]{1,0:T(8,128)(2,1)} %bitcast.2), channel_id=1, source_target_pairs={{0,6},{1,7},{2,4},{3,5},{4,2},{5,3},{6,0},{7,1},{8,14},{9,15},{10,... | collective-permute-start | bytes 196616 | tf_op jit(solution)/shard_map/ppermute | solution.py:319
  5.8 5.8 %collective-permute-start.3 = (bf16[64,512]{1,0:T(8,128)(2,1)}, bf16[64,512]{1,0:T(8,128)(2,1)S(1)}, u32[]{:S(2)}, u32[]{:S(2)}) collective-permute-start(bf16[64,512]{1,0:T(8,128)(2,1)} %bitcast.3), channel_id=1, source_target_pairs={{0,4},{1,5},{2,6},{3,7},{4,0},{5,1},{6,2},{7,3},{8,12},{9,13},{10,... | collective-permute-start | bytes 196616 | tf_op jit(solution)/shard_map/ppermute | solution.py:319
  5.8 5.8 %collective-permute-start.1 = (bf16[64,512]{1,0:T(8,128)(2,1)}, bf16[64,512]{1,0:T(8,128)(2,1)S(1)}, u32[]{:S(2)}, u32[]{:S(2)}) collective-permute-start(bf16[64,512]{1,0:T(8,128)(2,1)} %bitcast.4), channel_id=1, source_target_pairs={{0,2},{1,3},{2,0},{3,1},{4,6},{5,7},{6,4},{7,5},{8,10},{9,11},{10,... | collective-permute-start | bytes 196616 | tf_op jit(solution)/shard_map/ppermute | solution.py:319
  6.4 8.4 %collective-permute-start = (bf16[64,512]{1,0:T(8,128)(2,1)}, bf16[64,512]{1,0:T(8,128)(2,1)S(1)}, u32[]{:S(2)}, u32[]{:S(2)}) collective-permute-start(bf16[64,512]{1,0:T(8,128)(2,1)} %bitcast.5), channel_id=1, source_target_pairs={{0,1},{1,0},{2,3},{3,2},{4,5},{5,4},{6,7},{7,6},{8,9},{9,8},{10,11... | collective-permute-start | bytes 196616 | tf_op jit(solution)/shard_map/ppermute | solution.py:319
  8.6 6.2 %collective-permute-start.6 = (bf16[64,512]{1,0:T(8,128)(2,1)S(1)}, bf16[64,512]{1,0:T(8,128)(2,1)S(1)}, u32[]{:S(2)}, u32[]{:S(2)}) collective-permute-start(bf16[64,512]{1,0:T(8,128)(2,1)S(1)} %collective-permute-done.5.refs_6_), channel_id=1, source_target_pairs={{0,1},{1,0},{2,3},{3,2},{4,5},{5,4},{6,7},{7,6},{8,9},{9,8},{10,11... | collective-permute-start | bytes 196616 | tf_op jit(solution)/shard_map/ppermute | solution.py:319
  11.6 3.2 %collective-permute-start.4 = (bf16[64,512]{1,0:T(8,128)(2,1)S(1)}, bf16[64,512]{1,0:T(8,128)(2,1)S(1)}, u32[]{:S(2)}, u32[]{:S(2)}) collective-permute-start(bf16[64,512]{1,0:T(8,128)(2,1)S(1)} %collective-permute-done.3.refs_4_), channel_id=1, source_target_pairs={{0,1},{1,0},{2,3},{3,2},{4,5},{5,4},{6,7},{7,6},{8,9},{9,8},{10,11... | collective-permute-start | bytes 196616 | tf_op jit(solution)/shard_map/ppermute | solution.py:319
  11.6 3.2 %collective-permute-start.2 = (bf16[64,512]{1,0:T(8,128)(2,1)S(1)}, bf16[64,512]{1,0:T(8,128)(2,1)S(1)}, u32[]{:S(2)}, u32[]{:S(2)}) collective-permute-start(bf16[64,512]{1,0:T(8,128)(2,1)S(1)} %collective-permute-done.1.refs_2_), channel_id=1, source_target_pairs={{0,1},{1,0},{2,3},{3,2},{4,5},{5,4},{6,7},{7,6},{8,9},{9,8},{10,11... | collective-permute-start | bytes 196616 | tf_op jit(solution)/shard_map/ppermute | solution.py:319
  22.0 2.0 %collective-permute-start.7 = (bf16[256,1024]{1,0:T(8,128)(2,1)S(1)}, bf16[256,1024]{1,0:T(8,128)(2,1)S(1)}, u32[]{:S(2)}, u32[]{:S(2)}) collective-permute-start(bf16[256,1024]{1,0:T(8,128)(2,1)S(1)} %get-tuple-element.40), channel_id=1, source_target_pairs={{0,1},{1,0},{2,3},{3,2},{4,5},{5,4},{6,7},{7,6},{8,9},{9,8},{10,11... | collective-permute-start | bytes 1572872 | tf_op jit(solution)/shard_map/ppermute | solution.py:319
  22.1 2.6 %collective-permute-start.8 = (bf16[256,1024]{1,0:T(8,128)(2,1)S(1)}, bf16[256,1024]{1,0:T(8,128)(2,1)S(1)}, u32[]{:S(2)}, u32[]{:S(2)}) collective-permute-start(bf16[256,1024]{1,0:T(8,128)(2,1)S(1)} %get-tuple-element.42), channel_id=1, source_target_pairs={{0,1},{1,0},{2,3},{3,2},{4,5},{5,4},{6,7},{7,6},{8,9},{9,8},{10,11... | collective-permute-start | bytes 1572872 | tf_op jit(solution)/shard_map/ppermute | solution.py:319
  22.6 2.9 %collective-permute-start.9 = (bf16[256,1024]{1,0:T(8,128)(2,1)S(1)}, bf16[256,1024]{1,0:T(8,128)(2,1)S(1)}, u32[]{:S(2)}, u32[]{:S(2)}) collective-permute-start(bf16[256,1024]{1,0:T(8,128)(2,1)S(1)} %get-tuple-element.44), channel_id=1, source_target_pairs={{0,1},{1,0},{2,3},{3,2},{4,5},{5,4},{6,7},{7,6},{8,9},{9,8},{10,11... | collective-permute-start | bytes 1572872 | tf_op jit(solution)/shard_map/ppermute | solution.py:319
  24.7 4.9 %copy-start = (bf16[512,512]{1,0:T(8,128)(2,1)S(1)}, bf16[512,512]{1,0:T(8,128)(2,1)}, u32[]{:S(2)}) copy-start(bf16[512,512]{1,0:T(8,128)(2,1)} %wout_ref.1) | copy-start | bytes 1572868
  25.7 8.4 %collective-permute-start.12 = (bf16[128,1024]{1,0:T(8,128)(2,1)S(1)}, bf16[128,1024]{1,0:T(8,128)(2,1)S(1)}, u32[]{:S(2)}, u32[]{:S(2)}) collective-permute-start(bf16[128,1024]{1,0:T(8,128)(2,1)S(1)} %slice.65), channel_id=1, source_target_pairs={{0,2},{1,3},{2,0},{3,1},{4,6},{5,7},{6,4},{7,5},{8,10},{9,11},{10,... | collective-permute-start | bytes 786440 | tf_op jit(solution)/shard_map/ppermute | solution.py:297
  26.5 8.4 %collective-permute-start.11 = (bf16[128,1024]{1,0:T(8,128)(2,1)S(1)}, bf16[128,1024]{1,0:T(8,128)(2,1)S(1)}, u32[]{:S(2)}, u32[]{:S(2)}) collective-permute-start(bf16[128,1024]{1,0:T(8,128)(2,1)S(1)} %slice.63), channel_id=1, source_target_pairs={{0,16},{8,24},{16,0},{24,8},{1,17},{9,25},{17,1},{25,9},{2,18},{10... | collective-permute-start | bytes 786440 | tf_op jit(solution)/shard_map/ppermute | solution.py:299
  28.1 8.1 %collective-permute-start.10 = (bf16[128,1024]{1,0:T(8,128)(2,1)S(1)}, bf16[128,1024]{1,0:T(8,128)(2,1)S(1)}, u32[]{:S(2)}, u32[]{:S(2)}) collective-permute-start(bf16[128,1024]{1,0:T(8,128)(2,1)S(1)} %slice.61), channel_id=1, source_target_pairs={{0,8},{8,0},{16,24},{24,16},{1,9},{9,1},{17,25},{25,17},{2,10},{10... | collective-permute-start | bytes 786440 | tf_op jit(solution)/shard_map/ppermute | solution.py:299
  36.3 5.0 %collective-permute-start.17 = (bf16[64,1024]{1,0:T(8,128)(2,1)S(1)}, bf16[64,1024]{1,0:T(8,128)(2,1)S(1)}, u32[]{:S(2)}, u32[]{:S(2)}) collective-permute-start(bf16[64,1024]{1,0:T(8,128)(2,1)S(1)} %slice.75), channel_id=1, source_target_pairs={{0,8},{8,0},{16,24},{24,16},{1,9},{9,1},{17,25},{25,17},{2,10},{10... | collective-permute-start | bytes 393224 | tf_op jit(solution)/shard_map/ppermute | solution.py:299
  37.9 5.0 %collective-permute-start.15 = (bf16[64,1024]{1,0:T(8,128)(2,1)S(1)}, bf16[64,1024]{1,0:T(8,128)(2,1)S(1)}, u32[]{:S(2)}, u32[]{:S(2)}) collective-permute-start(bf16[64,1024]{1,0:T(8,128)(2,1)S(1)} %slice.71), channel_id=1, source_target_pairs={{0,2},{1,3},{2,0},{3,1},{4,6},{5,7},{6,4},{7,5},{8,10},{9,11},{10,... | collective-permute-start | bytes 393224 | tf_op jit(solution)/shard_map/ppermute | solution.py:297
  39.0 5.0 %collective-permute-start.13 = (bf16[64,1024]{1,0:T(8,128)(2,1)S(1)}, bf16[64,1024]{1,0:T(8,128)(2,1)S(1)}, u32[]{:S(2)}, u32[]{:S(2)}) collective-permute-start(bf16[64,1024]{1,0:T(8,128)(2,1)S(1)} %slice.67), channel_id=1, source_target_pairs={{0,16},{8,24},{16,0},{24,8},{1,17},{9,25},{17,1},{25,9},{2,18},{10... | collective-permute-start | bytes 393224 | tf_op jit(solution)/shard_map/ppermute | solution.py:299
  41.4 4.3 %collective-permute-start.18 = (bf16[32,1024]{1,0:T(8,128)(2,1)S(1)}, bf16[32,1024]{1,0:T(8,128)(2,1)S(1)}, u32[]{:S(2)}, u32[]{:S(2)}) collective-permute-start(bf16[32,1024]{1,0:T(8,128)(2,1)S(1)} %slice.85), channel_id=1, source_target_pairs={{0,16},{8,24},{16,0},{24,8},{1,17},{9,25},{17,1},{25,9},{2,18},{10... | collective-permute-start | bytes 196616 | tf_op jit(solution)/shard_map/ppermute | solution.py:299
  43.0 4.3 %collective-permute-start.16 = (bf16[32,1024]{1,0:T(8,128)(2,1)S(1)}, bf16[32,1024]{1,0:T(8,128)(2,1)S(1)}, u32[]{:S(2)}, u32[]{:S(2)}) collective-permute-start(bf16[32,1024]{1,0:T(8,128)(2,1)S(1)} %slice.83), channel_id=1, source_target_pairs={{0,8},{8,0},{16,24},{24,16},{1,9},{9,1},{17,25},{25,17},{2,10},{10... | collective-permute-start | bytes 196616 | tf_op jit(solution)/shard_map/ppermute | solution.py:299
  44.1 5.1 %collective-permute-start.14 = (bf16[32,1024]{1,0:T(8,128)(2,1)S(1)}, bf16[32,1024]{1,0:T(8,128)(2,1)S(1)}, u32[]{:S(2)}, u32[]{:S(2)}) collective-permute-start(bf16[32,1024]{1,0:T(8,128)(2,1)S(1)} %slice.81), channel_id=1, source_target_pairs={{0,2},{1,3},{2,0},{3,1},{4,6},{5,7},{6,4},{7,5},{8,10},{9,11},{10,... | collective-permute-start | bytes 196616 | tf_op jit(solution)/shard_map/ppermute | solution.py:297
  49.2 6.5 %collective-permute-start.19 = (bf16[16,3072]{1,0:T(8,128)(2,1)S(1)}, bf16[16,3072]{1,0:T(8,128)(2,1)S(1)}, u32[]{:S(2)}, u32[]{:S(2)}) collective-permute-start(bf16[16,3072]{1,0:T(8,128)(2,1)S(1)} %get-tuple-element.56), channel_id=1, source_target_pairs={{0,4},{1,5},{2,6},{3,7},{4,0},{5,1},{6,2},{7,3},{8,12},{9,13},{10,... | collective-permute-start | bytes 294920 | tf_op jit(solution)/shard_map/ppermute | solution.py:297

commit v5 on v4

--- a/solution.py
+++ b/solution.py
@@ -274,14 +274,17 @@
                 ]
 
 
-def finish_kernel(keep_ref, got_ref, grad_u_ref, grad_o_ref, grad_t_ref):
+def finish_kernel(*refs):
+    grad_u_ref, grad_o_ref, grad_t_ref = refs[-3:]
     blk, width = grad_o_ref.shape
     feats, span = grad_t_ref.shape
-    total = keep_ref[...].astype(F32) + got_ref[...].astype(F32)
-    grad_o_ref[...] = total[:, :width]
-    grad_u_ref[...] = total[:, width : 5 * width]
+    first, second, third = (refs[n][...].astype(F32) + refs[n + 1][...].astype(F32) for n in range(0, 6, 2))
+    grad_o_ref[...] = first[:, :width]
+    grad_u_ref[:, :width] = first[:, width:]
+    grad_u_ref[:, width : 3 * width] = second
+    grad_u_ref[:, 3 * width :] = third[:, :width]
     for j in range(feats // blk):
-        grad_t_ref[j * blk : (j + 1) * blk, :] = total[:, 5 * width + j * span : 5 * width + (j + 1) * span]
+        grad_t_ref[j * blk : (j + 1) * blk, :] = third[:, width + j * span : width + (j + 1) * span]
 
 
 VMEM_SPEC = pl.BlockSpec(memory_space=pltpu.VMEM)
@@ -413,24 +416,24 @@
         return v[:h], v[h:]
 
     totals = [add(keep, other(send, 1)) for keep, send in zip(grads[::2], grads[1::2])]
-    gated, *totals = lax.optimization_barrier((gated, *totals))
+    gated, totals[0] = lax.optimization_barrier((gated, totals[0]))
     output = finish_output(gated)
     for n in range(len(ring)):
         for c in range(colours):
             keep, send = halves(totals[c])
             totals[c] = add(keep, swap(send, order[c][1 + n], tab_bits, dps, tabs))
-        if n == 0:
-            output, *totals = lax.optimization_barrier((output, *totals))
-    keep, send = halves(jnp.concatenate(totals, axis=1))
-    got = swap(send, tab_bits - 1, tab_bits, dps, tabs)
+    last = []
+    for total in totals:
+        keep, send = halves(total)
+        last += [keep, swap(send, tab_bits - 1, tab_bits, dps, tabs)]
     grad_uvqk, grad_out_t, grad_t = pl.pallas_call(
         finish_kernel,
         out_shape=(sds((blk, 4 * width), F32), sds((blk, width), F32), sds((feats, span), F32)),
-        in_specs=[VMEM_SPEC] * 2,
+        in_specs=[VMEM_SPEC] * len(last),
         out_specs=(VMEM_SPEC,) * 3,
         compiler_params=pltpu.CompilerParams(vmem_limit_bytes=8 << 20),
         name="finish",
-    )(keep, got)
+    )(*last)
     return (output, grad_t.T, grad_uvqk, grad_out_t)
 
 

time: 56.6 us -> 52 us (0.919)
  waiting for transfers between devices: 23.8 us -> 14.2 us
  starting transfers between devices: 18.3 us -> 23.3 us
    ppermute x4 -> x6, waiting for transfers between devices: 9.88 us -> 2.56 us  [swap(): return lax.ppermute(v, 'table', [(i, i ^ 1 << bit) for i in range(tabs)])]
    ppermute x4 -> x6, starting transfers between devices: 4.99 us -> 8.27 us  [swap(): return lax.ppermute(v, 'table', [(i, i ^ 1 << bit) for i in range(tabs)])]
    ppermute x6, starting transfers between devices: 6.39 us -> 8.06 us  [swap(): return lax.ppermute(v, 'dp', [(i, i ^ 1 << b) for i in range(dps)])]
    ppermute x6, waiting for transfers between devices: 6.36 us -> 5.16 us  [swap(): return lax.ppermute(v, 'dp', [(i, i ^ 1 << b) for i in range(dps)])]
    ppermute x10, waiting for transfers between devices: 7.6 us -> 6.5 us  [other(): return lax.ppermute(v, 'table', [(i, i ^ rel) for i in range(tabs)])]
  transfers between devices with their start and end apart: 20 -> 22, of which waited for: 15 -> 10; matrix products, arithmetic and copies ran while one was open for 3% -> 3% of each run, Pallas kernels for 7% -> 7%
where the time goes in v5:
time: 52 us; the launch traced here: 51.7 us
  starting transfers between devices  23.3 us (45%)
  waiting for transfers between devices  14.2 us (27%)
  Pallas kernels  11.6 us (22%)
  other arithmetic  0.93 us (2%)
  between operations  0.86 us (2%)
  local copies, waits for them, and re-layouts  0.85 us (2%)
    ppermute x6, starting transfers between devices, swap(): return lax.ppermute(v, 'table', [(i, i ^ 1 << bit) for i in range(tabs)])  8.27 us
    ppermute x6, starting transfers between devices, swap(): return lax.ppermute(v, 'dp', [(i, i ^ 1 << b) for i in range(dps)])  8.06 us
    pallas_call x1, Pallas kernels, layer(): pl.pallas_call(functools.partial(layer_kernel, order, (dps, tabs)), out_s...  7.17 us
    ppermute x10, starting transfers between devices, other(): return lax.ppermute(v, 'table', [(i, i ^ rel) for i in range(tabs)])  6.96 us
    ppermute x10, waiting for transfers between devices, other(): return lax.ppermute(v, 'table', [(i, i ^ rel) for i in range(tabs)])  6.5 us
    ppermute x6, waiting for transfers between devices, swap(): return lax.ppermute(v, 'dp', [(i, i ^ 1 << b) for i in range(dps)])  5.16 us
    ppermute x6, waiting for transfers between devices, swap(): return lax.ppermute(v, 'table', [(i, i ^ 1 << bit) for i in range(tabs)])  2.56 us
    pallas_call x1, Pallas kernels, layer(): pl.pallas_call(prep_kernel, out_shape=(sds((live, items), BF), sds((live,...  1.97 us
  transfers between devices with their start and end apart: 22, of which 10 were waited for; matrix products, arithmetic and copies ran while one was open for 3% of the time, Pallas kernels for 7%

profile of v5, /device:TPU:0, one launch (start us, length us, event | category | flops | bytes accessed | tf_op | source)
XLA Modules:
  0.0 51.7 jit_solution(13000358786350614606)
XLA Ops:
  0.6 5.1 %collective-permute-start.5 = (bf16[64,512]{1,0:T(8,128)(2,1)}, bf16[64,512]{1,0:T(8,128)(2,1)S(1)}, u32[]{:S(2)}, u32[]{:S(2)}) collective-permute-start(bf16[64,512]{1,0:T(8,128)(2,1)} %bitcast.2), channel_id=1, source_target_pairs={{0,6},{1,7},{2,4},{3,5},{4,2},{5,3},{6,0},{7,1},{8,14},{9,15},{10,... | collective-permute-start | bytes 196616 | tf_op jit(solution)/shard_map/ppermute | solution.py:322
  5.8 0.6 %collective-permute-start.1 = (bf16[64,512]{1,0:T(8,128)(2,1)}, bf16[64,512]{1,0:T(8,128)(2,1)S(1)}, u32[]{:S(2)}, u32[]{:S(2)}) collective-permute-start(bf16[64,512]{1,0:T(8,128)(2,1)} %bitcast.4), channel_id=1, source_target_pairs={{0,2},{1,3},{2,0},{3,1},{4,6},{5,7},{6,4},{7,5},{8,10},{9,11},{10,... | collective-permute-start | bytes 196616 | tf_op jit(solution)/shard_map/ppermute | solution.py:322
  6.4 2.2 %collective-permute-done.5.refs_6_ = bf16[64,512]{1,0:T(8,128)(2,1)S(1)} collective-permute-done((bf16[64,512]{1,0:T(8,128)(2,1)}, bf16[64,512]{1,0:T(8,128)(2,1)S(1)}, u32[]{:S(2)}, u32[]{:S(2)}) %collective-permute-start.5) | collective-permute-done | bytes 65568 | tf_op jit(solution)/shard_map/ppermute | solution.py:322
  8.6 3.0 %collective-permute-done.3.refs_4_ = bf16[64,512]{1,0:T(8,128)(2,1)S(1)} collective-permute-done((bf16[64,512]{1,0:T(8,128)(2,1)}, bf16[64,512]{1,0:T(8,128)(2,1)S(1)}, u32[]{:S(2)}, u32[]{:S(2)}) %collective-permute-start.3) | collective-permute-done | bytes 65568 | tf_op jit(solution)/shard_map/ppermute | solution.py:322
  12.1 0.7 %reshape.11.ids_ref = s32[8,512]{1,0:T(8,128)S(1)} reshape(s32[4096]{0:T(1024)} %param.6) | data formatting | bytes 32768 | tf_op jit(solution)/shard_map/reshape | solution.py:317
  12.8 2.0 %prep.1 = (bf16[320,512]{1,0:T(8,128)(2,1)S(1)}, bf16[320,512]{1,0:T(8,128)(2,1)S(1)}, bf16[320,512]{1,0:T(8,128)(2,1)S(1)}, s32[320,128]{1,0:T(8,128)S(1)}, s32...) custom-call(s32[1,8]{1,0:T(1,128)} %len_hbm.1, s32[8,512]{1,0:T(8,128)S(1)} %reshape.11.ids_ref, ...), custom_call_target="tpu_custom_call" | custom-call | tf_op jit(solution)/shard_map/prep/pallas_call | solution.py:328
  14.8 7.2 %layer.1 = (bf16[320,512]{1,0:T(8,128)(2,1)S(1)}, bf16[512,512]{1,0:T(8,128)(2,1)S(1)}, bf16[256,1024]{1,0:T(8,128)(2,1)S(1)}, bf16[256,1024]{1,0:T(8,128)(2,1)S...) custom-call(s32[320,128]{1,0:T(8,128)S(1)} %get-tuple-element.25.sta, ...), custom_call_target="tpu_custom_call" | custom-call | tf_op jit(solution)/shard_map/layer/pallas_call | solution.py:367
  22.7 1.3 %collective-permute-done.7 = bf16[256,1024]{1,0:T(8,128)(2,1)S(1)} collective-permute-done((bf16[256,1024]{1,0:T(8,128)(2,1)S(1)}, bf16[256,1024]{1,0:T(8,128)(2,1)S(1)}, u32[]{:S(2)}, u32[]{:S(2)}) %collective-permute-start.7) | collective-permute-done | bytes 524320 | tf_op jit(solution)/shard_map/ppermute | solution.py:322
  24.2 1.6 %collective-permute-start.8 = (bf16[128,1024]{1,0:T(8,128)(2,1)S(1)}, bf16[128,1024]{1,0:T(8,128)(2,1)S(1)}, u32[]{:S(2)}, u32[]{:S(2)}) collective-permute-start(bf16[128,1024]{1,0:T(8,128)(2,1)S(1)} %slice.73), channel_id=1, source_target_pairs={{0,8},{8,0},{16,24},{24,16},{1,9},{9,1},{17,25},{25,17},{2,10},{10... | collective-permute-start | bytes 786440 | tf_op jit(solution)/shard_map/ppermute | solution.py:302
  26.0 1.6 %collective-permute-start.13 = (bf16[128,1024]{1,0:T(8,128)(2,1)S(1)}, bf16[128,1024]{1,0:T(8,128)(2,1)S(1)}, u32[]{:S(2)}, u32[]{:S(2)}) collective-permute-start(bf16[128,1024]{1,0:T(8,128)(2,1)S(1)} %slice.103), channel_id=1, source_target_pairs={{0,16},{8,24},{16,0},{24,8},{1,17},{9,25},{17,1},{25,9},{2,18},{10... | collective-permute-start | bytes 786440 | tf_op jit(solution)/shard_map/ppermute | solution.py:302
  27.8 0.8 %collective-permute-start.18 = (bf16[128,1024]{1,0:T(8,128)(2,1)S(1)}, bf16[128,1024]{1,0:T(8,128)(2,1)S(1)}, u32[]{:S(2)}, u32[]{:S(2)}) collective-permute-start(bf16[128,1024]{1,0:T(8,128)(2,1)S(1)} %slice.111), channel_id=1, source_target_pairs={{0,2},{1,3},{2,0},{3,1},{4,6},{5,7},{6,4},{7,5},{8,10},{9,11},{10,... | collective-permute-start | bytes 786440 | tf_op jit(solution)/shard_map/ppermute | solution.py:300
  28.6 4.0 %collective-permute-done.8 = bf16[128,1024]{1,0:T(8,128)(2,1)S(1)} collective-permute-done((bf16[128,1024]{1,0:T(8,128)(2,1)S(1)}, bf16[128,1024]{1,0:T(8,128)(2,1)S(1)}, u32[]{:S(2)}, u32[]{:S(2)}) %collective-permute-start.8) | collective-permute-done | bytes 262176 | tf_op jit(solution)/shard_map/ppermute | solution.py:302
  32.7 1.6 %collective-permute-start.9 = (bf16[64,1024]{1,0:T(8,128)(2,1)S(1)}, bf16[64,1024]{1,0:T(8,128)(2,1)S(1)}, u32[]{:S(2)}, u32[]{:S(2)}) collective-permute-start(bf16[64,1024]{1,0:T(8,128)(2,1)S(1)} %slice.97), channel_id=1, source_target_pairs={{0,16},{8,24},{16,0},{24,8},{1,17},{9,25},{17,1},{25,9},{2,18},{10... | collective-permute-start | bytes 393224 | tf_op jit(solution)/shard_map/ppermute | solution.py:302
  34.4 1.0 %collective-permute-start.14 = (bf16[64,1024]{1,0:T(8,128)(2,1)S(1)}, bf16[64,1024]{1,0:T(8,128)(2,1)S(1)}, u32[]{:S(2)}, u32[]{:S(2)}) collective-permute-start(bf16[64,1024]{1,0:T(8,128)(2,1)S(1)} %slice.105), channel_id=1, source_target_pairs={{0,2},{1,3},{2,0},{3,1},{4,6},{5,7},{6,4},{7,5},{8,10},{9,11},{10,... | collective-permute-start | bytes 393224 | tf_op jit(solution)/shard_map/ppermute | solution.py:300
  35.8 1.3 %collective-permute-start.19 = (bf16[64,1024]{1,0:T(8,128)(2,1)S(1)}, bf16[64,1024]{1,0:T(8,128)(2,1)S(1)}, u32[]{:S(2)}, u32[]{:S(2)}) collective-permute-start(bf16[64,1024]{1,0:T(8,128)(2,1)S(1)} %slice.113), channel_id=1, source_target_pairs={{0,8},{8,0},{16,24},{24,16},{1,9},{9,1},{17,25},{25,17},{2,10},{10... | collective-permute-start | bytes 393224 | tf_op jit(solution)/shard_map/ppermute | solution.py:302
  37.1 0.7 %collective-permute-done.9 = bf16[64,1024]{1,0:T(8,128)(2,1)S(1)} collective-permute-done((bf16[64,1024]{1,0:T(8,128)(2,1)S(1)}, bf16[64,1024]{1,0:T(8,128)(2,1)S(1)}, u32[]{:S(2)}, u32[]{:S(2)}) %collective-permute-start.9) | collective-permute-done | bytes 131104 | tf_op jit(solution)/shard_map/ppermute | solution.py:302
  37.8 1.0 %collective-permute-start.10 = (bf16[32,1024]{1,0:T(8,128)(2,1)S(1)}, bf16[32,1024]{1,0:T(8,128)(2,1)S(1)}, u32[]{:S(2)}, u32[]{:S(2)}) collective-permute-start(bf16[32,1024]{1,0:T(8,128)(2,1)S(1)} %slice.99), channel_id=1, source_target_pairs={{0,2},{1,3},{2,0},{3,1},{4,6},{5,7},{6,4},{7,5},{8,10},{9,11},{10,... | collective-permute-start | bytes 196616 | tf_op jit(solution)/shard_map/ppermute | solution.py:300
  38.8 1.3 %collective-permute-done.14 = bf16[64,1024]{1,0:T(8,128)(2,1)S(1)} collective-permute-done((bf16[64,1024]{1,0:T(8,128)(2,1)S(1)}, bf16[64,1024]{1,0:T(8,128)(2,1)S(1)}, u32[]{:S(2)}, u32[]{:S(2)}) %collective-permute-start.14) | collective-permute-done | bytes 131104 | tf_op jit(solution)/shard_map/ppermute | solution.py:300
  40.2 1.6 %collective-permute-start.15 = (bf16[32,1024]{1,0:T(8,128)(2,1)S(1)}, bf16[32,1024]{1,0:T(8,128)(2,1)S(1)}, u32[]{:S(2)}, u32[]{:S(2)}) collective-permute-start(bf16[32,1024]{1,0:T(8,128)(2,1)S(1)} %slice.107), channel_id=1, source_target_pairs={{0,8},{8,0},{16,24},{24,16},{1,9},{9,1},{17,25},{25,17},{2,10},{10... | collective-permute-start | bytes 196616 | tf_op jit(solution)/shard_map/ppermute | solution.py:302
  42.3 2.8 %collective-permute-start.11 = (bf16[16,1024]{1,0:T(8,128)(2,1)S(1)}, bf16[16,1024]{1,0:T(8,128)(2,1)S(1)}, u32[]{:S(2)}, u32[]{:S(2)}) collective-permute-start(bf16[16,1024]{1,0:T(8,128)(2,1)S(1)} %get-tuple-element.48), channel_id=1, source_target_pairs={{0,4},{1,5},{2,6},{3,7},{4,0},{5,1},{6,2},{7,3},{8,12},{9,13},{10,... | collective-permute-start | bytes 98312 | tf_op jit(solution)/shard_map/ppermute | solution.py:300
  46.2 2.1 %collective-permute-start.21 = (bf16[16,1024]{1,0:T(8,128)(2,1)S(1)}, bf16[16,1024]{1,0:T(8,128)(2,1)S(1)}, u32[]{:S(2)}, u32[]{:S(2)}) collective-permute-start(bf16[16,1024]{1,0:T(8,128)(2,1)S(1)} %get-tuple-element.44), channel_id=1, source_target_pairs={{0,4},{1,5},{2,6},{3,7},{4,0},{5,1},{6,2},{7,3},{8,12},{9,13},{10,... | collective-permute-start | bytes 98312 | tf_op jit(solution)/shard_map/ppermute | solution.py:300
  48.3 1.8 %out.1 = bf16[512,512]{1,0:T(8,128)(2,1)} custom-call(s32[8,320]{1,0:T(8,128)S(1)} %get-tuple-element.24.origin_ref, s32[8,512]{1,0:T(8,128)S(1)} %reshape.11.ids_ref, bf16[512,512]{1,0:T(8,128)(2,1)S(1)} %get-tuple-element.31.tab_ref, bf16[320,512]{1,0:T(8,128)(2,1)S(1)} %get-tuple-element.35.gated_ref, bf16[512,512]{1,0:T(8,128)(2,1)S(1)} %copy-done), custom_call_target="tpu_custom_call" | custom-call | tf_op jit(solution)/shard_map/out/pallas_call | solution.py:392
  50.2 0.8 %collective-permute-done.21.refs_5_ = bf16[16,1024]{1,0:T(8,128)(2,1)S(1)} collective-permute-done((bf16[16,1024]{1,0:T(8,128)(2,1)S(1)}, bf16[16,1024]{1,0:T(8,128)(2,1)S(1)}, u32[]{:S(2)}, u32[]{:S(2)}) %collective-permute-start.21) | collective-permute-done | bytes 32800 | tf_op jit(solution)/shard_map/ppermute | solution.py:300
  51.1 0.7 %finish.1 = (f32[16,2048]{1,0:T(8,128)}, f32[16,512]{1,0:T(8,128)}, f32[64,128]{1,0:T(8,128)}) custom-call(bf16[16,1024]{1,0:T(8,128)(2,1)S(1)} %get-tuple-element.49.refs_0_, bf16[16,1024]{1,0:T(8,128)(2,1)S(1)} %collective-permute-done.11.refs_1_, bf16[16,1024]{1,0:T(8,128)(2,1)S(1)} %get-tuple-element.47.refs_2_, ...), custom_call_target="tpu_custom_call" | custom-call | tf_op jit(solution)/shard_map/finish/pallas_call | solution.py:429
  (51 shorter events, 4.1 us)
Async XLA Ops:
  0.6 7.9 %collective-permute-start.5 = (bf16[64,512]{1,0:T(8,128)(2,1)}, bf16[64,512]{1,0:T(8,128)(2,1)S(1)}, u32[]{:S(2)}, u32[]{:S(2)}) collective-permute-start(bf16[64,512]{1,0:T(8,128)(2,1)} %bitcast.2), channel_id=1, source_target_pairs={{0,6},{1,7},{2,4},{3,5},{4,2},{5,3},{6,0},{7,1},{8,14},{9,15},{10,... | collective-permute-start | bytes 196616 | tf_op jit(solution)/shard_map/ppermute | solution.py:322
  5.8 5.8 %collective-permute-start.3 = (bf16[64,512]{1,0:T(8,128)(2,1)}, bf16[64,512]{1,0:T(8,128)(2,1)S(1)}, u32[]{:S(2)}, u32[]{:S(2)}) collective-permute-start(bf16[64,512]{1,0:T(8,128)(2,1)} %bitcast.3), channel_id=1, source_target_pairs={{0,4},{1,5},{2,6},{3,7},{4,0},{5,1},{6,2},{7,3},{8,12},{9,13},{10,... | collective-permute-start | bytes 196616 | tf_op jit(solution)/shard_map/ppermute | solution.py:322
  5.8 5.8 %collective-permute-start.1 = (bf16[64,512]{1,0:T(8,128)(2,1)}, bf16[64,512]{1,0:T(8,128)(2,1)S(1)}, u32[]{:S(2)}, u32[]{:S(2)}) collective-permute-start(bf16[64,512]{1,0:T(8,128)(2,1)} %bitcast.4), channel_id=1, source_target_pairs={{0,2},{1,3},{2,0},{3,1},{4,6},{5,7},{6,4},{7,5},{8,10},{9,11},{10,... | collective-permute-start | bytes 196616 | tf_op jit(solution)/shard_map/ppermute | solution.py:322
  6.4 8.4 %collective-permute-start = (bf16[64,512]{1,0:T(8,128)(2,1)}, bf16[64,512]{1,0:T(8,128)(2,1)S(1)}, u32[]{:S(2)}, u32[]{:S(2)}) collective-permute-start(bf16[64,512]{1,0:T(8,128)(2,1)} %bitcast.5), channel_id=1, source_target_pairs={{0,1},{1,0},{2,3},{3,2},{4,5},{5,4},{6,7},{7,6},{8,9},{9,8},{10,11... | collective-permute-start | bytes 196616 | tf_op jit(solution)/shard_map/ppermute | solution.py:322
  8.6 6.2 %collective-permute-start.6 = (bf16[64,512]{1,0:T(8,128)(2,1)S(1)}, bf16[64,512]{1,0:T(8,128)(2,1)S(1)}, u32[]{:S(2)}, u32[]{:S(2)}) collective-permute-start(bf16[64,512]{1,0:T(8,128)(2,1)S(1)} %collective-permute-done.5.refs_6_), channel_id=1, source_target_pairs={{0,1},{1,0},{2,3},{3,2},{4,5},{5,4},{6,7},{7,6},{8,9},{9,8},{10,11... | collective-permute-start | bytes 196616 | tf_op jit(solution)/shard_map/ppermute | solution.py:322
  11.6 3.2 %collective-permute-start.4 = (bf16[64,512]{1,0:T(8,128)(2,1)S(1)}, bf16[64,512]{1,0:T(8,128)(2,1)S(1)}, u32[]{:S(2)}, u32[]{:S(2)}) collective-permute-start(bf16[64,512]{1,0:T(8,128)(2,1)S(1)} %collective-permute-done.3.refs_4_), channel_id=1, source_target_pairs={{0,1},{1,0},{2,3},{3,2},{4,5},{5,4},{6,7},{7,6},{8,9},{9,8},{10,11... | collective-permute-start | bytes 196616 | tf_op jit(solution)/shard_map/ppermute | solution.py:322
  11.6 3.2 %collective-permute-start.2 = (bf16[64,512]{1,0:T(8,128)(2,1)S(1)}, bf16[64,512]{1,0:T(8,128)(2,1)S(1)}, u32[]{:S(2)}, u32[]{:S(2)}) collective-permute-start(bf16[64,512]{1,0:T(8,128)(2,1)S(1)} %collective-permute-done.1.refs_2_), channel_id=1, source_target_pairs={{0,1},{1,0},{2,3},{3,2},{4,5},{5,4},{6,7},{7,6},{8,9},{9,8},{10,11... | collective-permute-start | bytes 196616 | tf_op jit(solution)/shard_map/ppermute | solution.py:322
  22.0 2.0 %collective-permute-start.7 = (bf16[256,1024]{1,0:T(8,128)(2,1)S(1)}, bf16[256,1024]{1,0:T(8,128)(2,1)S(1)}, u32[]{:S(2)}, u32[]{:S(2)}) collective-permute-start(bf16[256,1024]{1,0:T(8,128)(2,1)S(1)} %get-tuple-element.34), channel_id=1, source_target_pairs={{0,1},{1,0},{2,3},{3,2},{4,5},{5,4},{6,7},{7,6},{8,9},{9,8},{10,11... | collective-permute-start | bytes 1572872 | tf_op jit(solution)/shard_map/ppermute | solution.py:322
  22.1 3.7 %collective-permute-start.12 = (bf16[256,1024]{1,0:T(8,128)(2,1)S(1)}, bf16[256,1024]{1,0:T(8,128)(2,1)S(1)}, u32[]{:S(2)}, u32[]{:S(2)}) collective-permute-start(bf16[256,1024]{1,0:T(8,128)(2,1)S(1)} %get-tuple-element.38), channel_id=1, source_target_pairs={{0,1},{1,0},{2,3},{3,2},{4,5},{5,4},{6,7},{7,6},{8,9},{9,8},{10,11... | collective-permute-start | bytes 1572872 | tf_op jit(solution)/shard_map/ppermute | solution.py:322
  22.6 5.0 %collective-permute-start.17 = (bf16[256,1024]{1,0:T(8,128)(2,1)S(1)}, bf16[256,1024]{1,0:T(8,128)(2,1)S(1)}, u32[]{:S(2)}, u32[]{:S(2)}) collective-permute-start(bf16[256,1024]{1,0:T(8,128)(2,1)S(1)} %get-tuple-element.40), channel_id=1, source_target_pairs={{0,1},{1,0},{2,3},{3,2},{4,5},{5,4},{6,7},{7,6},{8,9},{9,8},{10,11... | collective-permute-start | bytes 1572872 | tf_op jit(solution)/shard_map/ppermute | solution.py:322
  24.2 8.4 %collective-permute-start.8 = (bf16[128,1024]{1,0:T(8,128)(2,1)S(1)}, bf16[128,1024]{1,0:T(8,128)(2,1)S(1)}, u32[]{:S(2)}, u32[]{:S(2)}) collective-permute-start(bf16[128,1024]{1,0:T(8,128)(2,1)S(1)} %slice.73), channel_id=1, source_target_pairs={{0,8},{8,0},{16,24},{24,16},{1,9},{9,1},{17,25},{25,17},{2,10},{10... | collective-permute-start | bytes 786440 | tf_op jit(solution)/shard_map/ppermute | solution.py:302
  26.0 8.3 %collective-permute-start.13 = (bf16[128,1024]{1,0:T(8,128)(2,1)S(1)}, bf16[128,1024]{1,0:T(8,128)(2,1)S(1)}, u32[]{:S(2)}, u32[]{:S(2)}) collective-permute-start(bf16[128,1024]{1,0:T(8,128)(2,1)S(1)} %slice.103), channel_id=1, source_target_pairs={{0,16},{8,24},{16,0},{24,8},{1,17},{9,25},{17,1},{25,9},{2,18},{10... | collective-permute-start | bytes 786440 | tf_op jit(solution)/shard_map/ppermute | solution.py:302
  27.8 7.9 %collective-permute-start.18 = (bf16[128,1024]{1,0:T(8,128)(2,1)S(1)}, bf16[128,1024]{1,0:T(8,128)(2,1)S(1)}, u32[]{:S(2)}, u32[]{:S(2)}) collective-permute-start(bf16[128,1024]{1,0:T(8,128)(2,1)S(1)} %slice.111), channel_id=1, source_target_pairs={{0,2},{1,3},{2,0},{3,1},{4,6},{5,7},{6,4},{7,5},{8,10},{9,11},{10,... | collective-permute-start | bytes 786440 | tf_op jit(solution)/shard_map/ppermute | solution.py:300
  32.7 5.0 %collective-permute-start.9 = (bf16[64,1024]{1,0:T(8,128)(2,1)S(1)}, bf16[64,1024]{1,0:T(8,128)(2,1)S(1)}, u32[]{:S(2)}, u32[]{:S(2)}) collective-permute-start(bf16[64,1024]{1,0:T(8,128)(2,1)S(1)} %slice.97), channel_id=1, source_target_pairs={{0,16},{8,24},{16,0},{24,8},{1,17},{9,25},{17,1},{25,9},{2,18},{10... | collective-permute-start | bytes 393224 | tf_op jit(solution)/shard_map/ppermute | solution.py:302
  34.4 13.9 %copy-start = (bf16[512,512]{1,0:T(8,128)(2,1)S(1)}, bf16[512,512]{1,0:T(8,128)(2,1)}, u32[]{:S(2)}) copy-start(bf16[512,512]{1,0:T(8,128)(2,1)} %wout_ref.1) | copy-start | bytes 1572868
  34.4 5.7 %collective-permute-start.14 = (bf16[64,1024]{1,0:T(8,128)(2,1)S(1)}, bf16[64,1024]{1,0:T(8,128)(2,1)S(1)}, u32[]{:S(2)}, u32[]{:S(2)}) collective-permute-start(bf16[64,1024]{1,0:T(8,128)(2,1)S(1)} %slice.105), channel_id=1, source_target_pairs={{0,2},{1,3},{2,0},{3,1},{4,6},{5,7},{6,4},{7,5},{8,10},{9,11},{10,... | collective-permute-start | bytes 393224 | tf_op jit(solution)/shard_map/ppermute | solution.py:300
  35.8 6.0 %collective-permute-start.19 = (bf16[64,1024]{1,0:T(8,128)(2,1)S(1)}, bf16[64,1024]{1,0:T(8,128)(2,1)S(1)}, u32[]{:S(2)}, u32[]{:S(2)}) collective-permute-start(bf16[64,1024]{1,0:T(8,128)(2,1)S(1)} %slice.113), channel_id=1, source_target_pairs={{0,8},{8,0},{16,24},{24,16},{1,9},{9,1},{17,25},{25,17},{2,10},{10... | collective-permute-start | bytes 393224 | tf_op jit(solution)/shard_map/ppermute | solution.py:302
  37.8 4.5 %collective-permute-start.10 = (bf16[32,1024]{1,0:T(8,128)(2,1)S(1)}, bf16[32,1024]{1,0:T(8,128)(2,1)S(1)}, u32[]{:S(2)}, u32[]{:S(2)}) collective-permute-start(bf16[32,1024]{1,0:T(8,128)(2,1)S(1)} %slice.99), channel_id=1, source_target_pairs={{0,2},{1,3},{2,0},{3,1},{4,6},{5,7},{6,4},{7,5},{8,10},{9,11},{10,... | collective-permute-start | bytes 196616 | tf_op jit(solution)/shard_map/ppermute | solution.py:300
  40.2 5.0 %collective-permute-start.15 = (bf16[32,1024]{1,0:T(8,128)(2,1)S(1)}, bf16[32,1024]{1,0:T(8,128)(2,1)S(1)}, u32[]{:S(2)}, u32[]{:S(2)}) collective-permute-start(bf16[32,1024]{1,0:T(8,128)(2,1)S(1)} %slice.107), channel_id=1, source_target_pairs={{0,8},{8,0},{16,24},{24,16},{1,9},{9,1},{17,25},{25,17},{2,10},{10... | collective-permute-start | bytes 196616 | tf_op jit(solution)/shard_map/ppermute | solution.py:302
  41.8 4.3 %collective-permute-start.20 = (bf16[32,1024]{1,0:T(8,128)(2,1)S(1)}, bf16[32,1024]{1,0:T(8,128)(2,1)S(1)}, u32[]{:S(2)}, u32[]{:S(2)}) collective-permute-start(bf16[32,1024]{1,0:T(8,128)(2,1)S(1)} %slice.115), channel_id=1, source_target_pairs={{0,16},{8,24},{16,0},{24,8},{1,17},{9,25},{17,1},{25,9},{2,18},{10... | collective-permute-start | bytes 196616 | tf_op jit(solution)/shard_map/ppermute | solution.py:302
  42.3 7.8 %collective-permute-start.11 = (bf16[16,1024]{1,0:T(8,128)(2,1)S(1)}, bf16[16,1024]{1,0:T(8,128)(2,1)S(1)}, u32[]{:S(2)}, u32[]{:S(2)}) collective-permute-start(bf16[16,1024]{1,0:T(8,128)(2,1)S(1)} %get-tuple-element.48), channel_id=1, source_target_pairs={{0,4},{1,5},{2,6},{3,7},{4,0},{5,1},{6,2},{7,3},{8,12},{9,13},{10,... | collective-permute-start | bytes 98312 | tf_op jit(solution)/shard_map/ppermute | solution.py:300
  45.2 5.0 %collective-permute-start.16 = (bf16[16,1024]{1,0:T(8,128)(2,1)S(1)}, bf16[16,1024]{1,0:T(8,128)(2,1)S(1)}, u32[]{:S(2)}, u32[]{:S(2)}) collective-permute-start(bf16[16,1024]{1,0:T(8,128)(2,1)S(1)} %get-tuple-element.46), channel_id=1, source_target_pairs={{0,4},{1,5},{2,6},{3,7},{4,0},{5,1},{6,2},{7,3},{8,12},{9,13},{10,... | collective-permute-start | bytes 98312 | tf_op jit(solution)/shard_map/ppermute | solution.py:300
  46.2 4.9 %collective-permute-start.21 = (bf16[16,1024]{1,0:T(8,128)(2,1)S(1)}, bf16[16,1024]{1,0:T(8,128)(2,1)S(1)}, u32[]{:S(2)}, u32[]{:S(2)}) collective-permute-start(bf16[16,1024]{1,0:T(8,128)(2,1)S(1)} %get-tuple-element.44), channel_id=1, source_target_pairs={{0,4},{1,5},{2,6},{3,7},{4,0},{5,1},{6,2},{7,3},{8,12},{9,13},{10,... | collective-permute-start | bytes 98312 | tf_op jit(solution)/shard_map/ppermute | solution.py:300

commit v6 on v5

--- a/solution.py
+++ b/solution.py
@@ -11,7 +11,6 @@
 MAXLEN = 64
 LANES = 128
 EPS = 1e-05
-SCRATCH = 13
 BF = jnp.bfloat16
 F32 = jnp.float32
 
@@ -47,9 +46,9 @@
 
 
 def prep_kernel(
-    len_hbm, ids_ref, cot_hbm, wout_hbm, w_hbm, mine_hbm,
-    onehot_ref, outg_ref, gg_ref, start_ref, origin_ref, w_ref, mine_ref,
-    len_ref, cot_ref, wout_ref, sems,
+    orders, shape, len_hbm, ids_ref, cot_hbm, wout_hbm, w_hbm, mine_hbm,
+    onehot_ref, outg_ref, gg_ref, start_ref, origin_ref, w_ref, mine_ref, outgt_ref,
+    len_ref, cot_ref, wout_ref, tmp_ref, sems,
 ):
     moves = [
         pltpu.make_async_copy(src, dst, sems.at[n])
@@ -78,6 +77,11 @@
     outg_ref[...] = out_grad
     moves[2].wait()
     gg_ref[...] = nt(out_grad, wout_ref[...]).astype(BF)
+    tmp_ref[...] = jnp.transpose(out_grad)
+    if orders is None:
+        outgt_ref[...] = tmp_ref[...]
+    else:
+        relative_rows(orders[0], shape, tmp_ref, outgt_ref)
     moves[3].wait()
     moves[4].wait()
 
@@ -98,66 +102,94 @@
     out_ref[...] = (nt(onehot, tab_ref[...]) + nn(gated, wout_ref[...])).astype(BF)
 
 
-def layer_kernel(order, shape, start_ref, onehot_ref, outg_ref, gg_ref, w_ref, *refs):
+def row_place(order, rel):
+    place = 0
+    for bit in order:
+        place = place * 2 + ((rel >> bit) & 1)
+    return place
+
+
+def relative_rows(order, shape, src_ref, out_ref):
+    dps, tabs = shape
+    devices = dps * tabs
+    me = lax.axis_index("dp") * tabs + lax.axis_index("table")
+    blk = src_ref.shape[0] // devices
+    for rel in range(devices):
+        at = row_place(order, rel) * blk
+        src_at = pl.multiple_of((me ^ rel) * blk, blk)
+        out_ref[at : at + blk, :] = src_ref[pl.ds(src_at, blk), :]
+    return out_ref[...]
+
+
+def emit(pair, at, lhs, rhs):
+    res = nn(lhs, rhs)
+    cols = slice(at, at + rhs.shape[1])
+    half = res.shape[0] // len(pair)
+    for n, ref in enumerate(pair):
+        ref[:, cols] = res[n * half : (n + 1) * half].astype(ref.dtype)
+
+
+def low_half():
+    return lax.broadcasted_iota(jnp.int32, (MAXLEN, LANES), 1) < DH
+
+
+def stack(v):
+    zero = jnp.zeros_like(v)
+    return jnp.concatenate([jnp.where(low_half(), v, zero), jnp.where(low_half(), zero, v)], axis=0)
+
+
+def merge(v):
+    return jnp.where(low_half(), v[:MAXLEN], v[MAXLEN:])
+
+
+def spots_of(live, width):
+    pairs = width // LANES
+    return [
+        (t * pairs + c, t * MAXLEN, max(t - 1, 0) * MAXLEN, c * LANES)
+        for t in range(live // MAXLEN)
+        for c in range(pairs)
+    ]
+
+
+def front_kernel(orders, shape, n_grads, start_ref, onehot_ref, outgt_ref, gg_ref, w_ref, *refs):
     _, tabs = shape
     pieces, refs = refs[:tabs], refs[tabs:]
-    gated_ref, tab_ref = refs[:2]
-    grads, scratch = refs[2:-SCRATCH], refs[-SCRATCH:]
+    grads, refs = refs[:n_grads], refs[n_grads:]
+    (
+        gated_ref, tab_ref, act_ref, dact_ref, fac_ref, att_ref, qs_ref, datt_ref, xhat_ref, rstd_ref, pgu_ref,
+        normt_ref, sc_ref, attended_ref, lhs_ref,
+    ) = refs
+    live = onehot_ref.shape[0]
+    width = tab_ref.shape[0]
     me_tab = lax.axis_index("table")
     for rel in range(tabs):
         feats = pieces[rel].shape[0]
         at = pl.multiple_of((me_tab ^ rel) * feats, feats)
         tab_ref[pl.ds(at, feats), :] = pieces[rel][...]
-    layer_body(order, shape, start_ref, tab_ref, onehot_ref, outg_ref, gg_ref, w_ref, gated_ref, grads, *scratch)
-
-
-def layer_body(
-    order, shape, start_ref, tab_ref, onehot_ref, outg_ref, gg_ref, w_ref, gated_ref, grads,
-    act_ref, dact_ref, sc_ref, fac_ref, qs_ref, das_ref, att_ref, ds_ref, turned_ref,
-    attended_ref, pg_ref, tmp_ref, lhs_ref,
-):
-    live, items = onehot_ref.shape
-    width = tab_ref.shape[0]
-    dps, tabs = shape
-    devices = dps * tabs
-    me_dp = lax.axis_index("dp")
-    me_tab = lax.axis_index("table")
-    me = me_dp * tabs + me_tab
-    blk = width // devices
-    half = width // 2
 
     x = nt(onehot_ref[...], tab_ref[...])
     centred = x - jnp.mean(x, axis=1, keepdims=True)
     rstd = lax.rsqrt(jnp.mean(centred * centred, axis=1, keepdims=True) + EPS)
     xhat = centred * rstd
+    xhat_ref[...] = xhat
+    rstd_ref[...] = jnp.broadcast_to(rstd, rstd_ref.shape)
     normed = xhat.astype(BF)
-    for g in range(4):
+    for g in (2, 3, 1, 0):
         cols = slice(g * width, (g + 1) * width)
         p = nn(normed, w_ref[:, cols])
         s = sigmoid(p)
         a = p * s
         act_ref[:, cols] = a.astype(BF)
         dact_ref[:, cols] = s + a * (1.0 - s)
-
-    tiles = live // MAXLEN
+    normt_ref[...] = jnp.transpose(normed)
+
+    spots = spots_of(live, width)
     pairs = width // LANES
-    low = lax.broadcasted_iota(jnp.int32, (MAXLEN, LANES), 1) < DH
-    zero = jnp.zeros((MAXLEN, LANES), BF)
-
-    def stack(v):
-        return jnp.concatenate([jnp.where(low, v, zero), jnp.where(low, zero, v)], axis=0)
-
-    def merge(v):
-        return jnp.where(low, v[:MAXLEN], v[MAXLEN:])
-
-    spots = [
-        (t * pairs + c, t * MAXLEN, max(t - 1, 0) * MAXLEN, c * LANES) for t in range(tiles) for c in range(pairs)
-    ]
     for n, r0, w0, lo in spots:
         q = stack(act_ref[r0 : r0 + MAXLEN, 2 * width + lo : 2 * width + lo + LANES])
         qs_ref[n] = q
         sc_ref[n] = nt(q, act_ref[w0 : w0 + LANES, 3 * width + lo : 3 * width + lo + LANES])
-    for t in range(tiles):
+    for t in range(live // MAXLEN):
         r0 = t * MAXLEN
         row = r0 + lax.broadcasted_iota(jnp.int32, (MAXLEN, LANES), 0)
         col = max(t - 1, 0) * MAXLEN + lax.broadcasted_iota(jnp.int32, (MAXLEN, LANES), 1)
@@ -184,13 +216,27 @@
     gated = (yhat * u).astype(BF)
     gated_ref[...] = gated
     gg = gg_ref[...].astype(F32)
-    pg_ref[:, :width] = ((gg * yhat).astype(BF).astype(F32) * dact_ref[:, :width]).astype(BF)
+    pg_u = ((gg * yhat).astype(BF).astype(F32) * dact_ref[:, :width]).astype(BF)
+    pgu_ref[...] = pg_u
     dy = gg * u
     datt = r * (dy - jnp.mean(dy, axis=1, keepdims=True) - yhat * jnp.mean(dy * yhat, axis=1, keepdims=True))
-    attended_ref[...] = datt
-
+    datt_ref[...] = datt.astype(BF)
+
+    if orders is None:
+        emit(grads[:1], 0, outgt_ref[...], gated)
+        emit(grads[1:], 0, normt_ref[...], pg_u)
+    else:
+        emit(grads, 0, outgt_ref[...], gated)
+        emit(grads, width, relative_rows(orders[0], shape, normt_ref, lhs_ref), pg_u)
+
+
+def mid_kernel(act_ref, dact_ref, fac_ref, att_ref, qs_ref, datt_ref, pg_ref, sc_ref, das_ref, ds_ref, turned_ref):
+    live, width = datt_ref.shape
+    pairs = width // LANES
+    tiles = live // MAXLEN
+    spots = spots_of(live, width)
     for n, r0, w0, lo in spots:
-        da = stack(attended_ref[r0 : r0 + MAXLEN, lo : lo + LANES].astype(BF))
+        da = stack(datt_ref[r0 : r0 + MAXLEN, lo : lo + LANES])
         das_ref[n] = da
         sc_ref[n] = nt(da, act_ref[w0 : w0 + LANES, width + lo : width + lo + LANES])
     for n in range(tiles * pairs):
@@ -199,9 +245,9 @@
     for n, r0, w0, lo in spots:
         k = act_ref[w0 : w0 + LANES, 3 * width + lo : 3 * width + lo + LANES]
         dq = merge(nn(ds_ref[n * LANES : (n + 1) * LANES, :], k)).astype(BF).astype(F32)
-        qc = slice(2 * width + lo, 2 * width + lo + LANES)
-        pg_ref[r0 : r0 + MAXLEN, qc] = (dq * dact_ref[r0 : r0 + MAXLEN, qc]).astype(BF)
-    for src_ref, rhs_ref, g in ((att_ref, das_ref, 1), (ds_ref, qs_ref, 3)):
+        slope = dact_ref[r0 : r0 + MAXLEN, 2 * width + lo : 2 * width + lo + LANES]
+        pg_ref[r0 : r0 + MAXLEN, width + lo : width + lo + LANES] = (dq * slope).astype(BF)
+    for src_ref, rhs_ref, g in ((att_ref, das_ref, 0), (ds_ref, qs_ref, 2)):
         turned_ref[...] = jnp.transpose(src_ref[...])
         for t in range(tiles):
             off = MAXLEN if t else 0
@@ -213,51 +259,37 @@
                     m = n + pairs
                     lhs = jnp.concatenate([lhs, turned_ref[:MAXLEN, m * LANES : (m + 1) * LANES]], axis=1)
                     rhs = jnp.concatenate([rhs, rhs_ref[m]], axis=0)
-                cols = slice(g * width + c * LANES, g * width + (c + 1) * LANES)
+                at = g * width + c * LANES
                 rows = slice(t * MAXLEN, (t + 1) * MAXLEN)
                 d = nn(lhs, rhs).astype(BF).astype(F32)
-                pg_ref[rows, cols] = (d * dact_ref[rows, cols]).astype(BF)
-
-    dn = nt(pg_ref[...], w_ref[...]).astype(BF).astype(F32)
-    dx = rstd * (dn - jnp.mean(dn, axis=1, keepdims=True) - xhat * jnp.mean(dn * xhat, axis=1, keepdims=True))
-    in_grad = (dx + outg_ref[...].astype(F32)).astype(BF)
-
-    def position(colour, rel):
-        place = 0
-        for bit in order[colour]:
-            place = place * 2 + ((rel >> bit) & 1)
-        return place
-
-    def relative(colour, src):
-        tmp_ref[...] = src
-        for rel in range(devices):
-            at = position(colour, rel) * blk
-            src_at = pl.multiple_of((me ^ rel) * blk, blk)
-            lhs_ref[at : at + blk, :] = tmp_ref[pl.ds(src_at, blk), :]
-        return lhs_ref[...]
-
-    normed_t = jnp.transpose(normed)
-    outg_t = jnp.transpose(outg_ref[...])
-    if order is None:
-        grad_o_ref, grad_u_ref, grad_t_ref = grads
-        grad_o_ref[...] = nn(outg_t, gated)
-        grad_u_ref[...] = nn(normed_t, pg_ref[...])
-        grad_t_ref[...] = nn(jnp.transpose(in_grad), onehot_ref[...]).astype(BF)
+                slope = dact_ref[rows, width + at : width + at + LANES]
+                pg_ref[rows, at : at + LANES] = (d * slope).astype(BF)
+
+
+def back_kernel(
+    orders, shape, n_grads, pgu_ref, pg_ref, w_ref, xhat_ref, rstd_ref, outg_ref, normt_ref, onehot_ref, *refs
+):
+    dps, tabs = shape
+    grads, (tmp_ref, lhs_ref) = refs[:n_grads], refs[n_grads:]
+    _, width = pgu_ref.shape
+    items = onehot_ref.shape[1]
+    dn = (nt(pgu_ref[...], w_ref[:, :width]) + nt(pg_ref[...], w_ref[:, width:])).astype(BF).astype(F32)
+    xhat = xhat_ref[...]
+    dx = dn - jnp.mean(dn, axis=1, keepdims=True) - xhat * jnp.mean(dn * xhat, axis=1, keepdims=True)
+    in_grad = (rstd_ref[:, :1] * dx + outg_ref[...].astype(F32)).astype(BF)
+    tmp_ref[...] = jnp.transpose(in_grad)
+    if orders is None:
+        emit(grads[:1], 0, normt_ref[...], pg_ref[...])
+        emit(grads[1:], 0, tmp_ref[...], onehot_ref[...])
         return
-
-    def emit(colour, at, lhs, rhs):
-        res = nn(lhs, rhs).astype(BF)
-        cols = slice(at, at + rhs.shape[1])
-        grads[2 * colour][:, cols] = res[:half]
-        grads[2 * colour + 1][:, cols] = res[half:]
-
-    emit(0, 0, relative(0, outg_t), gated)
-    emit(0, width, relative(0, normed_t), pg_ref[:, :width])
-    emit(1, 0, relative(1, normed_t), pg_ref[:, width : 3 * width])
-    emit(2, 0, relative(2, normed_t), pg_ref[:, 3 * width :])
-    tmp_ref[...] = jnp.transpose(in_grad)
+    emit(grads[:2], 0, relative_rows(orders[1], shape, normt_ref, lhs_ref), pg_ref[:, : 2 * width])
+    emit(grads[2:], 0, relative_rows(orders[2], shape, normt_ref, lhs_ref), pg_ref[:, 2 * width :])
+    me_dp = lax.axis_index("dp")
+    me_tab = lax.axis_index("table")
     feats = width // tabs
     span = items // dps
+    blk = width // (dps * tabs)
+    half = width // 2
     for rt in range(tabs):
         at = pl.multiple_of((me_tab ^ rt) * feats, feats)
         lhs_ref[rt * feats : (rt + 1) * feats, :] = tmp_ref[pl.ds(at, feats), :]
@@ -265,8 +297,8 @@
         at = pl.multiple_of((me_dp ^ rd) * span, span)
         res = nn(lhs_ref[...], onehot_ref[:, pl.ds(at, span)]).astype(BF)
         for rt in range(tabs):
-            place = position(2, rd * tabs + rt) * blk
-            dst = grads[4] if place < half else grads[5]
+            place = row_place(orders[2], rd * tabs + rt) * blk
+            dst = grads[2] if place < half else grads[3]
             place = place % half
             for j in range(feats // blk):
                 dst[place : place + blk, width + j * span : width + (j + 1) * span] = res[
@@ -317,6 +349,20 @@
     ids2 = ids.reshape(tabs, rows)
 
     sds = jax.ShapeDtypeStruct
+    ring = list(range(tab_bits, bits)) + list(range(1, tab_bits - 1))
+    colours = 3
+    blk = width // devices
+    span = items // dps
+    halving = blk % 16 == 0 and span == LANES and feats % blk == 0 and feats // blk * span == width
+    if halving:
+        orders = [[0] + ring[c:] + ring[:c] + [tab_bits - 1] for c in (0, 1, 2)]
+        front_grads = (sds((width // 2, 2 * width), BF),) * 2
+        back_grads = front_grads * 2
+    else:
+        orders = None
+        front_grads = (sds((width, width), F32),) * 2
+        back_grads = (sds((width, 3 * width), F32), sds((width, items), BF))
+
 
     def other(v, rel):
         return lax.ppermute(v, "table", [(i, i ^ rel) for i in range(tabs)])
@@ -325,8 +371,8 @@
     far = {}
     for rel in range(2, tabs, 2):
         far[rel] = other(mine, rel)
-    onehot, outg, gg, start, origin, w_near, mine_near = pl.pallas_call(
-        prep_kernel,
+    onehot, outg, gg, start, origin, w_near, mine_near, outg_t = pl.pallas_call(
+        functools.partial(prep_kernel, orders, (dps, tabs)),
         out_shape=(
             sds((live, items), BF),
             sds((live, width), BF),
@@ -335,13 +381,15 @@
             sds((8, live), jnp.int32),
             sds(w_uvqk.shape, BF),
             sds(mine.shape, BF),
+            sds((width, live), BF),
         ),
         in_specs=[HBM_SPEC, VMEM_SPEC] + [HBM_SPEC] * 4,
-        out_specs=(VMEM_SPEC,) * 7,
+        out_specs=(VMEM_SPEC,) * 8,
         scratch_shapes=[
             pltpu.SMEM(lengths.shape, jnp.int32),
             pltpu.VMEM(cotangent.shape, BF),
             pltpu.VMEM(w_out.shape, BF),
+            pltpu.VMEM((width, live), BF),
             pltpu.SemaphoreType.DMA((5,)),
         ],
         compiler_params=pltpu.CompilerParams(vmem_limit_bytes=16 << 20),
@@ -351,42 +399,66 @@
     for rel in range(2, tabs, 2):
         pieces += [far[rel], other(far[rel], 1)]
 
-    ring = list(range(tab_bits, bits)) + list(range(1, tab_bits - 1))
-    colours = 3
-    order = [[0] + ring[c:] + ring[:c] + [tab_bits - 1] for c in range(colours)]
-    w1 = 2 * width
-    blk = width // devices
-    span = items // dps
-    halving = blk % 16 == 0 and feats % blk == 0 and span == LANES and width % (feats // blk * span) == 0
-    if halving:
-        grad_shapes = (sds((width // 2, w1), BF),) * (2 * colours)
-    else:
-        order = None
-        grad_shapes = (sds((width, width), F32), sds((width, 4 * width), F32), sds((width, items), BF))
-    tiles = live // MAXLEN * (width // LANES)
-    gated, tab_t, *grads = pl.pallas_call(
-        functools.partial(layer_kernel, order, (dps, tabs)),
-        out_shape=(sds((live, width), BF), sds((width, items), BF)) + grad_shapes,
-        in_specs=[VMEM_SPEC] * (5 + tabs),
-        out_specs=(VMEM_SPEC,) * (2 + len(grad_shapes)),
-        scratch_shapes=[
-            pltpu.VMEM((live, 4 * width), BF),
-            pltpu.VMEM((live, 4 * width), F32),
-            pltpu.VMEM((tiles, LANES, LANES), F32),
-            pltpu.VMEM((tiles, LANES, LANES), F32),
-            pltpu.VMEM((tiles, LANES, LANES), BF),
-            pltpu.VMEM((tiles, LANES, LANES), BF),
-            pltpu.VMEM((tiles * LANES, LANES), BF),
-            pltpu.VMEM((tiles * LANES, LANES), BF),
-            pltpu.VMEM((LANES, tiles * LANES), BF),
+    spots = live // MAXLEN * (width // LANES)
+
+    def kernel(body, operands, outs, scratch, mib):
+        return pl.pallas_call(
+            body,
+            out_shape=outs,
+            in_specs=[VMEM_SPEC] * len(operands),
+            out_specs=(VMEM_SPEC,) * len(outs),
+            scratch_shapes=scratch,
+            compiler_params=pltpu.CompilerParams(vmem_limit_bytes=mib << 20),
+        )(*operands)
+
+    outs = kernel(
+        functools.partial(front_kernel, orders, (dps, tabs), len(front_grads)),
+        (start, onehot, outg_t, gg, w_near, *pieces),
+        front_grads
+        + (
+            sds((live, width), BF),
+            sds((width, items), BF),
+            sds((live, 4 * width), BF),
+            sds((live, 4 * width), F32),
+            sds((spots, LANES, LANES), F32),
+            sds((spots * LANES, LANES), BF),
+            sds((spots, LANES, LANES), BF),
+            sds((live, width), BF),
+            sds((live, width), F32),
+            sds((live, LANES), F32),
+            sds((live, width), BF),
+            sds((width, live), BF),
+        ),
+        [
+            pltpu.VMEM((spots, LANES, LANES), F32),
             pltpu.VMEM((live, width), F32),
-            pltpu.VMEM((live, 4 * width), BF),
-            pltpu.VMEM((width, live), BF),
             pltpu.VMEM((width, live), BF),
         ],
-        compiler_params=pltpu.CompilerParams(vmem_limit_bytes=32 << 20),
-        name="layer",
-    )(start, onehot, outg, gg, w_near, *pieces)
+        24,
+    )
+    grads, outs = list(outs[: len(front_grads)]), outs[len(front_grads) :]
+    gated, tab_t, act, dact, fac, att, qs, datt, xhat, rstd, pg_u, norm_t = outs
+    (pg,) = kernel(
+        mid_kernel,
+        (act, dact, fac, att, qs, datt),
+        (sds((live, 3 * width), BF),),
+        [
+            pltpu.VMEM((spots, LANES, LANES), F32),
+            pltpu.VMEM((spots, LANES, LANES), BF),
+            pltpu.VMEM((spots * LANES, LANES), BF),
+            pltpu.VMEM((LANES, spots * LANES), BF),
+        ],
+        16,
+    )
+
+    def back(pg):
+        return kernel(
+            functools.partial(back_kernel, orders, (dps, tabs), len(back_grads)),
+            (pg_u, pg, w_near, xhat, rstd, outg, norm_t, onehot),
+            back_grads,
+            [pltpu.VMEM((width, live), BF)] * 2,
+            24,
+        )
 
     def finish_output(gated):
         return pl.pallas_call(
@@ -399,7 +471,9 @@
         )(origin, ids2, tab_t, gated, w_out)
 
     if not halving:
-        grad_o, grad_u, grad_t = grads
+        grad_o, grad_gate = grads
+        grad_rest, grad_t = back(pg)
+        grad_u = jnp.concatenate([grad_gate, grad_rest], axis=1)
         grad_t = grad_t.reshape(tabs, feats, dps, span).transpose(2, 0, 1, 3).reshape(devices, feats * span)
 
         def share(v):
@@ -415,17 +489,23 @@
         h = v.shape[0] // 2
         return v[:h], v[h:]
 
-    totals = [add(keep, other(send, 1)) for keep, send in zip(grads[::2], grads[1::2])]
-    gated, totals[0] = lax.optimization_barrier((gated, totals[0]))
+    def step(total, colour, n):
+        keep, send = halves(total) if n else total
+        got = swap(send, orders[colour][n], tab_bits, dps, tabs)
+        if n == len(orders[colour]) - 1:
+            return keep, got
+        return add(keep, got)
+
+    first = step(grads, 0, 0)
+    rest = back(pg)
+    totals = [first, step(rest[:2], 1, 0), step(rest[2:], 2, 0)]
+    gated, totals[1] = lax.optimization_barrier((gated, totals[1]))
     output = finish_output(gated)
-    for n in range(len(ring)):
-        for c in range(colours):
-            keep, send = halves(totals[c])
-            totals[c] = add(keep, swap(send, order[c][1 + n], tab_bits, dps, tabs))
+    for n in range(1, len(orders[0]) - 1):
+        totals = [step(totals[c], c, n) for c in range(colours)]
     last = []
-    for total in totals:
-        keep, send = halves(total)
-        last += [keep, swap(send, tab_bits - 1, tab_bits, dps, tabs)]
+    for c in range(colours):
+        last += step(totals[c], c, len(orders[0]) - 1)
     grad_uvqk, grad_out_t, grad_t = pl.pallas_call(
         finish_kernel,
         out_shape=(sds((blk, 4 * width), F32), sds((blk, width), F32), sds((feats, span), F32)),

time: 52 us -> 50.8 us (0.977)
  waiting for transfers between devices: 14.2 us -> 12.4 us
    ppermute x10 -> x7, waiting for transfers between devices: 6.5 us -> 5.18 us  [other(): return lax.ppermute(v, 'table', [(i, i ^ rel) for i in range(tabs)])]
    ppermute x6, starting transfers between devices: 8.06 us -> 8.78 us  [swap(): return lax.ppermute(v, 'dp', [(i, i ^ 1 << b) for i in range(dps)])]
    ppermute x10 -> x7, starting transfers between devices: 6.96 us -> 6.3 us  [other(): return lax.ppermute(v, 'table', [(i, i ^ rel) for i in range(tabs)])]
    ppermute x6, waiting for transfers between devices: 5.16 us -> 4.63 us  [swap(): return lax.ppermute(v, 'dp', [(i, i ^ 1 << b) for i in range(dps)])]
    ppermute x6 -> x9, starting transfers between devices: 8.27 us -> 8.62 us  [swap(): return lax.ppermute(v, 'table', [(i, i ^ 1 << bit) for i in range(tabs)])]
    pallas_call x2 -> x4, Pallas kernels: 9.14 us -> 9.3 us  [the longest x3 7.33 us: kernel(): pl.pallas_call(body, out_shape=outs, in_specs=[VMEM_SPEC] * len(operands)...]
    ppermute x6 -> x9, waiting for transfers between devices: 2.56 us -> 2.56 us  [swap(): return lax.ppermute(v, 'table', [(i, i ^ 1 << bit) for i in range(tabs)])]
  transfers between devices with their start and end apart: 22 -> 22, of which waited for: 10 -> 7; matrix products, arithmetic and copies ran while one was open for 3% -> 4% of each run, Pallas kernels for 7% -> 14%
where the time goes in v6:
time: 50.8 us; the launch traced here: 50.5 us
  starting transfers between devices  23.7 us (47%)
  waiting for transfers between devices  12.4 us (24%)
  Pallas kernels  11.8 us (23%)
  other arithmetic  0.93 us (2%)
  between operations  0.89 us (2%)
  local copies, waits for them, and re-layouts  0.85 us (2%)
    ppermute x6, starting transfers between devices, swap(): return lax.ppermute(v, 'dp', [(i, i ^ 1 << b) for i in range(dps)])  8.78 us
    ppermute x9, starting transfers between devices, swap(): return lax.ppermute(v, 'table', [(i, i ^ 1 << bit) for i in range(tabs)])  8.62 us
    pallas_call x3, Pallas kernels, kernel(): pl.pallas_call(body, out_shape=outs, in_specs=[VMEM_SPEC] * len(operands)...  7.33 us
    ppermute x7, starting transfers between devices, other(): return lax.ppermute(v, 'table', [(i, i ^ rel) for i in range(tabs)])  6.3 us
    ppermute x7, waiting for transfers between devices, other(): return lax.ppermute(v, 'table', [(i, i ^ rel) for i in range(tabs)])  5.18 us
    ppermute x6, waiting for transfers between devices, swap(): return lax.ppermute(v, 'dp', [(i, i ^ 1 << b) for i in range(dps)])  4.63 us
    ppermute x9, waiting for transfers between devices, swap(): return lax.ppermute(v, 'table', [(i, i ^ 1 << bit) for i in range(tabs)])  2.56 us
    pallas_call x1, Pallas kernels, layer(): pl.pallas_call(functools.partial(prep_kernel, orders, (dps, tabs)), out_s...  1.97 us
  transfers between devices with their start and end apart: 22, of which 7 were waited for; matrix products, arithmetic and copies ran while one was open for 4% of the time, Pallas kernels for 14%

profile of v6, /device:TPU:0, one launch (start us, length us, event | category | flops | bytes accessed | tf_op | source)
XLA Modules:
  0.0 50.5 jit_solution(10145172717661928089)
XLA Ops:
  0.6 5.1 %collective-permute-start.5 = (bf16[64,512]{1,0:T(8,128)(2,1)}, bf16[64,512]{1,0:T(8,128)(2,1)S(1)}, u32[]{:S(2)}, u32[]{:S(2)}) collective-permute-start(bf16[64,512]{1,0:T(8,128)(2,1)} %bitcast.2), channel_id=1, source_target_pairs={{0,6},{1,7},{2,4},{3,5},{4,2},{5,3},{6,0},{7,1},{8,14},{9,15},{10,... | collective-permute-start | bytes 196616 | tf_op jit(solution)/shard_map/ppermute | solution.py:368
  6.4 2.2 %collective-permute-done.5.refs_6_ = bf16[64,512]{1,0:T(8,128)(2,1)S(1)} collective-permute-done((bf16[64,512]{1,0:T(8,128)(2,1)}, bf16[64,512]{1,0:T(8,128)(2,1)S(1)}, u32[]{:S(2)}, u32[]{:S(2)}) %collective-permute-start.5) | collective-permute-done | bytes 65568 | tf_op jit(solution)/shard_map/ppermute | solution.py:368
  8.6 3.0 %collective-permute-done.3.refs_4_ = bf16[64,512]{1,0:T(8,128)(2,1)S(1)} collective-permute-done((bf16[64,512]{1,0:T(8,128)(2,1)}, bf16[64,512]{1,0:T(8,128)(2,1)S(1)}, u32[]{:S(2)}, u32[]{:S(2)}) %collective-permute-start.3) | collective-permute-done | bytes 65568 | tf_op jit(solution)/shard_map/ppermute | solution.py:368
  12.1 0.7 %reshape.11.ids_ref = s32[8,512]{1,0:T(8,128)S(1)} reshape(s32[4096]{0:T(1024)} %param.6) | data formatting | bytes 32768 | tf_op jit(solution)/shard_map/reshape | solution.py:349
  12.8 2.0 %prep.1 = (bf16[320,512]{1,0:T(8,128)(2,1)S(1)}, bf16[320,512]{1,0:T(8,128)(2,1)S(1)}, bf16[320,512]{1,0:T(8,128)(2,1)S(1)}, s32[320,128]{1,0:T(8,128)S(1)}, s32...) custom-call(s32[1,8]{1,0:T(1,128)} %len_hbm.1, ...), custom_call_target="tpu_custom_call" | custom-call | tf_op jit(solution)/shard_map/prep/pallas_call | solution.py:374
  14.8 3.8 %shard_map.93 = (bf16[256,1024]{1,0:T(8,128)(2,1)S(1)}, bf16[256,1024]{1,0:T(8,128)(2,1)S(1)}, bf16[320,512]{1,0:T(8,128)(2,1)S(1)}, bf16[512,512]{1,0:T(8,128)(...) custom-call(s32[320,128]{1,0:T(8,128)S(1)} %get-tuple-element.36.sta, ...), custom_call_target="tpu_custom_call" | custom-call | tf_op jit(solution)/shard_map/pallas_call | solution.py:405
  18.8 1.3 %shard_map.94.pg_ref = bf16[320,1536]{1,0:T(8,128)(2,1)S(1)} custom-call(bf16[320,2048]{1,0:T(8,128)(2,1)S(1)} %get-tuple-element.45.act_ref, f32[320,2048]{1,0:T(8,128)S(1)} %get-tuple-element.46.dact_ref, f32[20,128,128]{2,1,0:T(8,128)S(1)} %get-tuple-element.47.fac_ref, bf16[2560,128]{1,0:T(8,128)(2,1)S(1)} %get-tuple-element.48.att_ref, ...), custom_call_target="tpu_custom_call" | custom-call | tf_op jit(solution)/shard_map/pallas_call | solution.py:405
  20.0 2.2 %shard_map.95 = (bf16[256,1024]{1,0:T(8,128)(2,1)S(1)}, bf16[256,1024]{1,0:T(8,128)(2,1)S(1)}, bf16[256,1024]{1,0:T(8,128)(2,1)S(1)}, bf16[256,1024]{1,0:T(8,128)(2,1)S(1)}) custom-call(bf16[320,512]{1,0:T(8,128)(2,1)S(1)} %get-tuple-element.44.pgu_ref, bf16[320,1536]{1,0:T(8,128)(2,1)S(1)} %shard_map.94.pg_ref, ...), custom_call_target="tpu_custom_call" | custom-call | tf_op jit(solution)/shard_map/pallas_call | solution.py:405
  23.1 1.6 %collective-permute-start.9 = (bf16[128,1024]{1,0:T(8,128)(2,1)S(1)}, bf16[128,1024]{1,0:T(8,128)(2,1)S(1)}, u32[]{:S(2)}, u32[]{:S(2)}) collective-permute-start(bf16[128,1024]{1,0:T(8,128)(2,1)S(1)} %slice.97), channel_id=1, source_target_pairs={{0,8},{8,0},{16,24},{24,16},{1,9},{9,1},{17,25},{25,17},{2,10},{10... | collective-permute-start | bytes 786440 | tf_op jit(solution)/shard_map/ppermute | solution.py:334
  24.9 1.6 %collective-permute-start.13 = (bf16[128,1024]{1,0:T(8,128)(2,1)S(1)}, bf16[128,1024]{1,0:T(8,128)(2,1)S(1)}, u32[]{:S(2)}, u32[]{:S(2)}) collective-permute-start(bf16[128,1024]{1,0:T(8,128)(2,1)S(1)} %slice.81), channel_id=1, source_target_pairs={{0,16},{8,24},{16,0},{24,8},{1,17},{9,25},{17,1},{25,9},{2,18},{10... | collective-permute-start | bytes 786440 | tf_op jit(solution)/shard_map/ppermute | solution.py:334
  26.7 1.1 %collective-permute-start.18 = (bf16[128,1024]{1,0:T(8,128)(2,1)S(1)}, bf16[128,1024]{1,0:T(8,128)(2,1)S(1)}, u32[]{:S(2)}, u32[]{:S(2)}) collective-permute-start(bf16[128,1024]{1,0:T(8,128)(2,1)S(1)} %slice.111), channel_id=1, source_target_pairs={{0,2},{1,3},{2,0},{3,1},{4,6},{5,7},{6,4},{7,5},{8,10},{9,11},{10,... | collective-permute-start | bytes 786440 | tf_op jit(solution)/shard_map/ppermute | solution.py:332
  27.8 4.0 %collective-permute-done.9 = bf16[128,1024]{1,0:T(8,128)(2,1)S(1)} collective-permute-done((bf16[128,1024]{1,0:T(8,128)(2,1)S(1)}, bf16[128,1024]{1,0:T(8,128)(2,1)S(1)}, u32[]{:S(2)}, u32[]{:S(2)}) %collective-permute-start.9) | collective-permute-done | bytes 262176 | tf_op jit(solution)/shard_map/ppermute | solution.py:334
  31.9 1.6 %collective-permute-start.10 = (bf16[64,1024]{1,0:T(8,128)(2,1)S(1)}, bf16[64,1024]{1,0:T(8,128)(2,1)S(1)}, u32[]{:S(2)}, u32[]{:S(2)}) collective-permute-start(bf16[64,1024]{1,0:T(8,128)(2,1)S(1)} %slice.99), channel_id=1, source_target_pairs={{0,16},{8,24},{16,0},{24,8},{1,17},{9,25},{17,1},{25,9},{2,18},{10... | collective-permute-start | bytes 393224 | tf_op jit(solution)/shard_map/ppermute | solution.py:334
  33.6 0.7 %collective-permute-start.14 = (bf16[64,1024]{1,0:T(8,128)(2,1)S(1)}, bf16[64,1024]{1,0:T(8,128)(2,1)S(1)}, u32[]{:S(2)}, u32[]{:S(2)}) collective-permute-start(bf16[64,1024]{1,0:T(8,128)(2,1)S(1)} %slice.105), channel_id=1, source_target_pairs={{0,2},{1,3},{2,0},{3,1},{4,6},{5,7},{6,4},{7,5},{8,10},{9,11},{10,... | collective-permute-start | bytes 393224 | tf_op jit(solution)/shard_map/ppermute | solution.py:332
  35.0 1.4 %collective-permute-start.19 = (bf16[64,1024]{1,0:T(8,128)(2,1)S(1)}, bf16[64,1024]{1,0:T(8,128)(2,1)S(1)}, u32[]{:S(2)}, u32[]{:S(2)}) collective-permute-start(bf16[64,1024]{1,0:T(8,128)(2,1)S(1)} %slice.113), channel_id=1, source_target_pairs={{0,8},{8,0},{16,24},{24,16},{1,9},{9,1},{17,25},{25,17},{2,10},{10... | collective-permute-start | bytes 393224 | tf_op jit(solution)/shard_map/ppermute | solution.py:334
  37.0 0.7 %collective-permute-start.11 = (bf16[32,1024]{1,0:T(8,128)(2,1)S(1)}, bf16[32,1024]{1,0:T(8,128)(2,1)S(1)}, u32[]{:S(2)}, u32[]{:S(2)}) collective-permute-start(bf16[32,1024]{1,0:T(8,128)(2,1)S(1)} %slice.101), channel_id=1, source_target_pairs={{0,2},{1,3},{2,0},{3,1},{4,6},{5,7},{6,4},{7,5},{8,10},{9,11},{10,... | collective-permute-start | bytes 196616 | tf_op jit(solution)/shard_map/ppermute | solution.py:332
  37.8 1.2 %collective-permute-done.14 = bf16[64,1024]{1,0:T(8,128)(2,1)S(1)} collective-permute-done((bf16[64,1024]{1,0:T(8,128)(2,1)S(1)}, bf16[64,1024]{1,0:T(8,128)(2,1)S(1)}, u32[]{:S(2)}, u32[]{:S(2)}) %collective-permute-start.14) | collective-permute-done | bytes 131104 | tf_op jit(solution)/shard_map/ppermute | solution.py:332
  39.0 1.6 %collective-permute-start.15 = (bf16[32,1024]{1,0:T(8,128)(2,1)S(1)}, bf16[32,1024]{1,0:T(8,128)(2,1)S(1)}, u32[]{:S(2)}, u32[]{:S(2)}) collective-permute-start(bf16[32,1024]{1,0:T(8,128)(2,1)S(1)} %slice.107), channel_id=1, source_target_pairs={{0,8},{8,0},{16,24},{24,16},{1,9},{9,1},{17,25},{25,17},{2,10},{10... | collective-permute-start | bytes 196616 | tf_op jit(solution)/shard_map/ppermute | solution.py:334
  40.6 1.1 %collective-permute-start.20 = (bf16[32,1024]{1,0:T(8,128)(2,1)S(1)}, bf16[32,1024]{1,0:T(8,128)(2,1)S(1)}, u32[]{:S(2)}, u32[]{:S(2)}) collective-permute-start(bf16[32,1024]{1,0:T(8,128)(2,1)S(1)} %slice.115), channel_id=1, source_target_pairs={{0,16},{8,24},{16,0},{24,8},{1,17},{9,25},{17,1},{25,9},{2,18},{10... | collective-permute-start | bytes 196616 | tf_op jit(solution)/shard_map/ppermute | solution.py:334
  41.7 2.4 %collective-permute-start.12 = (bf16[16,1024]{1,0:T(8,128)(2,1)S(1)}, bf16[16,1024]{1,0:T(8,128)(2,1)S(1)}, u32[]{:S(2)}, u32[]{:S(2)}) collective-permute-start(bf16[16,1024]{1,0:T(8,128)(2,1)S(1)} %get-tuple-element.70), channel_id=1, source_target_pairs={{0,4},{1,5},{2,6},{3,7},{4,0},{5,1},{6,2},{7,3},{8,12},{9,13},{10,... | collective-permute-start | bytes 98312 | tf_op jit(solution)/shard_map/ppermute | solution.py:332
  44.1 0.8 %collective-permute-start.16 = (bf16[16,1024]{1,0:T(8,128)(2,1)S(1)}, bf16[16,1024]{1,0:T(8,128)(2,1)S(1)}, u32[]{:S(2)}, u32[]{:S(2)}) collective-permute-start(bf16[16,1024]{1,0:T(8,128)(2,1)S(1)} %get-tuple-element.68), channel_id=1, source_target_pairs={{0,4},{1,5},{2,6},{3,7},{4,0},{5,1},{6,2},{7,3},{8,12},{9,13},{10,... | collective-permute-start | bytes 98312 | tf_op jit(solution)/shard_map/ppermute | solution.py:332
  45.0 2.3 %collective-permute-start.21 = (bf16[16,1024]{1,0:T(8,128)(2,1)S(1)}, bf16[16,1024]{1,0:T(8,128)(2,1)S(1)}, u32[]{:S(2)}, u32[]{:S(2)}) collective-permute-start(bf16[16,1024]{1,0:T(8,128)(2,1)S(1)} %get-tuple-element.66), channel_id=1, source_target_pairs={{0,4},{1,5},{2,6},{3,7},{4,0},{5,1},{6,2},{7,3},{8,12},{9,13},{10,... | collective-permute-start | bytes 98312 | tf_op jit(solution)/shard_map/ppermute | solution.py:332
  47.2 1.8 %out.1 = bf16[512,512]{1,0:T(8,128)(2,1)} custom-call(s32[8,320]{1,0:T(8,128)S(1)} %get-tuple-element.35.origin_ref, s32[8,512]{1,0:T(8,128)S(1)} %reshape.11.ids_ref, bf16[512,512]{1,0:T(8,128)(2,1)S(1)} %get-tuple-element.42.tab_ref, bf16[320,512]{1,0:T(8,128)(2,1)S(1)} %get-tuple-element.57.gated_ref, bf16[512,512]{1,0:T(8,128)(2,1)S(1)} %copy-done), custom_call_target="tpu_custom_call" | custom-call | tf_op jit(solution)/shard_map/out/pallas_call | solution.py:464
  49.0 0.8 %collective-permute-done.21.refs_5_ = bf16[16,1024]{1,0:T(8,128)(2,1)S(1)} collective-permute-done((bf16[16,1024]{1,0:T(8,128)(2,1)S(1)}, bf16[16,1024]{1,0:T(8,128)(2,1)S(1)}, u32[]{:S(2)}, u32[]{:S(2)}) %collective-permute-start.21) | collective-permute-done | bytes 32800 | tf_op jit(solution)/shard_map/ppermute | solution.py:332
  (53 shorter events, 4.8 us)
Async XLA Ops:
  0.6 7.9 %collective-permute-start.5 = (bf16[64,512]{1,0:T(8,128)(2,1)}, bf16[64,512]{1,0:T(8,128)(2,1)S(1)}, u32[]{:S(2)}, u32[]{:S(2)}) collective-permute-start(bf16[64,512]{1,0:T(8,128)(2,1)} %bitcast.2), channel_id=1, source_target_pairs={{0,6},{1,7},{2,4},{3,5},{4,2},{5,3},{6,0},{7,1},{8,14},{9,15},{10,... | collective-permute-start | bytes 196616 | tf_op jit(solution)/shard_map/ppermute | solution.py:368
  5.8 5.8 %collective-permute-start.3 = (bf16[64,512]{1,0:T(8,128)(2,1)}, bf16[64,512]{1,0:T(8,128)(2,1)S(1)}, u32[]{:S(2)}, u32[]{:S(2)}) collective-permute-start(bf16[64,512]{1,0:T(8,128)(2,1)} %bitcast.3), channel_id=1, source_target_pairs={{0,4},{1,5},{2,6},{3,7},{4,0},{5,1},{6,2},{7,3},{8,12},{9,13},{10,... | collective-permute-start | bytes 196616 | tf_op jit(solution)/shard_map/ppermute | solution.py:368
  5.8 5.8 %collective-permute-start.1 = (bf16[64,512]{1,0:T(8,128)(2,1)}, bf16[64,512]{1,0:T(8,128)(2,1)S(1)}, u32[]{:S(2)}, u32[]{:S(2)}) collective-permute-start(bf16[64,512]{1,0:T(8,128)(2,1)} %bitcast.4), channel_id=1, source_target_pairs={{0,2},{1,3},{2,0},{3,1},{4,6},{5,7},{6,4},{7,5},{8,10},{9,11},{10,... | collective-permute-start | bytes 196616 | tf_op jit(solution)/shard_map/ppermute | solution.py:368
  6.4 8.4 %collective-permute-start = (bf16[64,512]{1,0:T(8,128)(2,1)}, bf16[64,512]{1,0:T(8,128)(2,1)S(1)}, u32[]{:S(2)}, u32[]{:S(2)}) collective-permute-start(bf16[64,512]{1,0:T(8,128)(2,1)} %bitcast.5), channel_id=1, source_target_pairs={{0,1},{1,0},{2,3},{3,2},{4,5},{5,4},{6,7},{7,6},{8,9},{9,8},{10,11... | collective-permute-start | bytes 196616 | tf_op jit(solution)/shard_map/ppermute | solution.py:368
  8.6 6.2 %collective-permute-start.6 = (bf16[64,512]{1,0:T(8,128)(2,1)S(1)}, bf16[64,512]{1,0:T(8,128)(2,1)S(1)}, u32[]{:S(2)}, u32[]{:S(2)}) collective-permute-start(bf16[64,512]{1,0:T(8,128)(2,1)S(1)} %collective-permute-done.5.refs_6_), channel_id=1, source_target_pairs={{0,1},{1,0},{2,3},{3,2},{4,5},{5,4},{6,7},{7,6},{8,9},{9,8},{10,11... | collective-permute-start | bytes 196616 | tf_op jit(solution)/shard_map/ppermute | solution.py:368
  11.6 3.2 %collective-permute-start.4 = (bf16[64,512]{1,0:T(8,128)(2,1)S(1)}, bf16[64,512]{1,0:T(8,128)(2,1)S(1)}, u32[]{:S(2)}, u32[]{:S(2)}) collective-permute-start(bf16[64,512]{1,0:T(8,128)(2,1)S(1)} %collective-permute-done.3.refs_4_), channel_id=1, source_target_pairs={{0,1},{1,0},{2,3},{3,2},{4,5},{5,4},{6,7},{7,6},{8,9},{9,8},{10,11... | collective-permute-start | bytes 196616 | tf_op jit(solution)/shard_map/ppermute | solution.py:368
  11.6 3.2 %collective-permute-start.2 = (bf16[64,512]{1,0:T(8,128)(2,1)S(1)}, bf16[64,512]{1,0:T(8,128)(2,1)S(1)}, u32[]{:S(2)}, u32[]{:S(2)}) collective-permute-start(bf16[64,512]{1,0:T(8,128)(2,1)S(1)} %collective-permute-done.1.refs_2_), channel_id=1, source_target_pairs={{0,1},{1,0},{2,3},{3,2},{4,5},{5,4},{6,7},{7,6},{8,9},{9,8},{10,11... | collective-permute-start | bytes 196616 | tf_op jit(solution)/shard_map/ppermute | solution.py:368
  18.7 4.2 %collective-permute-start.8 = (bf16[256,1024]{1,0:T(8,128)(2,1)S(1)}, bf16[256,1024]{1,0:T(8,128)(2,1)S(1)}, u32[]{:S(2)}, u32[]{:S(2)}) collective-permute-start(bf16[256,1024]{1,0:T(8,128)(2,1)S(1)} %get-tuple-element.59), channel_id=1, source_target_pairs={{0,1},{1,0},{2,3},{3,2},{4,5},{5,4},{6,7},{7,6},{8,9},{9,8},{10,11... | collective-permute-start | bytes 1572872 | tf_op jit(solution)/shard_map/ppermute | solution.py:332
  22.3 2.4 %collective-permute-start.7 = (bf16[256,1024]{1,0:T(8,128)(2,1)S(1)}, bf16[256,1024]{1,0:T(8,128)(2,1)S(1)}, u32[]{:S(2)}, u32[]{:S(2)}) collective-permute-start(bf16[256,1024]{1,0:T(8,128)(2,1)S(1)} %get-tuple-element.56), channel_id=1, source_target_pairs={{0,1},{1,0},{2,3},{3,2},{4,5},{5,4},{6,7},{7,6},{8,9},{9,8},{10,11... | collective-permute-start | bytes 1572872 | tf_op jit(solution)/shard_map/ppermute | solution.py:332
  22.8 3.7 %collective-permute-start.17 = (bf16[256,1024]{1,0:T(8,128)(2,1)S(1)}, bf16[256,1024]{1,0:T(8,128)(2,1)S(1)}, u32[]{:S(2)}, u32[]{:S(2)}) collective-permute-start(bf16[256,1024]{1,0:T(8,128)(2,1)S(1)} %get-tuple-element.62), channel_id=1, source_target_pairs={{0,1},{1,0},{2,3},{3,2},{4,5},{5,4},{6,7},{7,6},{8,9},{9,8},{10,11... | collective-permute-start | bytes 1572872 | tf_op jit(solution)/shard_map/ppermute | solution.py:332
  23.1 8.7 %collective-permute-start.9 = (bf16[128,1024]{1,0:T(8,128)(2,1)S(1)}, bf16[128,1024]{1,0:T(8,128)(2,1)S(1)}, u32[]{:S(2)}, u32[]{:S(2)}) collective-permute-start(bf16[128,1024]{1,0:T(8,128)(2,1)S(1)} %slice.97), channel_id=1, source_target_pairs={{0,8},{8,0},{16,24},{24,16},{1,9},{9,1},{17,25},{25,17},{2,10},{10... | collective-permute-start | bytes 786440 | tf_op jit(solution)/shard_map/ppermute | solution.py:334
  24.9 8.6 %collective-permute-start.13 = (bf16[128,1024]{1,0:T(8,128)(2,1)S(1)}, bf16[128,1024]{1,0:T(8,128)(2,1)S(1)}, u32[]{:S(2)}, u32[]{:S(2)}) collective-permute-start(bf16[128,1024]{1,0:T(8,128)(2,1)S(1)} %slice.81), channel_id=1, source_target_pairs={{0,16},{8,24},{16,0},{24,8},{1,17},{9,25},{17,1},{25,9},{2,18},{10... | collective-permute-start | bytes 786440 | tf_op jit(solution)/shard_map/ppermute | solution.py:334
  26.7 8.1 %collective-permute-start.18 = (bf16[128,1024]{1,0:T(8,128)(2,1)S(1)}, bf16[128,1024]{1,0:T(8,128)(2,1)S(1)}, u32[]{:S(2)}, u32[]{:S(2)}) collective-permute-start(bf16[128,1024]{1,0:T(8,128)(2,1)S(1)} %slice.111), channel_id=1, source_target_pairs={{0,2},{1,3},{2,0},{3,1},{4,6},{5,7},{6,4},{7,5},{8,10},{9,11},{10,... | collective-permute-start | bytes 786440 | tf_op jit(solution)/shard_map/ppermute | solution.py:332
  31.9 5.0 %collective-permute-start.10 = (bf16[64,1024]{1,0:T(8,128)(2,1)S(1)}, bf16[64,1024]{1,0:T(8,128)(2,1)S(1)}, u32[]{:S(2)}, u32[]{:S(2)}) collective-permute-start(bf16[64,1024]{1,0:T(8,128)(2,1)S(1)} %slice.99), channel_id=1, source_target_pairs={{0,16},{8,24},{16,0},{24,8},{1,17},{9,25},{17,1},{25,9},{2,18},{10... | collective-permute-start | bytes 393224 | tf_op jit(solution)/shard_map/ppermute | solution.py:334
  33.6 13.6 %copy-start = (bf16[512,512]{1,0:T(8,128)(2,1)S(1)}, bf16[512,512]{1,0:T(8,128)(2,1)}, u32[]{:S(2)}) copy-start(bf16[512,512]{1,0:T(8,128)(2,1)} %wout_ref.1) | copy-start | bytes 1572868
  33.6 5.3 %collective-permute-start.14 = (bf16[64,1024]{1,0:T(8,128)(2,1)S(1)}, bf16[64,1024]{1,0:T(8,128)(2,1)S(1)}, u32[]{:S(2)}, u32[]{:S(2)}) collective-permute-start(bf16[64,1024]{1,0:T(8,128)(2,1)S(1)} %slice.105), channel_id=1, source_target_pairs={{0,2},{1,3},{2,0},{3,1},{4,6},{5,7},{6,4},{7,5},{8,10},{9,11},{10,... | collective-permute-start | bytes 393224 | tf_op jit(solution)/shard_map/ppermute | solution.py:332
  35.0 5.5 %collective-permute-start.19 = (bf16[64,1024]{1,0:T(8,128)(2,1)S(1)}, bf16[64,1024]{1,0:T(8,128)(2,1)S(1)}, u32[]{:S(2)}, u32[]{:S(2)}) collective-permute-start(bf16[64,1024]{1,0:T(8,128)(2,1)S(1)} %slice.113), channel_id=1, source_target_pairs={{0,8},{8,0},{16,24},{24,16},{1,9},{9,1},{17,25},{25,17},{2,10},{10... | collective-permute-start | bytes 393224 | tf_op jit(solution)/shard_map/ppermute | solution.py:334
  37.0 4.6 %collective-permute-start.11 = (bf16[32,1024]{1,0:T(8,128)(2,1)S(1)}, bf16[32,1024]{1,0:T(8,128)(2,1)S(1)}, u32[]{:S(2)}, u32[]{:S(2)}) collective-permute-start(bf16[32,1024]{1,0:T(8,128)(2,1)S(1)} %slice.101), channel_id=1, source_target_pairs={{0,2},{1,3},{2,0},{3,1},{4,6},{5,7},{6,4},{7,5},{8,10},{9,11},{10,... | collective-permute-start | bytes 196616 | tf_op jit(solution)/shard_map/ppermute | solution.py:332
  39.0 5.1 %collective-permute-start.15 = (bf16[32,1024]{1,0:T(8,128)(2,1)S(1)}, bf16[32,1024]{1,0:T(8,128)(2,1)S(1)}, u32[]{:S(2)}, u32[]{:S(2)}) collective-permute-start(bf16[32,1024]{1,0:T(8,128)(2,1)S(1)} %slice.107), channel_id=1, source_target_pairs={{0,8},{8,0},{16,24},{24,16},{1,9},{9,1},{17,25},{25,17},{2,10},{10... | collective-permute-start | bytes 196616 | tf_op jit(solution)/shard_map/ppermute | solution.py:334
  40.6 4.3 %collective-permute-start.20 = (bf16[32,1024]{1,0:T(8,128)(2,1)S(1)}, bf16[32,1024]{1,0:T(8,128)(2,1)S(1)}, u32[]{:S(2)}, u32[]{:S(2)}) collective-permute-start(bf16[32,1024]{1,0:T(8,128)(2,1)S(1)} %slice.115), channel_id=1, source_target_pairs={{0,16},{8,24},{16,0},{24,8},{1,17},{9,25},{17,1},{25,9},{2,18},{10... | collective-permute-start | bytes 196616 | tf_op jit(solution)/shard_map/ppermute | solution.py:334
  41.7 7.3 %collective-permute-start.12 = (bf16[16,1024]{1,0:T(8,128)(2,1)S(1)}, bf16[16,1024]{1,0:T(8,128)(2,1)S(1)}, u32[]{:S(2)}, u32[]{:S(2)}) collective-permute-start(bf16[16,1024]{1,0:T(8,128)(2,1)S(1)} %get-tuple-element.70), channel_id=1, source_target_pairs={{0,4},{1,5},{2,6},{3,7},{4,0},{5,1},{6,2},{7,3},{8,12},{9,13},{10,... | collective-permute-start | bytes 98312 | tf_op jit(solution)/shard_map/ppermute | solution.py:332
  44.1 4.9 %collective-permute-start.16 = (bf16[16,1024]{1,0:T(8,128)(2,1)S(1)}, bf16[16,1024]{1,0:T(8,128)(2,1)S(1)}, u32[]{:S(2)}, u32[]{:S(2)}) collective-permute-start(bf16[16,1024]{1,0:T(8,128)(2,1)S(1)} %get-tuple-element.68), channel_id=1, source_target_pairs={{0,4},{1,5},{2,6},{3,7},{4,0},{5,1},{6,2},{7,3},{8,12},{9,13},{10,... | collective-permute-start | bytes 98312 | tf_op jit(solution)/shard_map/ppermute | solution.py:332
  45.0 4.9 %collective-permute-start.21 = (bf16[16,1024]{1,0:T(8,128)(2,1)S(1)}, bf16[16,1024]{1,0:T(8,128)(2,1)S(1)}, u32[]{:S(2)}, u32[]{:S(2)}) collective-permute-start(bf16[16,1024]{1,0:T(8,128)(2,1)S(1)} %get-tuple-element.66), channel_id=1, source_target_pairs={{0,4},{1,5},{2,6},{3,7},{4,0},{5,1},{6,2},{7,3},{8,12},{9,13},{10,... | collective-permute-start | bytes 98312 | tf_op jit(solution)/shard_map/ppermute | solution.py:332

commit v7 on v6

--- a/solution.py
+++ b/solution.py
@@ -156,8 +156,8 @@
     pieces, refs = refs[:tabs], refs[tabs:]
     grads, refs = refs[:n_grads], refs[n_grads:]
     (
-        gated_ref, tab_ref, act_ref, dact_ref, fac_ref, att_ref, qs_ref, datt_ref, xhat_ref, rstd_ref, pgu_ref,
-        normt_ref, sc_ref, attended_ref, lhs_ref,
+        gated_ref, tab_ref, xhat_ref, rstd_ref, pgu_ref, normt_ref, pg_ref,
+        act_ref, dact_ref, fac_ref, att_ref, qs_ref, datt_ref, sc_ref, attended_ref, lhs_ref, das_ref, ds_ref, turned_ref,
     ) = refs
     live = onehot_ref.shape[0]
     width = tab_ref.shape[0]
@@ -230,7 +230,10 @@
         emit(grads, width, relative_rows(orders[0], shape, normt_ref, lhs_ref), pg_u)
 
 
-def mid_kernel(act_ref, dact_ref, fac_ref, att_ref, qs_ref, datt_ref, pg_ref, sc_ref, das_ref, ds_ref, turned_ref):
+    mid_body(act_ref, dact_ref, fac_ref, att_ref, qs_ref, datt_ref, pg_ref, sc_ref, das_ref, ds_ref, turned_ref)
+
+
+def mid_body(act_ref, dact_ref, fac_ref, att_ref, qs_ref, datt_ref, pg_ref, sc_ref, das_ref, ds_ref, turned_ref):
     live, width = datt_ref.shape
     pairs = width // LANES
     tiles = live // MAXLEN
@@ -418,38 +421,30 @@
         + (
             sds((live, width), BF),
             sds((width, items), BF),
-            sds((live, 4 * width), BF),
-            sds((live, 4 * width), F32),
-            sds((spots, LANES, LANES), F32),
-            sds((spots * LANES, LANES), BF),
-            sds((spots, LANES, LANES), BF),
-            sds((live, width), BF),
             sds((live, width), F32),
             sds((live, LANES), F32),
             sds((live, width), BF),
             sds((width, live), BF),
+            sds((live, 3 * width), BF),
         ),
         [
+            pltpu.VMEM((live, 4 * width), BF),
+            pltpu.VMEM((live, 4 * width), F32),
+            pltpu.VMEM((spots, LANES, LANES), F32),
+            pltpu.VMEM((spots * LANES, LANES), BF),
+            pltpu.VMEM((spots, LANES, LANES), BF),
+            pltpu.VMEM((live, width), BF),
             pltpu.VMEM((spots, LANES, LANES), F32),
             pltpu.VMEM((live, width), F32),
             pltpu.VMEM((width, live), BF),
-        ],
-        24,
-    )
-    grads, outs = list(outs[: len(front_grads)]), outs[len(front_grads) :]
-    gated, tab_t, act, dact, fac, att, qs, datt, xhat, rstd, pg_u, norm_t = outs
-    (pg,) = kernel(
-        mid_kernel,
-        (act, dact, fac, att, qs, datt),
-        (sds((live, 3 * width), BF),),
-        [
-            pltpu.VMEM((spots, LANES, LANES), F32),
             pltpu.VMEM((spots, LANES, LANES), BF),
             pltpu.VMEM((spots * LANES, LANES), BF),
             pltpu.VMEM((LANES, spots * LANES), BF),
         ],
-        16,
+        28,
     )
+    grads, outs = list(outs[: len(front_grads)]), outs[len(front_grads) :]
+    gated, tab_t, xhat, rstd, pg_u, norm_t, pg = outs
 
     def back(pg):
         return kernel(

time: 50.8 us -> 52 us (1.024)
  waiting for transfers between devices: 12.4 us -> 14.2 us
    ppermute x9, waiting for transfers between devices: 2.56 us -> 3.74 us  [swap(): return lax.ppermute(v, 'table', [(i, i ^ 1 << bit) for i in range(tabs)])]
    ppermute x6, waiting for transfers between devices: 4.63 us -> 5.32 us  [swap(): return lax.ppermute(v, 'dp', [(i, i ^ 1 << b) for i in range(dps)])]
    pallas_call x3 -> x2, Pallas kernels: 7.33 us -> 6.97 us  [kernel(): pl.pallas_call(body, out_shape=outs, in_specs=[VMEM_SPEC] * len(operands)...]
  transfers between devices with their start and end apart: 22 -> 22, of which waited for: 7 -> 11; matrix products, arithmetic and copies ran while one was open for 4% -> 3% of each run, Pallas kernels for 14% -> 7%
where the time goes in v7:
time: 52 us; the launch traced here: 51.8 us
  starting transfers between devices  23.5 us (45%)
  waiting for transfers between devices  14.2 us (27%)
  Pallas kernels  11.4 us (22%)
  other arithmetic  0.93 us (2%)
  between operations  0.88 us (2%)
  local copies, waits for them, and re-layouts  0.85 us (2%)
    ppermute x9, starting transfers between devices, swap(): return lax.ppermute(v, 'table', [(i, i ^ 1 << bit) for i in range(tabs)])  8.83 us
    ppermute x6, starting transfers between devices, swap(): return lax.ppermute(v, 'dp', [(i, i ^ 1 << b) for i in range(dps)])  8.36 us
    pallas_call x2, Pallas kernels, kernel(): pl.pallas_call(body, out_shape=outs, in_specs=[VMEM_SPEC] * len(operands)...  6.97 us
    ppermute x7, starting transfers between devices, other(): return lax.ppermute(v, 'table', [(i, i ^ rel) for i in range(tabs)])  6.3 us
    ppermute x6, waiting for transfers between devices, swap(): return lax.ppermute(v, 'dp', [(i, i ^ 1 << b) for i in range(dps)])  5.32 us
    ppermute x7, waiting for transfers between devices, other(): return lax.ppermute(v, 'table', [(i, i ^ rel) for i in range(tabs)])  5.18 us
    ppermute x9, waiting for transfers between devices, swap(): return lax.ppermute(v, 'table', [(i, i ^ 1 << bit) for i in range(tabs)])  3.74 us
    pallas_call x1, Pallas kernels, layer(): pl.pallas_call(functools.partial(prep_kernel, orders, (dps, tabs)), out_s...  1.97 us
  transfers between devices with their start and end apart: 22, of which 11 were waited for; matrix products, arithmetic and copies ran while one was open for 3% of the time, Pallas kernels for 7%

profile of v7, /device:TPU:0, one launch (start us, length us, event | category | flops | bytes accessed | tf_op | source)
XLA Modules:
  0.0 51.8 jit_solution(2566776193768744692)
XLA Ops:
  0.6 5.1 %collective-permute-start.5 = (bf16[64,512]{1,0:T(8,128)(2,1)}, bf16[64,512]{1,0:T(8,128)(2,1)S(1)}, u32[]{:S(2)}, u32[]{:S(2)}) collective-permute-start(bf16[64,512]{1,0:T(8,128)(2,1)} %bitcast.2), channel_id=1, source_target_pairs={{0,6},{1,7},{2,4},{3,5},{4,2},{5,3},{6,0},{7,1},{8,14},{9,15},{10,... | collective-permute-start | bytes 196616 | tf_op jit(solution)/shard_map/ppermute | solution.py:371
  6.4 2.2 %collective-permute-done.5.refs_6_ = bf16[64,512]{1,0:T(8,128)(2,1)S(1)} collective-permute-done((bf16[64,512]{1,0:T(8,128)(2,1)}, bf16[64,512]{1,0:T(8,128)(2,1)S(1)}, u32[]{:S(2)}, u32[]{:S(2)}) %collective-permute-start.5) | collective-permute-done | bytes 65568 | tf_op jit(solution)/shard_map/ppermute | solution.py:371
  8.6 3.0 %collective-permute-done.3.refs_4_ = bf16[64,512]{1,0:T(8,128)(2,1)S(1)} collective-permute-done((bf16[64,512]{1,0:T(8,128)(2,1)}, bf16[64,512]{1,0:T(8,128)(2,1)S(1)}, u32[]{:S(2)}, u32[]{:S(2)}) %collective-permute-start.3) | collective-permute-done | bytes 65568 | tf_op jit(solution)/shard_map/ppermute | solution.py:371
  12.1 0.7 %reshape.11.ids_ref = s32[8,512]{1,0:T(8,128)S(1)} reshape(s32[4096]{0:T(1024)} %param.6) | data formatting | bytes 32768 | tf_op jit(solution)/shard_map/reshape | solution.py:352
  12.8 2.0 %prep.1 = (bf16[320,512]{1,0:T(8,128)(2,1)S(1)}, bf16[320,512]{1,0:T(8,128)(2,1)S(1)}, bf16[320,512]{1,0:T(8,128)(2,1)S(1)}, s32[320,128]{1,0:T(8,128)S(1)}, s32...) custom-call(s32[1,8]{1,0:T(1,128)} %len_hbm.1, ...), custom_call_target="tpu_custom_call" | custom-call | tf_op jit(solution)/shard_map/prep/pallas_call | solution.py:377
  14.8 4.7 %shard_map.93 = (bf16[256,1024]{1,0:T(8,128)(2,1)S(1)}, bf16[256,1024]{1,0:T(8,128)(2,1)S(1)}, bf16[320,512]{1,0:T(8,128)(2,1)S(1)}, bf16[512,512]{1,0:T(8,128)(...) custom-call(s32[320,128]{1,0:T(8,128)S(1)} %get-tuple-element.31.sta, ...), custom_call_target="tpu_custom_call" | custom-call | tf_op jit(solution)/shard_map/pallas_call | solution.py:408
  19.6 2.2 %shard_map.94 = (bf16[256,1024]{1,0:T(8,128)(2,1)S(1)}, bf16[256,1024]{1,0:T(8,128)(2,1)S(1)}, bf16[256,1024]{1,0:T(8,128)(2,1)S(1)}, bf16[256,1024]{1,0:T(8,128)(2,1)S(1)}) custom-call(bf16[320,512]{1,0:T(8,128)(2,1)S(1)} %get-tuple-element.39.pgu_ref, bf16[320,1536]{1,0:T(8,128)(2,1)S(1)} %get-tuple-element.40.pg_ref, ...), custom_call_target="tpu_custom_call" | custom-call | tf_op jit(solution)/shard_map/pallas_call | solution.py:408
  22.5 1.3 %collective-permute-done.7 = bf16[256,1024]{1,0:T(8,128)(2,1)S(1)} collective-permute-done((bf16[256,1024]{1,0:T(8,128)(2,1)S(1)}, bf16[256,1024]{1,0:T(8,128)(2,1)S(1)}, u32[]{:S(2)}, u32[]{:S(2)}) %collective-permute-start.7) | collective-permute-done | bytes 524320 | tf_op jit(solution)/shard_map/ppermute | solution.py:335
  24.0 1.6 %collective-permute-start.13 = (bf16[128,1024]{1,0:T(8,128)(2,1)S(1)}, bf16[128,1024]{1,0:T(8,128)(2,1)S(1)}, u32[]{:S(2)}, u32[]{:S(2)}) collective-permute-start(bf16[128,1024]{1,0:T(8,128)(2,1)S(1)} %slice.81), channel_id=1, source_target_pairs={{0,16},{8,24},{16,0},{24,8},{1,17},{9,25},{17,1},{25,9},{2,18},{10... | collective-permute-start | bytes 786440 | tf_op jit(solution)/shard_map/ppermute | solution.py:337
  25.8 0.8 %collective-permute-start.18 = (bf16[128,1024]{1,0:T(8,128)(2,1)S(1)}, bf16[128,1024]{1,0:T(8,128)(2,1)S(1)}, u32[]{:S(2)}, u32[]{:S(2)}) collective-permute-start(bf16[128,1024]{1,0:T(8,128)(2,1)S(1)} %slice.111), channel_id=1, source_target_pairs={{0,2},{1,3},{2,0},{3,1},{4,6},{5,7},{6,4},{7,5},{8,10},{9,11},{10,... | collective-permute-start | bytes 786440 | tf_op jit(solution)/shard_map/ppermute | solution.py:335
  26.8 1.6 %collective-permute-start.9 = (bf16[128,1024]{1,0:T(8,128)(2,1)S(1)}, bf16[128,1024]{1,0:T(8,128)(2,1)S(1)}, u32[]{:S(2)}, u32[]{:S(2)}) collective-permute-start(bf16[128,1024]{1,0:T(8,128)(2,1)S(1)} %slice.97), channel_id=1, source_target_pairs={{0,8},{8,0},{16,24},{24,16},{1,9},{9,1},{17,25},{25,17},{2,10},{10... | collective-permute-start | bytes 786440 | tf_op jit(solution)/shard_map/ppermute | solution.py:337
  28.4 4.1 %collective-permute-done.13 = bf16[128,1024]{1,0:T(8,128)(2,1)S(1)} collective-permute-done((bf16[128,1024]{1,0:T(8,128)(2,1)S(1)}, bf16[128,1024]{1,0:T(8,128)(2,1)S(1)}, u32[]{:S(2)}, u32[]{:S(2)}) %collective-permute-start.13) | collective-permute-done | bytes 262176 | tf_op jit(solution)/shard_map/ppermute | solution.py:337
  32.5 1.0 %collective-permute-start.14 = (bf16[64,1024]{1,0:T(8,128)(2,1)S(1)}, bf16[64,1024]{1,0:T(8,128)(2,1)S(1)}, u32[]{:S(2)}, u32[]{:S(2)}) collective-permute-start(bf16[64,1024]{1,0:T(8,128)(2,1)S(1)} %slice.105), channel_id=1, source_target_pairs={{0,2},{1,3},{2,0},{3,1},{4,6},{5,7},{6,4},{7,5},{8,10},{9,11},{10,... | collective-permute-start | bytes 393224 | tf_op jit(solution)/shard_map/ppermute | solution.py:335
  34.1 1.6 %collective-permute-start.19 = (bf16[64,1024]{1,0:T(8,128)(2,1)S(1)}, bf16[64,1024]{1,0:T(8,128)(2,1)S(1)}, u32[]{:S(2)}, u32[]{:S(2)}) collective-permute-start(bf16[64,1024]{1,0:T(8,128)(2,1)S(1)} %slice.113), channel_id=1, source_target_pairs={{0,8},{8,0},{16,24},{24,16},{1,9},{9,1},{17,25},{25,17},{2,10},{10... | collective-permute-start | bytes 393224 | tf_op jit(solution)/shard_map/ppermute | solution.py:337
  35.7 1.2 %collective-permute-start.10 = (bf16[64,1024]{1,0:T(8,128)(2,1)S(1)}, bf16[64,1024]{1,0:T(8,128)(2,1)S(1)}, u32[]{:S(2)}, u32[]{:S(2)}) collective-permute-start(bf16[64,1024]{1,0:T(8,128)(2,1)S(1)} %slice.99), channel_id=1, source_target_pairs={{0,16},{8,24},{16,0},{24,8},{1,17},{9,25},{17,1},{25,9},{2,18},{10... | collective-permute-start | bytes 393224 | tf_op jit(solution)/shard_map/ppermute | solution.py:337
  36.9 0.7 %collective-permute-done.14 = bf16[64,1024]{1,0:T(8,128)(2,1)S(1)} collective-permute-done((bf16[64,1024]{1,0:T(8,128)(2,1)S(1)}, bf16[64,1024]{1,0:T(8,128)(2,1)S(1)}, u32[]{:S(2)}, u32[]{:S(2)}) %collective-permute-start.14) | collective-permute-done | bytes 131104 | tf_op jit(solution)/shard_map/ppermute | solution.py:335
  37.6 1.6 %collective-permute-start.15 = (bf16[32,1024]{1,0:T(8,128)(2,1)S(1)}, bf16[32,1024]{1,0:T(8,128)(2,1)S(1)}, u32[]{:S(2)}, u32[]{:S(2)}) collective-permute-start(bf16[32,1024]{1,0:T(8,128)(2,1)S(1)} %slice.107), channel_id=1, source_target_pairs={{0,8},{8,0},{16,24},{24,16},{1,9},{9,1},{17,25},{25,17},{2,10},{10... | collective-permute-start | bytes 196616 | tf_op jit(solution)/shard_map/ppermute | solution.py:337
  39.9 1.0 %collective-permute-start.20 = (bf16[32,1024]{1,0:T(8,128)(2,1)S(1)}, bf16[32,1024]{1,0:T(8,128)(2,1)S(1)}, u32[]{:S(2)}, u32[]{:S(2)}) collective-permute-start(bf16[32,1024]{1,0:T(8,128)(2,1)S(1)} %slice.115), channel_id=1, source_target_pairs={{0,16},{8,24},{16,0},{24,8},{1,17},{9,25},{17,1},{25,9},{2,18},{10... | collective-permute-start | bytes 196616 | tf_op jit(solution)/shard_map/ppermute | solution.py:337
  41.5 0.9 %collective-permute-start.11 = (bf16[32,1024]{1,0:T(8,128)(2,1)S(1)}, bf16[32,1024]{1,0:T(8,128)(2,1)S(1)}, u32[]{:S(2)}, u32[]{:S(2)}) collective-permute-start(bf16[32,1024]{1,0:T(8,128)(2,1)S(1)} %slice.101), channel_id=1, source_target_pairs={{0,2},{1,3},{2,0},{3,1},{4,6},{5,7},{6,4},{7,5},{8,10},{9,11},{10,... | collective-permute-start | bytes 196616 | tf_op jit(solution)/shard_map/ppermute | solution.py:335
  42.4 2.6 %collective-permute-start.16 = (bf16[16,1024]{1,0:T(8,128)(2,1)S(1)}, bf16[16,1024]{1,0:T(8,128)(2,1)S(1)}, u32[]{:S(2)}, u32[]{:S(2)}) collective-permute-start(bf16[16,1024]{1,0:T(8,128)(2,1)S(1)} %get-tuple-element.58), channel_id=1, source_target_pairs={{0,4},{1,5},{2,6},{3,7},{4,0},{5,1},{6,2},{7,3},{8,12},{9,13},{10,... | collective-permute-start | bytes 98312 | tf_op jit(solution)/shard_map/ppermute | solution.py:335
  45.0 1.1 %collective-permute-start.21 = (bf16[16,1024]{1,0:T(8,128)(2,1)S(1)}, bf16[16,1024]{1,0:T(8,128)(2,1)S(1)}, u32[]{:S(2)}, u32[]{:S(2)}) collective-permute-start(bf16[16,1024]{1,0:T(8,128)(2,1)S(1)} %get-tuple-element.56), channel_id=1, source_target_pairs={{0,4},{1,5},{2,6},{3,7},{4,0},{5,1},{6,2},{7,3},{8,12},{9,13},{10,... | collective-permute-start | bytes 98312 | tf_op jit(solution)/shard_map/ppermute | solution.py:335
  46.2 1.9 %collective-permute-start.12 = (bf16[16,1024]{1,0:T(8,128)(2,1)S(1)}, bf16[16,1024]{1,0:T(8,128)(2,1)S(1)}, u32[]{:S(2)}, u32[]{:S(2)}) collective-permute-start(bf16[16,1024]{1,0:T(8,128)(2,1)S(1)} %get-tuple-element.60), channel_id=1, source_target_pairs={{0,4},{1,5},{2,6},{3,7},{4,0},{5,1},{6,2},{7,3},{8,12},{9,13},{10,... | collective-permute-start | bytes 98312 | tf_op jit(solution)/shard_map/ppermute | solution.py:335
  48.1 1.8 %out.1 = bf16[512,512]{1,0:T(8,128)(2,1)} custom-call(s32[8,320]{1,0:T(8,128)S(1)} %get-tuple-element.30.origin_ref, s32[8,512]{1,0:T(8,128)S(1)} %reshape.11.ids_ref, bf16[512,512]{1,0:T(8,128)(2,1)S(1)} %get-tuple-element.37.tab_ref, bf16[320,512]{1,0:T(8,128)(2,1)S(1)} %get-tuple-element.47.gated_ref, bf16[512,512]{1,0:T(8,128)(2,1)S(1)} %copy-done), custom_call_target="tpu_custom_call" | custom-call | tf_op jit(solution)/shard_map/out/pallas_call | solution.py:459
  50.2 0.9 %collective-permute-done.12.refs_1_ = bf16[16,1024]{1,0:T(8,128)(2,1)S(1)} collective-permute-done((bf16[16,1024]{1,0:T(8,128)(2,1)S(1)}, bf16[16,1024]{1,0:T(8,128)(2,1)S(1)}, u32[]{:S(2)}, u32[]{:S(2)}) %collective-permute-start.12) | collective-permute-done | bytes 32800 | tf_op jit(solution)/shard_map/ppermute | solution.py:335
  (52 shorter events, 5.7 us)
Async XLA Ops:
  0.6 7.9 %collective-permute-start.5 = (bf16[64,512]{1,0:T(8,128)(2,1)}, bf16[64,512]{1,0:T(8,128)(2,1)S(1)}, u32[]{:S(2)}, u32[]{:S(2)}) collective-permute-start(bf16[64,512]{1,0:T(8,128)(2,1)} %bitcast.2), channel_id=1, source_target_pairs={{0,6},{1,7},{2,4},{3,5},{4,2},{5,3},{6,0},{7,1},{8,14},{9,15},{10,... | collective-permute-start | bytes 196616 | tf_op jit(solution)/shard_map/ppermute | solution.py:371
  5.8 5.8 %collective-permute-start.3 = (bf16[64,512]{1,0:T(8,128)(2,1)}, bf16[64,512]{1,0:T(8,128)(2,1)S(1)}, u32[]{:S(2)}, u32[]{:S(2)}) collective-permute-start(bf16[64,512]{1,0:T(8,128)(2,1)} %bitcast.3), channel_id=1, source_target_pairs={{0,4},{1,5},{2,6},{3,7},{4,0},{5,1},{6,2},{7,3},{8,12},{9,13},{10,... | collective-permute-start | bytes 196616 | tf_op jit(solution)/shard_map/ppermute | solution.py:371
  5.8 5.8 %collective-permute-start.1 = (bf16[64,512]{1,0:T(8,128)(2,1)}, bf16[64,512]{1,0:T(8,128)(2,1)S(1)}, u32[]{:S(2)}, u32[]{:S(2)}) collective-permute-start(bf16[64,512]{1,0:T(8,128)(2,1)} %bitcast.4), channel_id=1, source_target_pairs={{0,2},{1,3},{2,0},{3,1},{4,6},{5,7},{6,4},{7,5},{8,10},{9,11},{10,... | collective-permute-start | bytes 196616 | tf_op jit(solution)/shard_map/ppermute | solution.py:371
  6.4 8.4 %collective-permute-start = (bf16[64,512]{1,0:T(8,128)(2,1)}, bf16[64,512]{1,0:T(8,128)(2,1)S(1)}, u32[]{:S(2)}, u32[]{:S(2)}) collective-permute-start(bf16[64,512]{1,0:T(8,128)(2,1)} %bitcast.5), channel_id=1, source_target_pairs={{0,1},{1,0},{2,3},{3,2},{4,5},{5,4},{6,7},{7,6},{8,9},{9,8},{10,11... | collective-permute-start | bytes 196616 | tf_op jit(solution)/shard_map/ppermute | solution.py:371
  8.6 6.2 %collective-permute-start.6 = (bf16[64,512]{1,0:T(8,128)(2,1)S(1)}, bf16[64,512]{1,0:T(8,128)(2,1)S(1)}, u32[]{:S(2)}, u32[]{:S(2)}) collective-permute-start(bf16[64,512]{1,0:T(8,128)(2,1)S(1)} %collective-permute-done.5.refs_6_), channel_id=1, source_target_pairs={{0,1},{1,0},{2,3},{3,2},{4,5},{5,4},{6,7},{7,6},{8,9},{9,8},{10,11... | collective-permute-start | bytes 196616 | tf_op jit(solution)/shard_map/ppermute | solution.py:371
  11.6 3.2 %collective-permute-start.4 = (bf16[64,512]{1,0:T(8,128)(2,1)S(1)}, bf16[64,512]{1,0:T(8,128)(2,1)S(1)}, u32[]{:S(2)}, u32[]{:S(2)}) collective-permute-start(bf16[64,512]{1,0:T(8,128)(2,1)S(1)} %collective-permute-done.3.refs_4_), channel_id=1, source_target_pairs={{0,1},{1,0},{2,3},{3,2},{4,5},{5,4},{6,7},{7,6},{8,9},{9,8},{10,11... | collective-permute-start | bytes 196616 | tf_op jit(solution)/shard_map/ppermute | solution.py:371
  11.6 3.2 %collective-permute-start.2 = (bf16[64,512]{1,0:T(8,128)(2,1)S(1)}, bf16[64,512]{1,0:T(8,128)(2,1)S(1)}, u32[]{:S(2)}, u32[]{:S(2)}) collective-permute-start(bf16[64,512]{1,0:T(8,128)(2,1)S(1)} %collective-permute-done.1.refs_2_), channel_id=1, source_target_pairs={{0,1},{1,0},{2,3},{3,2},{4,5},{5,4},{6,7},{7,6},{8,9},{9,8},{10,11... | collective-permute-start | bytes 196616 | tf_op jit(solution)/shard_map/ppermute | solution.py:371
  21.8 2.0 %collective-permute-start.7 = (bf16[256,1024]{1,0:T(8,128)(2,1)S(1)}, bf16[256,1024]{1,0:T(8,128)(2,1)S(1)}, u32[]{:S(2)}, u32[]{:S(2)}) collective-permute-start(bf16[256,1024]{1,0:T(8,128)(2,1)S(1)} %get-tuple-element.46), channel_id=1, source_target_pairs={{0,1},{1,0},{2,3},{3,2},{4,5},{5,4},{6,7},{7,6},{8,9},{9,8},{10,11... | collective-permute-start | bytes 1572872 | tf_op jit(solution)/shard_map/ppermute | solution.py:335
  21.9 3.7 %collective-permute-start.17 = (bf16[256,1024]{1,0:T(8,128)(2,1)S(1)}, bf16[256,1024]{1,0:T(8,128)(2,1)S(1)}, u32[]{:S(2)}, u32[]{:S(2)}) collective-permute-start(bf16[256,1024]{1,0:T(8,128)(2,1)S(1)} %get-tuple-element.52), channel_id=1, source_target_pairs={{0,1},{1,0},{2,3},{3,2},{4,5},{5,4},{6,7},{7,6},{8,9},{9,8},{10,11... | collective-permute-start | bytes 1572872 | tf_op jit(solution)/shard_map/ppermute | solution.py:335
  22.4 4.2 %collective-permute-start.8 = (bf16[256,1024]{1,0:T(8,128)(2,1)S(1)}, bf16[256,1024]{1,0:T(8,128)(2,1)S(1)}, u32[]{:S(2)}, u32[]{:S(2)}) collective-permute-start(bf16[256,1024]{1,0:T(8,128)(2,1)S(1)} %get-tuple-element.49), channel_id=1, source_target_pairs={{0,1},{1,0},{2,3},{3,2},{4,5},{5,4},{6,7},{7,6},{8,9},{9,8},{10,11... | collective-permute-start | bytes 1572872 | tf_op jit(solution)/shard_map/ppermute | solution.py:335
  24.0 8.4 %collective-permute-start.13 = (bf16[128,1024]{1,0:T(8,128)(2,1)S(1)}, bf16[128,1024]{1,0:T(8,128)(2,1)S(1)}, u32[]{:S(2)}, u32[]{:S(2)}) collective-permute-start(bf16[128,1024]{1,0:T(8,128)(2,1)S(1)} %slice.81), channel_id=1, source_target_pairs={{0,16},{8,24},{16,0},{24,8},{1,17},{9,25},{17,1},{25,9},{2,18},{10... | collective-permute-start | bytes 786440 | tf_op jit(solution)/shard_map/ppermute | solution.py:337
  25.8 8.1 %collective-permute-start.18 = (bf16[128,1024]{1,0:T(8,128)(2,1)S(1)}, bf16[128,1024]{1,0:T(8,128)(2,1)S(1)}, u32[]{:S(2)}, u32[]{:S(2)}) collective-permute-start(bf16[128,1024]{1,0:T(8,128)(2,1)S(1)} %slice.111), channel_id=1, source_target_pairs={{0,2},{1,3},{2,0},{3,1},{4,6},{5,7},{6,4},{7,5},{8,10},{9,11},{10,... | collective-permute-start | bytes 786440 | tf_op jit(solution)/shard_map/ppermute | solution.py:335
  26.8 8.8 %collective-permute-start.9 = (bf16[128,1024]{1,0:T(8,128)(2,1)S(1)}, bf16[128,1024]{1,0:T(8,128)(2,1)S(1)}, u32[]{:S(2)}, u32[]{:S(2)}) collective-permute-start(bf16[128,1024]{1,0:T(8,128)(2,1)S(1)} %slice.97), channel_id=1, source_target_pairs={{0,8},{8,0},{16,24},{24,16},{1,9},{9,1},{17,25},{25,17},{2,10},{10... | collective-permute-start | bytes 786440 | tf_op jit(solution)/shard_map/ppermute | solution.py:337
  32.5 5.0 %collective-permute-start.14 = (bf16[64,1024]{1,0:T(8,128)(2,1)S(1)}, bf16[64,1024]{1,0:T(8,128)(2,1)S(1)}, u32[]{:S(2)}, u32[]{:S(2)}) collective-permute-start(bf16[64,1024]{1,0:T(8,128)(2,1)S(1)} %slice.105), channel_id=1, source_target_pairs={{0,2},{1,3},{2,0},{3,1},{4,6},{5,7},{6,4},{7,5},{8,10},{9,11},{10,... | collective-permute-start | bytes 393224 | tf_op jit(solution)/shard_map/ppermute | solution.py:335
  34.0 14.1 %copy-start = (bf16[512,512]{1,0:T(8,128)(2,1)S(1)}, bf16[512,512]{1,0:T(8,128)(2,1)}, u32[]{:S(2)}) copy-start(bf16[512,512]{1,0:T(8,128)(2,1)} %wout_ref.1) | copy-start | bytes 1572868
  34.1 5.7 %collective-permute-start.19 = (bf16[64,1024]{1,0:T(8,128)(2,1)S(1)}, bf16[64,1024]{1,0:T(8,128)(2,1)S(1)}, u32[]{:S(2)}, u32[]{:S(2)}) collective-permute-start(bf16[64,1024]{1,0:T(8,128)(2,1)S(1)} %slice.113), channel_id=1, source_target_pairs={{0,8},{8,0},{16,24},{24,16},{1,9},{9,1},{17,25},{25,17},{2,10},{10... | collective-permute-start | bytes 393224 | tf_op jit(solution)/shard_map/ppermute | solution.py:337
  35.7 5.7 %collective-permute-start.10 = (bf16[64,1024]{1,0:T(8,128)(2,1)S(1)}, bf16[64,1024]{1,0:T(8,128)(2,1)S(1)}, u32[]{:S(2)}, u32[]{:S(2)}) collective-permute-start(bf16[64,1024]{1,0:T(8,128)(2,1)S(1)} %slice.99), channel_id=1, source_target_pairs={{0,16},{8,24},{16,0},{24,8},{1,17},{9,25},{17,1},{25,9},{2,18},{10... | collective-permute-start | bytes 393224 | tf_op jit(solution)/shard_map/ppermute | solution.py:337
  37.6 4.7 %collective-permute-start.15 = (bf16[32,1024]{1,0:T(8,128)(2,1)S(1)}, bf16[32,1024]{1,0:T(8,128)(2,1)S(1)}, u32[]{:S(2)}, u32[]{:S(2)}) collective-permute-start(bf16[32,1024]{1,0:T(8,128)(2,1)S(1)} %slice.107), channel_id=1, source_target_pairs={{0,8},{8,0},{16,24},{24,16},{1,9},{9,1},{17,25},{25,17},{2,10},{10... | collective-permute-start | bytes 196616 | tf_op jit(solution)/shard_map/ppermute | solution.py:337
  39.9 5.1 %collective-permute-start.20 = (bf16[32,1024]{1,0:T(8,128)(2,1)S(1)}, bf16[32,1024]{1,0:T(8,128)(2,1)S(1)}, u32[]{:S(2)}, u32[]{:S(2)}) collective-permute-start(bf16[32,1024]{1,0:T(8,128)(2,1)S(1)} %slice.115), channel_id=1, source_target_pairs={{0,16},{8,24},{16,0},{24,8},{1,17},{9,25},{17,1},{25,9},{2,18},{10... | collective-permute-start | bytes 196616 | tf_op jit(solution)/shard_map/ppermute | solution.py:337
  41.5 4.7 %collective-permute-start.11 = (bf16[32,1024]{1,0:T(8,128)(2,1)S(1)}, bf16[32,1024]{1,0:T(8,128)(2,1)S(1)}, u32[]{:S(2)}, u32[]{:S(2)}) collective-permute-start(bf16[32,1024]{1,0:T(8,128)(2,1)S(1)} %slice.101), channel_id=1, source_target_pairs={{0,2},{1,3},{2,0},{3,1},{4,6},{5,7},{6,4},{7,5},{8,10},{9,11},{10,... | collective-permute-start | bytes 196616 | tf_op jit(solution)/shard_map/ppermute | solution.py:335
  42.4 7.5 %collective-permute-start.16 = (bf16[16,1024]{1,0:T(8,128)(2,1)S(1)}, bf16[16,1024]{1,0:T(8,128)(2,1)S(1)}, u32[]{:S(2)}, u32[]{:S(2)}) collective-permute-start(bf16[16,1024]{1,0:T(8,128)(2,1)S(1)} %get-tuple-element.58), channel_id=1, source_target_pairs={{0,4},{1,5},{2,6},{3,7},{4,0},{5,1},{6,2},{7,3},{8,12},{9,13},{10,... | collective-permute-start | bytes 98312 | tf_op jit(solution)/shard_map/ppermute | solution.py:335
  45.0 5.2 %collective-permute-start.21 = (bf16[16,1024]{1,0:T(8,128)(2,1)S(1)}, bf16[16,1024]{1,0:T(8,128)(2,1)S(1)}, u32[]{:S(2)}, u32[]{:S(2)}) collective-permute-start(bf16[16,1024]{1,0:T(8,128)(2,1)S(1)} %get-tuple-element.56), channel_id=1, source_target_pairs={{0,4},{1,5},{2,6},{3,7},{4,0},{5,1},{6,2},{7,3},{8,12},{9,13},{10,... | collective-permute-start | bytes 98312 | tf_op jit(solution)/shard_map/ppermute | solution.py:335
  46.2 4.9 %collective-permute-start.12 = (bf16[16,1024]{1,0:T(8,128)(2,1)S(1)}, bf16[16,1024]{1,0:T(8,128)(2,1)S(1)}, u32[]{:S(2)}, u32[]{:S(2)}) collective-permute-start(bf16[16,1024]{1,0:T(8,128)(2,1)S(1)} %get-tuple-element.60), channel_id=1, source_target_pairs={{0,4},{1,5},{2,6},{3,7},{4,0},{5,1},{6,2},{7,3},{8,12},{9,13},{10,... | collective-permute-start | bytes 98312 | tf_op jit(solution)/shard_map/ppermute | solution.py:335
